TPU v7x, 256 devices: a whole 4x4x8 slice. The times are simulated.
256 devices in a mesh: lat: 8 (over y_lo, x), lon: 32 (over y_hi, z, core).
Axes of the slice: x: 4, y: 4 (y_hi: 2, y_lo: 2; y = y_hi * 2 + y_lo), z: 8, core: 2. Of those that a mesh axis runs over, the one named last changes fastest.
Arguments:
- forcing: float32 [512, 8192], P('lat', 'lon'), may hold values from -32 to 32
- depth_east: float32 [512, 8192], P('lat', 'lon'), may hold values from 0.25 to 4
- depth_north: float32 [512, 8192], P('lat', 'lon'), may hold values from 0.25 to 4
- surface_term: float32 [512, 8192], P('lat', 'lon'), may hold values from 0.02 to 0.5
- ocean_mask: int32 [512, 8192], P('lat', 'lon'), may hold values 0 or 1
- cost_weights: float32 [8, 512, 8192], P(None, 'lat', 'lon'), may hold values from -6 to 6
Outputs:
- forcing_adjoint: float32 [8, 512, 8192], P(None, 'lat', 'lon')
- east_gradient: float32 [8, 512, 8192], P(None, 'lat', 'lon')
- north_gradient: float32 [8, 512, 8192], P(None, 'lat', 'lon')
Inputs may be any that keep to these rules, and one draw needn't show every extreme that they name: `ocean_mask`: 1 marks an ocean cell, 0 a land cell.
All inputs are finite; a program needn't handle non-finite values. No bound on the sum of `ocean_mask` on one device may be relied on, other than what follows from the above.
Results may differ from a plain program's by a relative error of at most 0.00018.
Values sent between devices are 32-bit elements; how exact they have to be, the bound alone decides.
No kernel may reach another device: no remote copies, remote signals or barrier semaphores. Data moves between devices by JAX's collectives and lax.ppermute only.
A program may use at most 64 MiB of HBM per device.

v0:
```python
import functools

import jax
import jax.numpy as jnp
from jax import lax
from jax.sharding import Mesh
from jax.sharding import PartitionSpec as P

ITERS = 6
LON = ("lon_0", "lon_1", "lon_2")
LAT = ("lat_0", "lat_1")
LAT_LON = ("lat_0", "lat_1", "lon_0", "lon_1", "lon_2")


def padded_2(block, sides, width, periodic):
    for axis, dim in sides:
        count = lax.axis_size(axis)
        forward = [(i, i + 1) for i in range(count - 1)]
        if periodic:
            forward.append((count - 1, 0))
        backward = [(target, source) for source, target in forward]
        low = lax.ppermute(
            lax.slice_in_dim(block, block.shape[dim] - width, None, axis=dim), axis, forward
        )
        high = lax.ppermute(lax.slice_in_dim(block, 0, width, axis=dim), axis, backward)
        block = jnp.concatenate([low, block, high], axis=dim)
    return block


def by_axis(array, axes):
    return functools.reduce(lax.psum, axes, array)


def shifted(value, axis, steps):
    count = lax.axis_size(axis)
    pairs = [(source, (source + steps) % count) for source in range(count)]
    return lax.ppermute(value, axis, pairs)


def shifted_2(block, axis, distance):
    devices = range(lax.axis_size(axis))
    route = [(i - distance, i) for i in devices if i - distance in devices]
    return lax.ppermute(block, axis, route)


def widen_coefs(stacked):
    wider = padded_2(stacked, ((LON, 2),), 1, True)
    return padded_2(wider, ((LAT, 1),), 1, False)


def widen_precond(field):
    wider = padded_2(field, ((LON, 1),), 1, True)
    return padded_2(wider, ((LAT, 0),), 1, False)


def widen_image(stack):
    wider = padded_2(stack, ((LON, 2),), 1, True)
    return padded_2(wider, ((LAT, 1),), 1, False)


def operate(padded, coefs):
    base, east_face, west_face, north_face, south_face = coefs
    centre = padded[..., 1:-1, 1:-1]
    return (
        base * centre
        + east_face * (centre - padded[..., 1:-1, 2:])
        + west_face * (centre - padded[..., 1:-1, :-2])
        + north_face * (centre - padded[..., 2:, 1:-1])
        + south_face * (centre - padded[..., :-2, 1:-1])
    )


def smoothed_terms(residual, diagonal, coefs):
    precond = residual / diagonal
    prec_pad = widen_precond(precond)
    smooth = operate(prec_pad, coefs)
    norm_value, delta = (
        by_axis(jnp.sum(residual * precond), LAT_LON),
        by_axis(jnp.sum(precond * smooth), LAT_LON),
    )
    return (prec_pad, smooth, norm_value, delta)


def body(forcing, depth_east, depth_north, surface_term, ocean_mask, cost_weights):
    stacked = jnp.stack([ocean_mask.astype(jnp.float32), depth_east, depth_north])
    padded = widen_coefs(stacked)
    wet = padded[0]
    east_all = padded[1][:, :-1] * wet[:, :-1] * wet[:, 1:]
    north_all = padded[2][:-1, :] * wet[:-1, :] * wet[1:, :]
    east_face = east_all[1:-1, 1:]
    west_face = east_all[1:-1, :-1]
    north_face = north_all[1:, 1:-1]
    south_face = north_all[:-1, 1:-1]
    ocean = wet[1:-1, 1:-1]
    mask_east = ocean * wet[1:-1, 2:]
    mask_north = ocean * wet[2:, 1:-1]
    base = ocean * surface_term + 1.0 - ocean
    diagonal = base + east_face + west_face + north_face + south_face
    coefs = (base, east_face, west_face, north_face, south_face)
    residual = forcing
    padded_dirs = []
    images = []
    residuals = []
    alphas = []
    betas = []
    pairs = []
    prec_pad, smooth, norm_first, delta = smoothed_terms(residual, diagonal, coefs)
    norms = [norm_first]
    alpha = norm_first / delta
    dir_pad = prec_pad
    image = smooth
    for step in range(ITERS):
        padded_dirs.append(dir_pad)
        images.append(image)
        alphas.append(alpha)
        pairs.append(norms[-1] / alpha)
        residual = residual - alpha * image
        if step < ITERS - 1:
            residuals.append(residual)
            prec_pad, smooth, norm_next, delta = smoothed_terms(residual, diagonal, coefs)
            beta = norm_next / norms[-1]
            alpha = norm_next / (delta - beta * norm_next / alpha)
            dir_pad = prec_pad + beta * dir_pad
            image = smooth + beta * image
            norms.append(norm_next)
            betas.append(beta)
    projections = by_axis(
        jnp.stack(
            [
                jnp.sum(cost_weights * padded_dirs[step][1:-1, 1:-1], axis=(1, 2))
                for step in range(ITERS)
            ]
        ),
        LAT_LON,
    )
    last = ITERS - 1
    dir_pad = padded_dirs[last]
    inner_dir = dir_pad[1:-1, 1:-1]
    alpha_bar = projections[last]
    norm_bar = alpha_bar / pairs[last]
    pair_bar = -alpha_bar * alphas[last] / pairs[last]
    scale = pair_bar[:, None, None]
    dir_bar = alphas[last] * cost_weights + 2.0 * scale * images[last]
    east_diff = inner_dir - dir_pad[1:-1, 2:]
    north_diff = inner_dir - dir_pad[2:, 1:-1]
    east_sum = scale * (east_diff * east_diff)
    north_sum = scale * (north_diff * north_diff)
    res_bar = jnp.zeros_like(cost_weights)
    depth_bar = jnp.zeros_like(cost_weights)
    for step in range(ITERS - 2, -1, -1):
        dir_pad = padded_dirs[step]
        inner_dir = dir_pad[1:-1, 1:-1]
        image = images[step]
        resid_next = residuals[step]
        precond_next = resid_next / diagonal
        scaled = dir_bar / diagonal
        beta_term, res_term, scaled_term, cross = (
            by_axis(jnp.sum(dir_bar * inner_dir, axis=(1, 2)), LAT_LON),
            by_axis(jnp.sum(res_bar * image, axis=(1, 2)), LAT_LON),
            by_axis(jnp.sum(scaled * image, axis=(1, 2)), LAT_LON),
            by_axis(jnp.sum(precond_next * image), LAT_LON),
        )
        norm_next_bar = norm_bar + beta_term / norms[step]
        alpha_bar = projections[step] - (res_term + scaled_term + 2.0 * norm_next_bar * cross)
        res_new = res_bar + scaled + 2.0 * norm_next_bar[:, None, None] * precond_next
        pre_bar = dir_bar + norm_next_bar[:, None, None] * resid_next
        depth_bar = depth_bar - pre_bar * precond_next / diagonal
        norm_bar = (
            -beta_term * norms[step + 1] / (norms[step] * norms[step]) + alpha_bar / pairs[step]
        )
        pair_bar = -alpha_bar * alphas[step] / pairs[step]
        scale = pair_bar[:, None, None]
        image_pad = widen_image(-alphas[step] * res_new + scale * inner_dir)
        dir_bar = (
            betas[step] * dir_bar
            + alphas[step] * cost_weights
            + scale * image
            + operate(image_pad, coefs)
        )
        centre = image_pad[:, 1:-1, 1:-1]
        east_sum = east_sum + (centre - image_pad[:, 1:-1, 2:]) * (inner_dir - dir_pad[1:-1, 2:])
        north_sum = north_sum + (centre - image_pad[:, 2:, 1:-1]) * (inner_dir - dir_pad[2:, 1:-1])
        res_bar = res_new
    precond_first = forcing / diagonal
    pre_bar = dir_bar + norm_bar[:, None, None] * forcing
    forcing_adjoint = res_bar + dir_bar / diagonal + 2.0 * norm_bar[:, None, None] * precond_first
    depth_bar = depth_bar - pre_bar * precond_first / diagonal
    east_column = shifted(depth_bar[:, :, :1], LON, -1)
    north_row = shifted_2(depth_bar[:, :1, :], LAT, -1)
    depth_eastward = jnp.concatenate([depth_bar[:, :, 1:], east_column], axis=2)
    depth_northward = jnp.concatenate([depth_bar[:, 1:, :], north_row], axis=1)
    east_gradient = mask_east * (east_sum + depth_bar + depth_eastward)
    north_gradient = mask_north * (north_sum + depth_bar + depth_northward)
    return (forcing_adjoint, east_gradient, north_gradient)


def solution(mesh):
    finer = Mesh(mesh.devices.reshape(2, 4, 2, 8, 2), ("lat_0", "lat_1", "lon_0", "lon_1", "lon_2"))
    return jax.shard_map(
        body,
        mesh=finer,
        in_specs=(
            P(LAT, LON),
            P(LAT, LON),
            P(LAT, LON),
            P(LAT, LON),
            P(LAT, LON),
            P(None, LAT, LON),
        ),
        out_specs=(P(None, LAT, LON), P(None, LAT, LON), P(None, LAT, LON)),
        check_vma=False,
    )
```

profile of v0, /device:TPU:1, one launch (start us, length us, event | category | flops | bytes accessed | tf_op | source)
XLA Modules:
  0.0 874.5 jit_solution(16298611728339549742)
XLA Ops:
  36.1 10.8 %all-reduce.54 = (f32[]{:T(128)}, f32[]{:T(128)}) all-reduce(f32[]{:T(128)} %get-tuple-element.39, f32[]{:T(128)} %get-tuple-element.38), channel_id=1, replica_groups=mesh['lat_0'=2,'lat_1'=4,'lon_0'=2,'lon_1'=8,'lon_2'=2] {'lat_0'}, use_global_device_ids=true, to_apply=%region_1.0 | all-reduce | flops 2 | bytes 16 | tf_op jit(solution)/shard_map/psum | solution.py:31
  59.7 14.7 %all-reduce.10 = (f32[]{:T(128)}, f32[]{:T(128)}) all-reduce(f32[]{:T(128)} %get-tuple-element.142, f32[]{:T(128)} %get-tuple-element.143), channel_id=1, replica_groups=mesh['lat_0'=2,'lat_1'=4,'lon_0'=2,'lon_1'=8,'lon_2'=2] {'lon_1'}, use_global_device_ids=true, to_apply=%region_4.0 | all-reduce | flops 2 | bytes 16 | tf_op jit(solution)/shard_map/psum | solution.py:31
  74.4 14.3 %all-reduce.32 = (f32[]{:T(128)}, f32[]{:T(128)}) all-reduce(f32[]{:T(128)} %get-tuple-element.64, f32[]{:T(128)} %get-tuple-element.65), channel_id=1, replica_groups=mesh['lat_0'=2,'lat_1'=4,'lon_0'=2,'lon_1'=8,'lon_2'=2] {'lon_2'}, use_global_device_ids=true, to_apply=%region_5.0 | all-reduce | flops 2 | bytes 16 | tf_op jit(solution)/shard_map/psum | solution.py:31
  121.0 16.4 %all-reduce.9 = (f32[]{:T(128)}, f32[]{:T(128)}) all-reduce(f32[]{:T(128)} %get-tuple-element.140, f32[]{:T(128)} %get-tuple-element.141), channel_id=1, replica_groups=mesh['lat_0'=2,'lat_1'=4,'lon_0'=2,'lon_1'=8,'lon_2'=2] {'lon_1'}, use_global_device_ids=true, to_apply=%region_16.0 | all-reduce | flops 2 | bytes 16 | tf_op jit(solution)/shard_map/psum | solution.py:31
  137.4 12.2 %all-reduce.31 = (f32[]{:T(128)}, f32[]{:T(128)}) all-reduce(f32[]{:T(128)} %get-tuple-element.62, f32[]{:T(128)} %get-tuple-element.63), channel_id=1, replica_groups=mesh['lat_0'=2,'lat_1'=4,'lon_0'=2,'lon_1'=8,'lon_2'=2] {'lon_2'}, use_global_device_ids=true, to_apply=%region_17.0 | all-reduce | flops 2 | bytes 16 | tf_op jit(solution)/shard_map/psum | solution.py:31
  187.1 14.5 %all-reduce.8 = (f32[]{:T(128)}, f32[]{:T(128)}) all-reduce(f32[]{:T(128)} %get-tuple-element.138, f32[]{:T(128)} %get-tuple-element.139), channel_id=1, replica_groups=mesh['lat_0'=2,'lat_1'=4,'lon_0'=2,'lon_1'=8,'lon_2'=2] {'lon_1'}, use_global_device_ids=true, to_apply=%region_28.0 | all-reduce | flops 2 | bytes 16 | tf_op jit(solution)/shard_map/psum | solution.py:31
  201.6 14.4 %all-reduce.30 = (f32[]{:T(128)}, f32[]{:T(128)}) all-reduce(f32[]{:T(128)} %get-tuple-element.60, f32[]{:T(128)} %get-tuple-element.61), channel_id=1, replica_groups=mesh['lat_0'=2,'lat_1'=4,'lon_0'=2,'lon_1'=8,'lon_2'=2] {'lon_2'}, use_global_device_ids=true, to_apply=%region_29.0 | all-reduce | flops 2 | bytes 16 | tf_op jit(solution)/shard_map/psum | solution.py:31
  251.0 16.4 %all-reduce.7 = (f32[]{:T(128)}, f32[]{:T(128)}) all-reduce(f32[]{:T(128)} %get-tuple-element.136, f32[]{:T(128)} %get-tuple-element.137), channel_id=1, replica_groups=mesh['lat_0'=2,'lat_1'=4,'lon_0'=2,'lon_1'=8,'lon_2'=2] {'lon_1'}, use_global_device_ids=true, to_apply=%region_40.0 | all-reduce | flops 2 | bytes 16 | tf_op jit(solution)/shard_map/psum | solution.py:31
  267.4 12.4 %all-reduce.29 = (f32[]{:T(128)}, f32[]{:T(128)}) all-reduce(f32[]{:T(128)} %get-tuple-element.58, f32[]{:T(128)} %get-tuple-element.59), channel_id=1, replica_groups=mesh['lat_0'=2,'lat_1'=4,'lon_0'=2,'lon_1'=8,'lon_2'=2] {'lon_2'}, use_global_device_ids=true, to_apply=%region_41.0 | all-reduce | flops 2 | bytes 16 | tf_op jit(solution)/shard_map/psum | solution.py:31
  316.7 14.5 %all-reduce.6 = (f32[]{:T(128)}, f32[]{:T(128)}) all-reduce(f32[]{:T(128)} %get-tuple-element.134, f32[]{:T(128)} %get-tuple-element.135), channel_id=1, replica_groups=mesh['lat_0'=2,'lat_1'=4,'lon_0'=2,'lon_1'=8,'lon_2'=2] {'lon_1'}, use_global_device_ids=true, to_apply=%region_52.0 | all-reduce | flops 2 | bytes 16 | tf_op jit(solution)/shard_map/psum | solution.py:31
  331.3 14.5 %all-reduce.28 = (f32[]{:T(128)}, f32[]{:T(128)}) all-reduce(f32[]{:T(128)} %get-tuple-element.56, f32[]{:T(128)} %get-tuple-element.57), channel_id=1, replica_groups=mesh['lat_0'=2,'lat_1'=4,'lon_0'=2,'lon_1'=8,'lon_2'=2] {'lon_2'}, use_global_device_ids=true, to_apply=%region_53.0 | all-reduce | flops 2 | bytes 16 | tf_op jit(solution)/shard_map/psum | solution.py:31
  381.0 16.4 %psum.1208 = f32[]{:T(128)} all-reduce(f32[]{:T(128)} %psum.1207), channel_id=1, replica_groups=mesh['lat_0'=2,'lat_1'=4,'lon_0'=2,'lon_1'=8,'lon_2'=2] {'lon_1'}, use_global_device_ids=true, to_apply=%region_64.0 | all-reduce | flops 1 | bytes 8 | tf_op jit(solution)/shard_map/psum | solution.py:31
  397.4 12.2 %psum.1209 = f32[]{:T(128)} all-reduce(f32[]{:T(128)} %psum.1208), channel_id=1, replica_groups=mesh['lat_0'=2,'lat_1'=4,'lon_0'=2,'lon_1'=8,'lon_2'=2] {'lon_2'}, use_global_device_ids=true, to_apply=%region_65.0 | all-reduce | flops 1 | bytes 8 | tf_op jit(solution)/shard_map/psum | solution.py:31
  420.1 8.5 all-reduce.16
  434.6 13.3 %all-reduce.5 = (f32[6,8]{1,0:T(8,128)S(1)}, f32[]{:T(128)}) all-reduce(f32[6,8]{1,0:T(8,128)S(1)} %get-tuple-element.132, f32[]{:T(128)} %get-tuple-element.133), channel_id=1, replica_groups=mesh['lat_0'=2,'lat_1'=4,'lon_0'=2,'lon_1'=8,'lon_2'=2] {'lon_1'}, use_global_device_ids=true, to_apply=%region_81.0 | all-reduce | flops 49 | bytes 392 | tf_op jit(solution)/shard_map/psum | solution.py:31
  447.9 10.9 %all-reduce.27 = (f32[6,8]{1,0:T(8,128)S(1)}, f32[]{:T(128)}) all-reduce(f32[6,8]{1,0:T(8,128)S(1)} %get-tuple-element.54, f32[]{:T(128)} %get-tuple-element.55), channel_id=1, replica_groups=mesh['lat_0'=2,'lat_1'=4,'lon_0'=2,'lon_1'=8,'lon_2'=2] {'lon_2'}, use_global_device_ids=true, to_apply=%region_82.0 | all-reduce | flops 49 | bytes 392 | tf_op jit(solution)/shard_map/psum | solution.py:31
  478.1 10.9 %psum.1223 = f32[8]{0:T(128)S(1)} all-reduce(f32[8]{0:T(128)S(1)} %psum.1222), channel_id=1, replica_groups=mesh['lat_0'=2,'lat_1'=4,'lon_0'=2,'lon_1'=8,'lon_2'=2] {'lon_1'}, use_global_device_ids=true, to_apply=%region_87.0 | all-reduce | flops 8 | bytes 64 | tf_op jit(solution)/shard_map/psum | solution.py:31
  489.7 9.8 %psum.1224 = f32[8]{0:T(128)S(1)} all-reduce(f32[8]{0:T(128)S(1)} %psum.1223), channel_id=1, replica_groups=mesh['lat_0'=2,'lat_1'=4,'lon_0'=2,'lon_1'=8,'lon_2'=2] {'lon_2'}, use_global_device_ids=true, to_apply=%region_88.0 | all-reduce | flops 8 | bytes 64 | tf_op jit(solution)/shard_map/psum | solution.py:31
  506.2 8.3 all-reduce.15
  520.5 13.1 %all-reduce.4 = (f32[8]{0:T(128)S(1)}, f32[]{:T(128)}) all-reduce(f32[8]{0:T(128)S(1)} %get-tuple-element.130, f32[]{:T(128)} %get-tuple-element.131), channel_id=1, replica_groups=mesh['lat_0'=2,'lat_1'=4,'lon_0'=2,'lon_1'=8,'lon_2'=2] {'lon_1'}, use_global_device_ids=true, to_apply=%region_93.0 | all-reduce | flops 9 | bytes 72 | tf_op jit(solution)/shard_map/psum | solution.py:31
  533.6 10.9 %all-reduce.26 = (f32[8]{0:T(128)S(1)}, f32[]{:T(128)}) all-reduce(f32[8]{0:T(128)S(1)} %get-tuple-element.52, f32[]{:T(128)} %get-tuple-element.53), channel_id=1, replica_groups=mesh['lat_0'=2,'lat_1'=4,'lon_0'=2,'lon_1'=8,'lon_2'=2] {'lon_2'}, use_global_device_ids=true, to_apply=%region_94.0 | all-reduce | flops 9 | bytes 72 | tf_op jit(solution)/shard_map/psum | solution.py:31
  569.5 8.7 all-reduce.14
  584.2 14.7 %all-reduce.3 = (f32[8]{0:T(128)S(1)}, f32[8]{0:T(128)S(1)}, f32[]{:T(128)}) all-reduce(f32[8]{0:T(128)S(1)} %get-tuple-element.127, f32[8]{0:T(128)S(1)} %get-tuple-element.128, f32[]{:T(128)} %get-tuple-element.129), channel_id=1, replica_groups=mesh['lat_0'=2,'lat_1'=4,'lon_0'=2,'lon_1'=8,'lon_2'=2] {'lon_1'}, use_global_device_ids=true, to_apply=%region_111.0 | all-reduce | flops 17 | bytes 136 | tf_op jit(solution)/shard_map/psum | solution.py:31
  598.9 13.5 %all-reduce.25 = (f32[8]{0:T(128)S(1)}, f32[8]{0:T(128)S(1)}, f32[]{:T(128)}) all-reduce(f32[8]{0:T(128)S(1)} %get-tuple-element.49, f32[8]{0:T(128)S(1)} %get-tuple-element.50, f32[]{:T(128)} %get-tuple-element.51), channel_id=1, replica_groups=mesh['lat_0'=2,'lat_1'=4,'lon_0'=2,'lon_1'=8,'lon_2'=2] {'lon_2'}, use_global_device_ids=true, to_apply=%region_112.0 | all-reduce | flops 17 | bytes 136 | tf_op jit(solution)/shard_map/psum | solution.py:31
  642.0 8.7 all-reduce.13
  656.7 16.5 %all-reduce.2 = (f32[8]{0:T(128)S(1)}, f32[8]{0:T(128)S(1)}, f32[]{:T(128)}) all-reduce(f32[8]{0:T(128)S(1)} %get-tuple-element.124, f32[8]{0:T(128)S(1)} %get-tuple-element.125, f32[]{:T(128)} %get-tuple-element.126), channel_id=1, replica_groups=mesh['lat_0'=2,'lat_1'=4,'lon_0'=2,'lon_1'=8,'lon_2'=2] {'lon_1'}, use_global_device_ids=true, to_apply=%region_135.0 | all-reduce | flops 17 | bytes 136 | tf_op jit(solution)/shard_map/psum | solution.py:31
  673.2 12.3 %all-reduce.24 = (f32[8]{0:T(128)S(1)}, f32[8]{0:T(128)S(1)}, f32[]{:T(128)}) all-reduce(f32[8]{0:T(128)S(1)} %get-tuple-element.46, f32[8]{0:T(128)S(1)} %get-tuple-element.47, f32[]{:T(128)} %get-tuple-element.48), channel_id=1, replica_groups=mesh['lat_0'=2,'lat_1'=4,'lon_0'=2,'lon_1'=8,'lon_2'=2] {'lon_2'}, use_global_device_ids=true, to_apply=%region_136.0 | all-reduce | flops 17 | bytes 136 | tf_op jit(solution)/shard_map/psum | solution.py:31
  730.6 16.5 %all-reduce.1 = (f32[8]{0:T(128)S(1)}, f32[8]{0:T(128)S(1)}, f32[]{:T(128)}) all-reduce(f32[8]{0:T(128)S(1)} %get-tuple-element.121, f32[8]{0:T(128)S(1)} %get-tuple-element.122, f32[]{:T(128)} %get-tuple-element.123), channel_id=1, replica_groups=mesh['lat_0'=2,'lat_1'=4,'lon_0'=2,'lon_1'=8,'lon_2'=2] {'lon_1'}, use_global_device_ids=true, to_apply=%region_159.0 | all-reduce | flops 17 | bytes 136 | tf_op jit(solution)/shard_map/psum | solution.py:31
  747.0 12.8 %all-reduce.23 = (f32[8]{0:T(128)S(1)}, f32[8]{0:T(128)S(1)}, f32[]{:T(128)}) all-reduce(f32[8]{0:T(128)S(1)} %get-tuple-element.43, f32[8]{0:T(128)S(1)} %get-tuple-element.44, f32[]{:T(128)} %get-tuple-element.45), channel_id=1, replica_groups=mesh['lat_0'=2,'lat_1'=4,'lon_0'=2,'lon_1'=8,'lon_2'=2] {'lon_2'}, use_global_device_ids=true, to_apply=%region_160.0 | all-reduce | flops 17 | bytes 136 | tf_op jit(solution)/shard_map/psum | solution.py:31
  793.3 8.3 all-reduce.11
  807.5 16.6 %all-reduce = (f32[8]{0:T(128)}, f32[8]{0:T(128)}, f32[]{:T(128)}) all-reduce(f32[8]{0:T(128)} %get-tuple-element.118, f32[8]{0:T(128)} %get-tuple-element.119, f32[]{:T(128)} %get-tuple-element.120), channel_id=1, replica_groups=mesh['lat_0'=2,'lat_1'=4,'lon_0'=2,'lon_1'=8,'lon_2'=2] {'lon_1'}, use_global_device_ids=true, to_apply=%region_189.0 | all-reduce | flops 17 | bytes 136 | tf_op jit(solution)/shard_map/psum | solution.py:31
  824.1 12.4 %all-reduce.22 = (f32[8]{0:T(128)}, f32[8]{0:T(128)}, f32[]{:T(128)}) all-reduce(f32[8]{0:T(128)} %get-tuple-element.40, f32[8]{0:T(128)} %get-tuple-element.41, f32[]{:T(128)} %get-tuple-element.42), channel_id=1, replica_groups=mesh['lat_0'=2,'lat_1'=4,'lon_0'=2,'lon_1'=8,'lon_2'=2] {'lon_2'}, use_global_device_ids=true, to_apply=%region_190.0 | all-reduce | flops 17 | bytes 136 | tf_op jit(solution)/shard_map/psum | solution.py:31
  (456 shorter events, 421.1 us)
Async XLA Ops:
  1.7 4.7 collective-permute-start
  18.4 7.0 collective-permute-start.4
  29.3 5.3 collective-permute-start.6
  93.8 5.3 collective-permute-start.10
  154.7 4.8 collective-permute-start.13
  159.6 5.3 collective-permute-start.14
  223.7 5.3 collective-permute-start.18
  284.3 4.8 collective-permute-start.21
  289.2 5.3 collective-permute-start.22
  353.7 5.3 collective-permute-start.26
  546.6 5.9 collective-permute-start.28
  547.1 5.5 collective-permute-start.29
  552.7 8.1 collective-permute-start.30
  554.0 6.8 collective-permute-start.31
  617.9 6.1 collective-permute-start.32
  618.4 5.7 collective-permute-start.33
  624.8 8.0 collective-permute-start.34
  626.1 6.7 collective-permute-start.35
  692.2 6.1 collective-permute-start.36
  692.6 5.7 collective-permute-start.37
  699.1 8.4 collective-permute-start.38
  700.4 7.2 collective-permute-start.39
  766.6 6.1 collective-permute-start.40
  767.0 5.7 collective-permute-start.41
  773.5 10.4 %collective-permute-start.42 = (f32[8,1,258]{2,1,0:T(1,128)}, f32[8,1,258]{2,1,0:T(1,128)}, u32[]{:S(2)}, u32[]{:S(2)}) collective-permute-start(f32[8,1,258]{2,1,0:T(1,128)} %get-tuple-element.232), channel_id=1, source_target_pairs={{32,0},{64,32},{96,64},{128,96},{160,128},{192,160},{224,192},{33,... | collective-permute-start | bytes 24776 | tf_op jit(solution)/shard_map/ppermute | solution.py:25
  774.8 9.1 %collective-permute-start.43 = (f32[8,1,258]{2,1,0:T(1,128)}, f32[8,1,258]{2,1,0:T(1,128)}, u32[]{:S(2)}, u32[]{:S(2)}) collective-permute-start(f32[8,1,258]{2,1,0:T(1,128)} %get-tuple-element.233), channel_id=1, source_target_pairs={{0,32},{32,64},{64,96},{96,128},{128,160},{160,192},{192,224},{1,3... | collective-permute-start | bytes 24776 | tf_op jit(solution)/shard_map/ppermute | solution.py:22
  842.2 6.3 collective-permute-start.44
  842.9 5.7 collective-permute-start.45
  848.7 5.6 collective-permute-start.46
  850.0 4.9 collective-permute-start.47
  856.7 14.2 %collective-permute-start.49 = (f32[8,1,256]{2,1,0:T(1,128)S(1)}, f32[8,1,256]{2,1,0:T(1,128)S(1)}, u32[]{:S(2)}, u32[]{:S(2)}) collective-permute-start(f32[8,1,256]{2,1,0:T(1,128)S(1)} %slice.651), channel_id=1, source_target_pairs={{32,0},{64,32},{96,64},{128,96},{160,128},{192,160},{224,192},{33,... | collective-permute-start | bytes 24584 | tf_op jit(solution)/shard_map/ppermute | solution.py:43
  858.2 9.5 %collective-permute-start.48 = (f32[8,64,1]{2,1,0:T(8,128)S(1)}, f32[8,64,1]{2,1,0:T(8,128)S(1)}, u32[]{:S(2)}, u32[]{:S(2)}) collective-permute-start(f32[8,64,1]{2,1,0:T(8,128)S(1)} %slice.643), channel_id=1, source_target_pairs={{0,31},{1,0},{2,1},{3,2},{4,3},{5,4},{6,5},{7,6},{8,7},{9,8},{10,9... | collective-permute-start | bytes 6152 | tf_op jit(solution)/shard_map/ppermute | solution.py:37
  (137 other events, 5138.3 us)
where the time goes:
time: 890 us; the launch traced here: 875 us
  blocking collectives  612 us (69%)
  starting transfers between devices  104 us (12%)
  other arithmetic  54.5 us (6%)
  waiting for transfers between devices  47.1 us (5%)
  between operations  42.9 us (5%)
  local copies, waits for them, and re-layouts  14.1 us (2%)
    psum x65, blocking collectives, by_axis(): return functools.reduce(lax.psum, axes, array)  612 us
    ppermute x24, starting transfers between devices, padded_2(): lax.ppermute(lax.slice_in_dim(block, block.shape[dim] - width, None, axis...  68.2 us
    ppermute x24, waiting for transfers between devices, padded_2(): lax.ppermute(lax.slice_in_dim(block, 0, width, axis=dim), axis, backward)  33.8 us
    ppermute x24, starting transfers between devices, padded_2(): lax.ppermute(lax.slice_in_dim(block, 0, width, axis=dim), axis, backward)  26 us
  transfers between devices with their start and end apart: 50, of which 24 were waited for; matrix products, arithmetic and copies ran while one was open for 0% of the time, Pallas kernels for 0%

commit v1 on v0

v1 whole, which is shorter than its diff:
```python
import functools

import jax
import jax.numpy as jnp
from jax import lax
from jax.experimental import pallas as pl
from jax.experimental.pallas import tpu as pltpu
from jax.sharding import PartitionSpec as P

ITERS = 6
COSTS = 8
ROWS = 64
COLS = 256
LANES = 128
WIDE = 384
DEEP = 13
SLIM = 6
EDGE = 16
FIELDS = 5
FRAME = 80
TALL = 96
MSG_W = FIELDS * EDGE
MSG_C = MSG_W + COSTS * 8
MSG = MSG_C + EDGE
N_LAM = COSTS * ITERS
N_RHS = N_LAM
N_MAT = N_LAM + ITERS
F32 = jnp.float32
HIGH = lax.Precision.HIGHEST


def lane_index(rows):
    return lax.broadcasted_iota(jnp.int32, (rows, LANES), 1)


def turn(value, amount):
    return pltpu.roll(value, amount % value.shape[1], 1)


def east_of(value):
    return pltpu.roll(value, value.shape[1] - 1, 1)


def west_of(value):
    return pltpu.roll(value, 1, 1)


def strips_kernel(f, de, dn, st, mask, w, to_east, to_west):
    lane = lane_index(ROWS)
    fields = [f[...], de[...], dn[...], st[...], mask[...].astype(F32)]
    fields += [w[n] for n in range(COSTS)]
    east = jnp.zeros((ROWS, LANES), F32)
    west = jnp.zeros((ROWS, LANES), F32)
    at = 0
    for k, field in enumerate(fields):
        wide = DEEP if k < FIELDS else SLIM
        here = (lane >= at) & (lane < at + wide)
        east = jnp.where(here, turn(field[:, LANES:], at - (LANES - wide)), east)
        west = jnp.where(here, turn(field[:, :LANES], at), west)
        at += wide
    to_east[...] = east
    to_west[...] = west


def bands_kernel(*refs):
    ins, (to_north, to_south) = refs[:-2], refs[-2:]
    for out, (f, de, dn, st, mask, w, sw, se) in ((to_north, ins[:8]), (to_south, ins[8:])):
        for k, field in enumerate((f, de, dn, st, mask)):
            out[EDGE * k : EDGE * (k + 1), :] = field[...].astype(F32)
        for n in range(COSTS):
            out[MSG_W + 8 * n : MSG_W + 8 * (n + 1), :] = w[n]
        out[MSG_C:, :LANES] = sw[...]
        out[MSG_C:, LANES:] = se[...]


def side_tile(pw, pe, at, wide):
    lane = lane_index(pw.shape[0])
    west = jnp.where(lane >= LANES - wide, turn(pw, LANES - wide - at), 0.0)
    return jnp.where(lane < wide, turn(pe, -at), west)


def forward_kernel(
    flags, f, de, dn, st, mask, w, ls, ln, sw, se,
    vecs, coefs, wside, wet, dots,
    raw, face, vec, part,
):
    own = (f, de, dn, st, mask)
    for rb in range(TALL // 8):
        at = 8 + 8 * rb
        if rb < 2:
            src, off = ls, 8 * rb
        elif rb >= 10:
            src, off = ln, 8 * rb - 80
        else:
            src, off = None, 8 * rb - 16
        if src is None:
            pw, pe = sw[off : off + 8, :], se[off : off + 8, :]
        else:
            pw = src[MSG_C + off : MSG_C + off + 8, :LANES]
            pe = src[MSG_C + off : MSG_C + off + 8, LANES:]
        for k in range(FIELDS):
            if src is None:
                body = own[k][off : off + 8, :].astype(F32)
            else:
                body = src[EDGE * k + off : EDGE * k + off + 8, :]
            side = side_tile(pw, pe, DEEP * k, DEEP)
            if k == FIELDS - 1 and src is not None:
                inside = flags[0 if rb < 2 else 1] > 0
                body = jnp.where(inside, body, 0.0)
                side = jnp.where(inside, side, 0.0)
            raw[k, at : at + 8, :COLS] = body
            raw[k, at : at + 8, COLS:] = side
        if 1 <= rb < 11:
            for n in range(COSTS):
                wside[n, 8 * rb - 8 : 8 * rb, :] = side_tile(
                    pw, pe, FIELDS * DEEP + SLIM * n, SLIM
                )
    for rb in range(TALL // 8):
        at = 8 + 8 * rb
        m = raw[4, at : at + 8, :]
        me = m * east_of(m)
        mn = m * raw[4, at + 1 : at + 9, :]
        ex = raw[1, at : at + 8, :] * me
        face[0, at : at + 8, :] = ex
        face[1, at : at + 8, :] = west_of(ex)
        face[2, at : at + 8, :] = raw[2, at : at + 8, :] * mn
        if 2 <= rb < 10:
            wet[0, 8 * rb - 16 : 8 * rb - 8, :] = me[:, :COLS]
            wet[1, 8 * rb - 16 : 8 * rb - 8, :] = mn[:, :COLS]
    for rb in range(TALL // 8):
        at = 8 + 8 * rb
        m = raw[4, at : at + 8, :]
        ex = face[0, at : at + 8, :]
        exw = face[1, at : at + 8, :]
        ey = face[2, at : at + 8, :]
        eys = face[2, at - 1 : at + 7, :]
        diag = m * raw[3, at : at + 8, :] + 1.0 - m + ex + exw + ey + eys
        inv = 1.0 / diag
        face[3, at : at + 8, :] = inv
        forcing = raw[0, at : at + 8, :]
        v0 = forcing * inv
        vec[0, at : at + 8, :] = v0
        if 1 <= rb < 11:
            to = slice(8 * rb - 8, 8 * rb)
            vecs[0, to, :] = v0
            for k, value in enumerate((ex, exw, ey, eys, inv, diag, forcing)):
                coefs[k, to, :] = value
    for j in range(ITERS):
        for rb in range(TALL // 8):
            at = 8 + 8 * rb
            v = vec[j, at : at + 8, :]
            image = (
                face[0, at : at + 8, :] * east_of(v)
                + face[1, at : at + 8, :] * west_of(v)
                + face[2, at : at + 8, :] * vec[j, at + 1 : at + 9, :]
                + face[2, at - 1 : at + 7, :] * vec[j, at - 1 : at + 7, :]
            ) * face[3, at : at + 8, :]
            new = image if j == 0 else image + image - vec[j - 1, at : at + 8, :]
            vec[j + 1, at : at + 8, :] = new
            if j < ITERS - 1 and 1 <= rb < 11:
                vecs[j + 1, 8 * rb - 8 : 8 * rb, :] = new
    count = ITERS + ITERS * (ITERS + 1) // 2
    sums = [None] * count
    for rb in range(ROWS // 8):
        for lt in range(COLS // LANES):
            lanes = slice(LANES * lt, LANES * (lt + 1))
            at = 24 + 8 * rb
            vs = [vec[j, at : at + 8, lanes] for j in range(ITERS + 1)]
            diag = coefs[5, 8 + 8 * rb : 16 + 8 * rb, lanes]
            forcing = f[8 * rb : 8 * rb + 8, lanes]
            terms = [forcing * vs[j] for j in range(ITERS)]
            for j in range(ITERS):
                turned = vs[1] if j == 0 else 0.5 * (vs[j + 1] + vs[j - 1])
                image = diag * (vs[j] - turned)
                terms += [image * vs[i] for i in range(j + 1)]
            sums = [t if a is None else a + t for a, t in zip(sums, terms)]
    part[...] = jnp.zeros((LANES, LANES), F32)
    for k in range(count):
        part[N_RHS + k : N_RHS + k + 1, :] = jnp.sum(sums[k], axis=0, keepdims=True)
    for n in range(COSTS):
        sums = [None] * ITERS
        for rb in range(ROWS // 8):
            for lt in range(COLS // LANES):
                lanes = slice(LANES * lt, LANES * (lt + 1))
                weight = w[n, 8 * rb : 8 * rb + 8, lanes]
                at = 24 + 8 * rb
                for j in range(ITERS):
                    t = weight * vec[j, at : at + 8, lanes]
                    sums[j] = t if sums[j] is None else sums[j] + t
        for j in range(ITERS):
            k = COSTS * j + n
            part[k : k + 1, :] = jnp.sum(sums[j], axis=0, keepdims=True)
    dots[...] = lax.dot_general(
        jnp.ones(dots.shape, F32), part[...], (((1,), (1,)), ((), ())),
        precision=HIGH, preferred_element_type=F32,
    )


def small_solve(total):
    wide = lambda k: jnp.broadcast_to(total[k : k + 1, :], (8, LANES))
    mat = {}
    k = N_MAT
    for j in range(ITERS):
        for i in range(j + 1):
            mat[j, i] = wide(k)
            k += 1
    low, inv = {}, []
    for j in range(ITERS):
        pivot = mat[j, j]
        for k in range(j):
            pivot = pivot - low[j, k] * mat[j, k]
        inv.append(1.0 / pivot)
        for i in range(j + 1, ITERS):
            entry = mat[i, j]
            for k in range(j):
                entry = entry - low[j, k] * mat[i, k]
            mat[i, j] = entry
            low[i, j] = entry * inv[j]

    def solve(rhs):
        y = []
        for i in range(ITERS):
            t = rhs[i]
            for k in range(i):
                t = t - low[i, k] * y[k]
            y.append(t)
        out = [None] * ITERS
        for i in range(ITERS - 1, -1, -1):
            t = y[i] * inv[i]
            for k in range(i + 1, ITERS):
                t = t - low[k, i] * out[k]
            out[i] = t
        return out

    return (
        solve([wide(N_RHS + i) for i in range(ITERS)]),
        solve([total[COSTS * j : COSTS * (j + 1), :] for j in range(ITERS)]),
    )


def triple(row):
    return jnp.concatenate([row, row, row], axis=1)


def adjoint_kernel(
    all_dots, vecs, coefs, mask, w, wside, ws, wn,
    adj, east, north,
    lam, cs, side, xs, ys, ss, ps, acc,
):
    n = pl.program_id(0)
    blocks = range(FRAME // 8)

    @pl.when(n == 0)
    def _():
        total = lax.dot_general(
            all_dots[...], jnp.ones(all_dots.shape, F32), (((0,), (0,)), ((), ())),
            precision=HIGH, preferred_element_type=F32,
        )
        c, weights = small_solve(total)
        for j in range(ITERS):
            lam[COSTS * j : COSTS * (j + 1), :] = weights[j]
            cs[8 * j : 8 * j + 8, :] = c[j]
        for rb in blocks:
            at = 8 + 8 * rb
            x = None
            for j in range(ITERS):
                t = triple(cs[8 * j : 8 * j + 8, :]) * vecs[j, 8 * rb : 8 * rb + 8, :]
                x = t if x is None else x + t
            xs[0, at : at + 8, :] = x
        for rb in blocks:
            at = 8 + 8 * rb
            x = xs[0, at : at + 8, :]
            xe, xn = east_of(x), xs[0, at + 1 : at + 9, :]
            here = slice(8 * rb, 8 * rb + 8)
            image = coefs[5, here, :] * x - (
                coefs[0, here, :] * xe + coefs[1, here, :] * west_of(x)
                + coefs[2, here, :] * xn + coefs[3, here, :] * xs[0, at - 1 : at + 7, :]
            )
            xs[1, at : at + 8, :] = coefs[6, here, :] - image
            if 1 <= rb < 9:
                own = slice(8 * rb - 8, 8 * rb)
                side[0, ITERS - 1, own, :] = xe[:, :COLS]
                side[1, ITERS - 1, own, :] = xn[:, :COLS]
                for j in range(ITERS - 1):
                    side[0, j, own, :] = east_of(vecs[j, here, :])[:, :COLS]
                    side[1, j, own, :] = vecs[j, 8 * rb + 1 : 8 * rb + 9, :COLS]

    rows = [triple(lam[pl.ds(COSTS * j + n, 1), :]) for j in range(ITERS)]

    def stencil(field, rb, ref_at):
        at = 8 + 8 * rb
        here = slice(8 * rb, 8 * rb + 8)
        fe, fw = east_of(field), west_of(field)
        fn, fs = ref_at(at + 1), ref_at(at - 1)
        image = (
            coefs[0, here, :] * fe + coefs[1, here, :] * fw
            + coefs[2, here, :] * fn + coefs[3, here, :] * fs
        )
        return image, fe, fn

    def gather(rb, field, fe, fn, slot, near, turned, first):
        at = 8 + 8 * rb
        if 1 <= rb < 9:
            own = slice(8 * rb - 8, 8 * rb)
            mid = field[:, :COLS]
            q = near[:, :COLS]
            e = mid * side[0, slot, own, :] + fe[:, :COLS] * q
            m = mid * side[1, slot, own, :] + fn[:, :COLS] * q
            acc[0, at : at + 8, :COLS] = e if first else acc[0, at : at + 8, :COLS] + e
            acc[1, at : at + 8, :COLS] = m if first else acc[1, at : at + 8, :COLS] + m
        if rb >= 1:
            d = field * turned
            acc[2, at : at + 8, :] = d if first else acc[2, at : at + 8, :] + d

    for rb in blocks:
        y = None
        for j in range(ITERS):
            t = rows[j] * vecs[j, 8 * rb : 8 * rb + 8, :]
            y = t if y is None else y + t
        ys[8 + 8 * rb : 16 + 8 * rb, :] = y
    for rb in blocks:
        at = 8 + 8 * rb
        here = slice(8 * rb, 8 * rb + 8)
        y = ys[at : at + 8, :]
        image, ye, yn = stencil(y, rb, lambda r: ys[r : r + 8, :])
        x = xs[0, at : at + 8, :]
        gather(rb, y, ye, yn, ITERS - 1, x, x, True)
        if rb == 0:
            weight = ws[...]
        elif rb == 9:
            weight = wn[...]
        else:
            weight = w[0, 8 * rb - 8 : 8 * rb, :]
        weight = jnp.concatenate([weight, wside[0, here, :]], axis=1)
        s = weight - coefs[5, here, :] * y + image
        ss[8 * rb : 8 * rb + 8, :] = s
        inv = coefs[4, here, :]
        bar = triple(cs[8 * ITERS - 8 : 8 * ITERS, :]) * s + rows[ITERS - 1] * xs[1, at : at + 8, :]
        ps[ITERS - 2, at : at + 8, :] = 2.0 * inv * bar
    for j in range(ITERS - 2, -1, -1):
        for rb in blocks:
            if j == 0 and rb == 0:
                continue
            at = 8 + 8 * rb
            here = slice(8 * rb, 8 * rb + 8)
            p = ps[j, at : at + 8, :]
            image, pe, pn = stencil(p, rb, lambda r: ps[j, r : r + 8, :])
            v = vecs[j, here, :]
            turned = vecs[1, here, :] if j == 0 else 0.5 * (vecs[j + 1, here, :] + vecs[j - 1, here, :])
            gather(rb, p, pe, pn, j, v, turned, False)
            u = triple(cs[8 * j : 8 * j + 8, :]) * ss[here, :] + rows[j] * xs[1, at : at + 8, :] + image
            scaled = coefs[4, here, :] * u
            if j >= 2:
                new = scaled + scaled
                if j + 1 <= ITERS - 2:
                    new = new - ps[j + 1, at : at + 8, :]
                ps[j - 1, at : at + 8, :] = new
            elif j == 1:
                ps[0, at : at + 8, :] = scaled - 0.5 * ps[2, at : at + 8, :]
            else:
                g = scaled - 0.5 * ps[1, at : at + 8, :]
                if rb < 9:
                    adj[0, 8 * rb - 8 : 8 * rb, :] = (ys[at : at + 8, :] + g)[:, :COLS]
                acc[2, at : at + 8, :] = acc[2, at : at + 8, :] + g * vecs[0, here, :]
    for rb in range(1, 9):
        at = 8 + 8 * rb
        own = slice(8 * rb - 8, 8 * rb)
        d = acc[2, at : at + 8, :]
        de = east_of(d)[:, :COLS]
        dn = acc[2, at + 1 : at + 9, :COLS]
        d = d[:, :COLS]
        east[0, own, :] = mask[0, own, :] * (acc[0, at : at + 8, :COLS] - d - de)
        north[0, own, :] = mask[1, own, :] * (acc[1, at : at + 8, :COLS] - d - dn)


def ring(axis, steps):
    count = lax.axis_size(axis)
    return [(source, (source + steps) % count) for source in range(count)]


def struct(*shape):
    return jax.ShapeDtypeStruct(shape, F32)


def whole():
    return pl.BlockSpec(memory_space=pltpu.VMEM)


def body(forcing, depth_east, depth_north, surface_term, ocean_mask, cost_weights):
    args = (forcing, depth_east, depth_north, surface_term, ocean_mask, cost_weights)
    lats = lax.axis_size("lat")
    devices = lats * lax.axis_size("lon")
    to_east, to_west = pl.pallas_call(
        strips_kernel,
        out_shape=(struct(ROWS, LANES), struct(ROWS, LANES)),
        name="strips",
    )(*args)
    side_w = lax.ppermute(to_east, "lon", ring("lon", 1))
    side_e = lax.ppermute(to_west, "lon", ring("lon", -1))

    def band_specs(top):
        field = pl.BlockSpec((EDGE, COLS), lambda i: (ROWS // EDGE - 1 if top else 0, 0))
        strip = pl.BlockSpec((EDGE, LANES), lambda i: (ROWS // EDGE - 1 if top else 0, 0))
        weights = pl.BlockSpec((COSTS, 8, COLS), lambda i: (0, ROWS // 8 - 1 if top else 0, 0))
        return [field] * 5 + [weights, strip, strip]

    sources = (*args, side_w, side_e)
    to_north, to_south = pl.pallas_call(
        bands_kernel,
        grid=(1,),
        in_specs=band_specs(True) + band_specs(False),
        out_specs=[pl.BlockSpec((MSG, COLS), lambda i: (0, 0))] * 2,
        out_shape=(struct(MSG, COLS), struct(MSG, COLS)),
        name="bands",
    )(*sources, *sources)
    band_s = lax.ppermute(to_north, "lat", ring("lat", 1))
    band_n = lax.ppermute(to_south, "lat", ring("lat", -1))
    row = lax.axis_index("lat")
    flags = jnp.stack([row > 0, row < lats - 1]).astype(jnp.int32)
    vecs, coefs, wside, wet, dots = pl.pallas_call(
        forward_kernel,
        in_specs=[pl.BlockSpec(memory_space=pltpu.SMEM)] + [whole()] * 10,
        out_specs=[whole()] * 5,
        out_shape=(
            struct(ITERS, FRAME, WIDE), struct(7, FRAME, WIDE),
            struct(COSTS, FRAME, LANES), struct(2, ROWS, COLS), struct(devices, LANES),
        ),
        scratch_shapes=[
            pltpu.VMEM((FIELDS, TALL + 16, WIDE), F32),
            pltpu.VMEM((4, TALL + 16, WIDE), F32),
            pltpu.VMEM((ITERS + 1, TALL + 16, WIDE), F32),
            pltpu.VMEM((LANES, LANES), F32),
        ],
        name="forward",
    )(flags, *args, band_s, band_n, side_w, side_e)
    all_dots = lax.all_to_all(dots, ("lat", "lon"), 0, 0, tiled=True)
    out_spec = pl.BlockSpec((1, ROWS, COLS), lambda n: (n, 0, 0))
    const3 = lambda a, b, c: pl.BlockSpec((a, b, c), lambda n: (0, 0, 0))
    return pl.pallas_call(
        adjoint_kernel,
        grid=(COSTS,),
        in_specs=[
            pl.BlockSpec((devices, LANES), lambda n: (0, 0)),
            const3(ITERS, FRAME, WIDE),
            const3(7, FRAME, WIDE),
            const3(2, ROWS, COLS),
            pl.BlockSpec((1, ROWS, COLS), lambda n: (n, 0, 0)),
            pl.BlockSpec((1, FRAME, LANES), lambda n: (n, 0, 0)),
            pl.BlockSpec((8, COLS), lambda n: (MSG_W // 8 + n, 0)),
            pl.BlockSpec((8, COLS), lambda n: (MSG_W // 8 + n, 0)),
        ],
        out_specs=[out_spec] * 3,
        out_shape=(struct(COSTS, ROWS, COLS),) * 3,
        scratch_shapes=[
            pltpu.VMEM((N_LAM, LANES), F32),
            pltpu.VMEM((8 * ITERS, LANES), F32),
            pltpu.VMEM((2, ITERS, ROWS, COLS), F32),
            pltpu.VMEM((2, FRAME + 16, WIDE), F32),
            pltpu.VMEM((FRAME + 16, WIDE), F32),
            pltpu.VMEM((FRAME, WIDE), F32),
            pltpu.VMEM((ITERS - 1, FRAME + 16, WIDE), F32),
            pltpu.VMEM((3, FRAME + 16, WIDE), F32),
        ],
        compiler_params=pltpu.CompilerParams(dimension_semantics=("arbitrary",)),
        name="adjoint",
    )(all_dots, vecs, coefs, wet, cost_weights, wside, band_s, band_n)


def solution(mesh):
    return jax.shard_map(
        body,
        mesh=mesh,
        in_specs=(P("lat", "lon"),) * 5 + (P(None, "lat", "lon"),),
        out_specs=(P(None, "lat", "lon"),) * 3,
        check_vma=False,
    )
```

time: 890 us -> 63 us (0.07); the launches traced: 875 us -> 62.6 us
  blocking collectives: 612 us -> 28.8 us
  starting transfers between devices: 104 us -> 6.78 us
  other arithmetic: 54.5 us -> 0.66 us
  between operations: 42.9 us -> 0.64 us
  waiting for transfers between devices: 47.1 us -> 5.62 us
  Pallas kernels: 0 us -> 18.1 us
  local copies, waits for them, and re-layouts: 14.1 us -> 1.96 us
    psum x65 -> x0, blocking collectives: 612 us -> none  [by_axis(): return functools.reduce(lax.psum, axes, array)]
    ppermute x50 -> x4, starting transfers between devices: 104 us -> 6.78 us  [the longest x1 3.02 us: body(): side_w = lax.ppermute(to_east, 'lon', ring('lon', 1))]
    ppermute x50 -> x4, waiting for transfers between devices: 47.1 us -> 5.62 us  [the longest x1 2.25 us: body(): band_s = lax.ppermute(to_north, 'lat', ring('lat', 1))]
    all_to_all x0 -> x1, blocking collectives: none -> 28.8 us  [body(): all_dots = lax.all_to_all(dots, ('lat', 'lon'), 0, 0, tiled=True)]
    reduce_sum x13 -> x0, other arithmetic: 18.9 us -> none  [the longest x3 8.84 us: body(): jnp.sum(scaled * image, axis=(1, 2))]
    pallas_call x0 -> x4, Pallas kernels: none -> 18.1 us  [the longest x1 10.3 us: body(): pl.pallas_call(adjoint_kernel, grid=(COSTS,), in_specs=[pl.BlockSpec((dev...]
    unnamed x238 -> x8, local copies, waits for them, and re-layouts: 12.6 us -> 1.96 us
    mul x13 -> x0, other arithmetic: 10.2 us -> none  [the longest x1 2.58 us: body(): 2.0 * norm_bar[:, None, None] * precond_first]
  transfers between devices with their start and end apart: 50 -> 4, of which waited for: 24 -> 3; matrix products, arithmetic and copies ran while one was open for 0% -> 1% of each run, Pallas kernels for 0% -> 0%
where the time goes in v1:
time: 63 us; the launch traced here: 62.6 us
  blocking collectives  28.8 us (46%)
  Pallas kernels  18.1 us (29%)
  starting transfers between devices  6.78 us (11%)
  waiting for transfers between devices  5.62 us (9%)
  local copies, waits for them, and re-layouts  1.96 us (3%)
  other arithmetic  0.66 us (1%)
  between operations  0.64 us (1%)
    all_to_all x1, blocking collectives, body(): all_dots = lax.all_to_all(dots, ('lat', 'lon'), 0, 0, tiled=True)  28.8 us
    pallas_call x1, Pallas kernels, body(): pl.pallas_call(adjoint_kernel, grid=(COSTS,), in_specs=[pl.BlockSpec((dev...  10.3 us
    pallas_call x1, Pallas kernels, body(): pl.pallas_call(forward_kernel, in_specs=[pl.BlockSpec(memory_space=pltpu....  4.02 us
    ppermute x1, starting transfers between devices, body(): side_w = lax.ppermute(to_east, 'lon', ring('lon', 1))  3.02 us
    ppermute x1, starting transfers between devices, body(): band_n = lax.ppermute(to_south, 'lat', ring('lat', -1))  2.36 us
    ppermute x1, waiting for transfers between devices, body(): band_s = lax.ppermute(to_north, 'lat', ring('lat', 1))  2.25 us
    ppermute x1, waiting for transfers between devices, body(): side_e = lax.ppermute(to_west, 'lon', ring('lon', -1))  2.21 us
    pallas_call x1, Pallas kernels, body(): pl.pallas_call(strips_kernel, out_shape=(struct(ROWS, LANES), struct(ROWS...  2.12 us
  transfers between devices with their start and end apart: 4, of which 3 were waited for; matrix products, arithmetic and copies ran while one was open for 1% of the time, Pallas kernels for 0%

profile of v1, /device:TPU:1, one launch (start us, length us, event | category | flops | bytes accessed | tf_op | source)
XLA Modules:
  0.0 62.6 jit_solution(17664264506877698909)
XLA Ops:
  0.6 2.1 %strips.1 = (f32[64,128]{1,0:T(8,128)}, f32[64,128]{1,0:T(8,128)}) custom-call(f32[64,256]{1,0:T(8,128)} %f.3, f32[64,256]{1,0:T(8,128)} %de.3, f32[64,256]{1,0:T(8,128)} %dn.3, f32[64,256]{1,0:T(8,128)} %st.3, s32[64,256]{1,0:T(8,128)} %mask.3, f32[8,64,256]{2,1,0:T(8,128)} %w.5), custom_call_target="tpu_custom_call" | custom-call | tf_op jit(solution)/shard_map/strips/pallas_call | solution.py:393
  2.8 3.0 %collective-permute-start = (f32[64,128]{1,0:T(8,128)}, f32[64,128]{1,0:T(8,128)S(1)}, u32[]{:S(2)}, u32[]{:S(2)}) collective-permute-start(f32[64,128]{1,0:T(8,128)} %get-tuple-element.12), channel_id=1, source_target_pairs={{0,1},{1,2},{2,3},{3,4},{4,5},{5,6},{6,7},{7,8},{8,9},{9,10},{10,1... | collective-permute-start | bytes 98312 | tf_op jit(solution)/shard_map/ppermute | solution.py:398
  5.8 0.2 collective-permute-start.1
  6.0 1.2 %collective-permute-done.refs_6_.refs_14_.sw = f32[64,128]{1,0:T(8,128)S(1)} collective-permute-done((f32[64,128]{1,0:T(8,128)}, f32[64,128]{1,0:T(8,128)S(1)}, u32[]{:S(2)}, u32[]{:S(2)}) %collective-permute-start) | collective-permute-done | bytes 32800 | tf_op jit(solution)/shard_map/ppermute | solution.py:398
  7.1 0.0 copy-start.2
  7.1 2.2 %collective-permute-done.1.refs_7_.refs_15_.se = f32[64,128]{1,0:T(8,128)S(1)} collective-permute-done((f32[64,128]{1,0:T(8,128)}, f32[64,128]{1,0:T(8,128)S(1)}, u32[]{:S(2)}, u32[]{:S(2)}) %collective-permute-start.1) | collective-permute-done | bytes 32800 | tf_op jit(solution)/shard_map/ppermute | solution.py:399
  9.3 0.0 copy-done.2
  9.3 0.0 copy-start.3
  9.3 0.6 copy-done.3
  9.9 1.7 %bands.1 = (f32[160,256]{1,0:T(8,128)}, f32[160,256]{1,0:T(8,128)}) custom-call(f32[64,256]{1,0:T(8,128)} %f.3, f32[64,256]{1,0:T(8,128)} %de.3, f32[64,256]{1,0:T(8,128)} %dn.3, f32[64,256]{1,0:T(8,128)} %st.3, s32[64,256]{1,0:T(8,128)} %mask.3, f32[8,64,256]{2,1,0:T(8,128)} %w.5, f32[64,128]{1,0:T(8,128)} %copy-done.2, f32[64,128]{1,0:T(8,128)} %copy-done.3, ...), custom_call_target="tpu_custom_call" | custom-call | tf_op jit(solution)/shard_map/bands/pallas_call | solution.py:408
  11.6 1.2 %collective-permute-start.2 = (f32[160,256]{1,0:T(8,128)}, f32[160,256]{1,0:T(8,128)S(1)}, u32[]{:S(2)}, u32[]{:S(2)}) collective-permute-start(f32[160,256]{1,0:T(8,128)} %get-tuple-element.14), channel_id=1, source_target_pairs={{0,32},{32,64},{64,96},{96,128},{128,160},{160,192},{192,224},{224... | collective-permute-start | bytes 491528 | tf_op jit(solution)/shard_map/ppermute | solution.py:416
  12.8 2.4 %collective-permute-start.3 = (f32[160,256]{1,0:T(8,128)}, f32[160,256]{1,0:T(8,128)S(1)}, u32[]{:S(2)}, u32[]{:S(2)}) collective-permute-start(f32[160,256]{1,0:T(8,128)} %get-tuple-element.15), channel_id=1, source_target_pairs={{0,224},{32,0},{64,32},{96,64},{128,96},{160,128},{192,160},{224,1... | collective-permute-start | bytes 491528 | tf_op jit(solution)/shard_map/ppermute | solution.py:417
  15.2 0.7 %add_convert_fusion.flags = s32[2]{0:T(128)} fusion(pred[1]{0:T(512)(128)(4,1)} %bitcast.1, pred[1]{0:T(512)(128)(4,1)} %bitcast), kind=kLoop, calls=%fused_computation | loop fusion | flops 4 | bytes 10 | tf_op jit(solution)/shard_map/convert_element_type | solution.py:419
  15.9 2.3 %collective-permute-done.2.ls.ws = f32[160,256]{1,0:T(8,128)S(1)} collective-permute-done((f32[160,256]{1,0:T(8,128)}, f32[160,256]{1,0:T(8,128)S(1)}, u32[]{:S(2)}, u32[]{:S(2)}) %collective-permute-start.2) | collective-permute-done | bytes 163872 | tf_op jit(solution)/shard_map/ppermute | solution.py:416
  18.1 0.0 copy-start
  18.1 0.0 collective-permute-done.3.ln.wn
  18.1 0.7 %copy-done = f32[160,256]{1,0:T(8,128)} copy-done((f32[160,256]{1,0:T(8,128)}, f32[160,256]{1,0:T(8,128)S(1)}, u32[]{:S(2)}) %copy-start) | copy-done | bytes 163864
  18.8 0.0 copy-start.1
  18.8 0.7 %copy-done.1 = f32[160,256]{1,0:T(8,128)} copy-done((f32[160,256]{1,0:T(8,128)}, f32[160,256]{1,0:T(8,128)S(1)}, u32[]{:S(2)}) %copy-start.1) | copy-done | bytes 163864
  19.5 4.0 %forward.1 = (f32[6,80,384]{2,1,0:T(8,128)}, f32[7,80,384]{2,1,0:T(8,128)}, f32[8,80,128]{2,1,0:T(8,128)}, f32[2,64,256]{2,1,0:T(8,128)}, f32[256,128]{1,0:T(8,128)}) custom-call(s32[2]{0:T(128)} %add_convert_fusion.flags, f32[64,256]{1,0:T(8,128)} %f.3, f32[64,256]{1,0:T(8,128)} %de.3, f32[64,256]{1,0:T(8,128)} %dn.3, f32[64,256]{1,0:T(8,128)} %st.3, ...), custom_call_target="tpu_custom_call" | custom-call | tf_op jit(solution)/shard_map/forward/pallas_call | solution.py:420
  23.5 28.8 %all_to_all.11 = f32[256,1,128]{2,1,0:T(1,128)} all-to-all(f32[256,1,128]{2,1,0:T(1,128)} %bitcast.7), channel_id=1, replica_groups=mesh['lat'=8,'lon'=32] {'lat','lon'}, dimensions={0} | all-to-all | bytes 262144 | tf_op jit(solution)/shard_map/all_to_all | solution.py:436
  52.3 10.3 %adjoint.1 = (f32[8,64,256]{2,1,0:T(8,128)}, f32[8,64,256]{2,1,0:T(8,128)}, f32[8,64,256]{2,1,0:T(8,128)}) custom-call(f32[256,128]{1,0:T(8,128)} %bitcast.6, f32[6,80,384]{2,1,0:T(8,128)} %get-tuple-element.17.vecs, f32[7,80,384]{2,1,0:T(8,128)} %get-tuple-element.18.coefs, f32[2,64,256]{2,1,0:T(8,128)} %get-tuple-element.19.mask, f32[8,64,256]{2,1,0:T(8,128)} %w.5, ...), custom_call_target="tpu_custom_call" | custom-call | tf_op jit(solution)/shard_map/adjoint/pallas_call | solution.py:439
Async XLA Ops:
  2.8 4.4 %collective-permute-start = (f32[64,128]{1,0:T(8,128)}, f32[64,128]{1,0:T(8,128)S(1)}, u32[]{:S(2)}, u32[]{:S(2)}) collective-permute-start(f32[64,128]{1,0:T(8,128)} %get-tuple-element.12), channel_id=1, source_target_pairs={{0,1},{1,2},{2,3},{3,4},{4,5},{5,6},{6,7},{7,8},{8,9},{9,10},{10,1... | collective-permute-start | bytes 98312 | tf_op jit(solution)/shard_map/ppermute | solution.py:398
  5.8 3.6 %collective-permute-start.1 = (f32[64,128]{1,0:T(8,128)}, f32[64,128]{1,0:T(8,128)S(1)}, u32[]{:S(2)}, u32[]{:S(2)}) collective-permute-start(f32[64,128]{1,0:T(8,128)} %get-tuple-element.13), channel_id=1, source_target_pairs={{0,31},{1,0},{2,1},{3,2},{4,3},{5,4},{6,5},{7,6},{8,7},{9,8},{10,9... | collective-permute-start | bytes 98312 | tf_op jit(solution)/shard_map/ppermute | solution.py:399
  7.1 2.2 %copy-start.2 = (f32[64,128]{1,0:T(8,128)}, f32[64,128]{1,0:T(8,128)S(1)}, u32[]{:S(2)}) copy-start(f32[64,128]{1,0:T(8,128)S(1)} %collective-permute-done.refs_6_.refs_14_.sw) | copy-start | bytes 98308
  9.3 0.6 copy-start.3
  11.6 6.5 %collective-permute-start.2 = (f32[160,256]{1,0:T(8,128)}, f32[160,256]{1,0:T(8,128)S(1)}, u32[]{:S(2)}, u32[]{:S(2)}) collective-permute-start(f32[160,256]{1,0:T(8,128)} %get-tuple-element.14), channel_id=1, source_target_pairs={{0,32},{32,64},{64,96},{96,128},{128,160},{160,192},{192,224},{224... | collective-permute-start | bytes 491528 | tf_op jit(solution)/shard_map/ppermute | solution.py:416
  12.8 5.3 %collective-permute-start.3 = (f32[160,256]{1,0:T(8,128)}, f32[160,256]{1,0:T(8,128)S(1)}, u32[]{:S(2)}, u32[]{:S(2)}) collective-permute-start(f32[160,256]{1,0:T(8,128)} %get-tuple-element.15), channel_id=1, source_target_pairs={{0,224},{32,0},{64,32},{96,64},{128,96},{160,128},{192,160},{224,1... | collective-permute-start | bytes 491528 | tf_op jit(solution)/shard_map/ppermute | solution.py:417
  18.1 0.7 %copy-start = (f32[160,256]{1,0:T(8,128)}, f32[160,256]{1,0:T(8,128)S(1)}, u32[]{:S(2)}) copy-start(f32[160,256]{1,0:T(8,128)S(1)} %collective-permute-done.2.ls.ws) | copy-start | bytes 491524
  18.8 0.7 %copy-start.1 = (f32[160,256]{1,0:T(8,128)}, f32[160,256]{1,0:T(8,128)S(1)}, u32[]{:S(2)}) copy-start(f32[160,256]{1,0:T(8,128)S(1)} %collective-permute-done.3.ln.wn) | copy-start | bytes 491524

commit v2 on v1

--- a/solution.py
+++ b/solution.py
@@ -393,6 +393,7 @@
     to_east, to_west = pl.pallas_call(
         strips_kernel,
         out_shape=(struct(ROWS, LANES), struct(ROWS, LANES)),
+        compiler_params=pltpu.CompilerParams(vmem_limit_bytes=4 << 20),
         name="strips",
     )(*args)
     side_w = lax.ppermute(to_east, "lon", ring("lon", 1))
@@ -411,6 +412,7 @@
         in_specs=band_specs(True) + band_specs(False),
         out_specs=[pl.BlockSpec((MSG, COLS), lambda i: (0, 0))] * 2,
         out_shape=(struct(MSG, COLS), struct(MSG, COLS)),
+        compiler_params=pltpu.CompilerParams(vmem_limit_bytes=4 << 20),
         name="bands",
     )(*sources, *sources)
     band_s = lax.ppermute(to_north, "lat", ring("lat", 1))
@@ -431,6 +433,7 @@
             pltpu.VMEM((ITERS + 1, TALL + 16, WIDE), F32),
             pltpu.VMEM((LANES, LANES), F32),
         ],
+        compiler_params=pltpu.CompilerParams(vmem_limit_bytes=12 << 20),
         name="forward",
     )(flags, *args, band_s, band_n, side_w, side_e)
     all_dots = lax.all_to_all(dots, ("lat", "lon"), 0, 0, tiled=True)
@@ -461,7 +464,7 @@
             pltpu.VMEM((ITERS - 1, FRAME + 16, WIDE), F32),
             pltpu.VMEM((3, FRAME + 16, WIDE), F32),
         ],
-        compiler_params=pltpu.CompilerParams(dimension_semantics=("arbitrary",)),
+        compiler_params=pltpu.CompilerParams(dimension_semantics=("arbitrary",), vmem_limit_bytes=14 << 20),
         name="adjoint",
     )(all_dots, vecs, coefs, wet, cost_weights, wside, band_s, band_n)
 

time: 63 us -> 59.9 us (0.951)
  Pallas kernels: 18.1 us -> 11.6 us
  local copies, waits for them, and re-layouts: 1.96 us -> 5.26 us
    unnamed x8 -> x24, local copies, waits for them, and re-layouts: 1.96 us -> 5.26 us
    pallas_call x1, Pallas kernels: 2.12 us -> 0.28 us  [body(): pl.pallas_call(strips_kernel, out_shape=(struct(ROWS, LANES), struct(ROWS...]
    pallas_call x1, Pallas kernels: 4.02 us -> 2.26 us  [body(): pl.pallas_call(forward_kernel, in_specs=[pl.BlockSpec(memory_space=pltpu....]
    pallas_call x1, Pallas kernels: 1.7 us -> 0.03 us  [body(): pl.pallas_call(bands_kernel, grid=(1,), in_specs=band_specs(True) + band_...]
    pallas_call x1, Pallas kernels: 10.3 us -> 9.05 us  [body(): pl.pallas_call(adjoint_kernel, grid=(COSTS,), in_specs=[pl.BlockSpec((dev...]
  transfers between devices with their start and end apart: 4 -> 4, of which waited for: 3 -> 3; matrix products, arithmetic and copies ran while one was open for 1% -> 0% of each run, Pallas kernels for 0% -> 0%
where the time goes in v2:
time: 59.9 us; the launch traced here: 59.5 us
  blocking collectives  29.1 us (49%)
  Pallas kernels  11.6 us (19%)
  starting transfers between devices  7.04 us (12%)
  waiting for transfers between devices  5.68 us (9%)
  local copies, waits for them, and re-layouts  5.26 us (9%)
  between operations  0.72 us (1%)
    all_to_all x1, blocking collectives, body(): all_dots = lax.all_to_all(dots, ('lat', 'lon'), 0, 0, tiled=True)  29.1 us
    pallas_call x1, Pallas kernels, body(): pl.pallas_call(adjoint_kernel, grid=(COSTS,), in_specs=[pl.BlockSpec((dev...  9.05 us
    unnamed x24, local copies, waits for them, and re-layouts  5.26 us
    ppermute x1, starting transfers between devices, body(): side_w = lax.ppermute(to_east, 'lon', ring('lon', 1))  3.09 us
    ppermute x1, waiting for transfers between devices, body(): band_s = lax.ppermute(to_north, 'lat', ring('lat', 1))  2.62 us
    ppermute x1, starting transfers between devices, body(): band_n = lax.ppermute(to_south, 'lat', ring('lat', -1))  2.37 us
    ppermute x1, waiting for transfers between devices, body(): side_e = lax.ppermute(to_west, 'lon', ring('lon', -1))  2.32 us
    pallas_call x1, Pallas kernels, body(): pl.pallas_call(forward_kernel, in_specs=[pl.BlockSpec(memory_space=pltpu....  2.26 us
  transfers between devices with their start and end apart: 4, of which 3 were waited for; matrix products, arithmetic and copies ran while one was open for 0% of the time, Pallas kernels for 0%

profile of v2, /device:TPU:1, one launch (start us, length us, event | category | flops | bytes accessed | tf_op | source)
XLA Modules:
  0.0 59.5 jit_solution(12469697153638036804)
XLA Ops:
  0.6 0.0 copy-start
  0.6 1.0 %copy-done = f32[8,64,256]{2,1,0:T(8,128)S(1)} copy-done((f32[8,64,256]{2,1,0:T(8,128)S(1)}, f32[8,64,256]{2,1,0:T(8,128)}, u32[]{:S(2)}) %copy-start) | copy-done | bytes 524312
  1.7 0.0 copy-start.2
  1.7 0.8 %copy-done.2 = f32[64,256]{1,0:T(8,128)S(1)} copy-done((f32[64,256]{1,0:T(8,128)S(1)}, f32[64,256]{1,0:T(8,128)}, u32[]{:S(2)}) %copy-start.2) | copy-done | bytes 65560
  2.5 0.0 copy-start.4
  2.5 0.8 %copy-done.4 = f32[64,256]{1,0:T(8,128)S(1)} copy-done((f32[64,256]{1,0:T(8,128)S(1)}, f32[64,256]{1,0:T(8,128)}, u32[]{:S(2)}) %copy-start.4) | copy-done | bytes 65560
  3.4 0.0 copy-start.6
  3.4 0.8 %copy-done.6 = f32[64,256]{1,0:T(8,128)S(1)} copy-done((f32[64,256]{1,0:T(8,128)S(1)}, f32[64,256]{1,0:T(8,128)}, u32[]{:S(2)}) %copy-start.6) | copy-done | bytes 65560
  4.2 0.0 copy-start.8
  4.2 0.8 %copy-done.8 = f32[64,256]{1,0:T(8,128)S(1)} copy-done((f32[64,256]{1,0:T(8,128)S(1)}, f32[64,256]{1,0:T(8,128)}, u32[]{:S(2)}) %copy-start.8) | copy-done | bytes 65560
  5.0 0.0 copy-start.10
  5.0 0.8 %copy-done.10 = s32[64,256]{1,0:T(8,128)S(1)} copy-done((s32[64,256]{1,0:T(8,128)S(1)}, s32[64,256]{1,0:T(8,128)}, u32[]{:S(2)}) %copy-start.10) | copy-done | bytes 65560
  5.9 0.3 strips.1
  6.2 3.1 %collective-permute-start = (f32[64,128]{1,0:T(8,128)S(1)}, f32[64,128]{1,0:T(8,128)S(1)}, u32[]{:S(2)}, u32[]{:S(2)}) collective-permute-start(f32[64,128]{1,0:T(8,128)S(1)} %get-tuple-element.12), channel_id=1, source_target_pairs={{0,1},{1,2},{2,3},{3,4},{4,5},{5,6},{6,7},{7,8},{8,9},{9,10},{10,1... | collective-permute-start | bytes 98312 | tf_op jit(solution)/shard_map/ppermute | solution.py:399
  9.3 0.3 collective-permute-start.1
  9.5 0.7 %collective-permute-done.refs_6_.refs_14_.sw = f32[64,128]{1,0:T(8,128)S(1)} collective-permute-done((f32[64,128]{1,0:T(8,128)S(1)}, f32[64,128]{1,0:T(8,128)S(1)}, u32[]{:S(2)}, u32[]{:S(2)}) %collective-permute-start) | collective-permute-done | bytes 32800 | tf_op jit(solution)/shard_map/ppermute | solution.py:399
  10.3 2.3 %collective-permute-done.1.refs_7_.refs_15_.se = f32[64,128]{1,0:T(8,128)S(1)} collective-permute-done((f32[64,128]{1,0:T(8,128)S(1)}, f32[64,128]{1,0:T(8,128)S(1)}, u32[]{:S(2)}, u32[]{:S(2)}) %collective-permute-start.1) | collective-permute-done | bytes 32800 | tf_op jit(solution)/shard_map/ppermute | solution.py:400
  12.6 0.0 copy-start.11
  12.7 1.3 %collective-permute-start.2 = (f32[160,256]{1,0:T(8,128)S(1)}, f32[160,256]{1,0:T(8,128)S(1)}, u32[]{:S(2)}, u32[]{:S(2)}) collective-permute-start(f32[160,256]{1,0:T(8,128)S(1)} %get-tuple-element.14), channel_id=1, source_target_pairs={{0,32},{32,64},{64,96},{96,128},{128,160},{160,192},{192,224},{224... | collective-permute-start | bytes 491528 | tf_op jit(solution)/shard_map/ppermute | solution.py:418
  13.9 2.4 %collective-permute-start.3 = (f32[160,256]{1,0:T(8,128)S(1)}, f32[160,256]{1,0:T(8,128)S(1)}, u32[]{:S(2)}, u32[]{:S(2)}) collective-permute-start(f32[160,256]{1,0:T(8,128)S(1)} %get-tuple-element.15), channel_id=1, source_target_pairs={{0,224},{32,0},{64,32},{96,64},{128,96},{160,128},{192,160},{224,1... | collective-permute-start | bytes 491528 | tf_op jit(solution)/shard_map/ppermute | solution.py:419
  16.3 0.1 add_convert_fusion.flags
  16.4 2.6 %collective-permute-done.2.ls.ws = f32[160,256]{1,0:T(8,128)S(1)} collective-permute-done((f32[160,256]{1,0:T(8,128)S(1)}, f32[160,256]{1,0:T(8,128)S(1)}, u32[]{:S(2)}, u32[]{:S(2)}) %collective-permute-start.2) | collective-permute-done | bytes 163872 | tf_op jit(solution)/shard_map/ppermute | solution.py:418
  19.0 0.0 collective-permute-done.3.ln.wn
  19.0 0.0 copy-done.1
  19.0 0.0 copy-done.3
  19.0 0.0 copy-done.5
  19.0 0.0 copy-done.7
  19.0 0.0 copy-done.9
  19.1 0.0 copy-done.11
  19.1 2.3 %forward.1 = (f32[6,80,384]{2,1,0:T(8,128)S(1)}, f32[7,80,384]{2,1,0:T(8,128)S(1)}, f32[8,80,128]{2,1,0:T(8,128)S(1)}, f32[2,64,256]{2,1,0:T(8,128)S(1)}, f32[256,128]{1,0:T(8,128)S(1)}) custom-call(s32[2]{0:T(128)S(1)} %add_convert_fusion.flags, f32[64,256]{1,0:T(8,128)S(1)} %copy-done.3, f32[64,256]{1,0:T(8,128)S(1)} %copy-done.5, ...), custom_call_target="tpu_custom_call" | custom-call | tf_op jit(solution)/shard_map/forward/pallas_call | solution.py:422
  21.3 29.1 %all_to_all.11 = f32[256,1,128]{2,1,0:T(1,128)S(1)} all-to-all(f32[256,1,128]{2,1,0:T(1,128)S(1)} %bitcast.7), channel_id=1, replica_groups=mesh['lat'=8,'lon'=32] {'lat','lon'}, dimensions={0} | all-to-all | bytes 262144 | tf_op jit(solution)/shard_map/all_to_all | solution.py:439
  50.5 9.1 %adjoint.1 = (f32[8,64,256]{2,1,0:T(8,128)}, f32[8,64,256]{2,1,0:T(8,128)}, f32[8,64,256]{2,1,0:T(8,128)}) custom-call(f32[256,128]{1,0:T(8,128)S(1)} %bitcast.6, f32[6,80,384]{2,1,0:T(8,128)S(1)} %get-tuple-element.17.vecs, f32[7,80,384]{2,1,0:T(8,128)S(1)} %get-tuple-element.18.coefs, f32[2,64,256]{2,1,0:T(8,128)S(1)} %get-tuple-element.19.mask, ...), custom_call_target="tpu_custom_call" | custom-call | tf_op jit(solution)/shard_map/adjoint/pallas_call | solution.py:442
  (6 shorter events, 0.0 us)
Async XLA Ops:
  0.6 1.0 %copy-start = (f32[8,64,256]{2,1,0:T(8,128)S(1)}, f32[8,64,256]{2,1,0:T(8,128)}, u32[]{:S(2)}) copy-start(f32[8,64,256]{2,1,0:T(8,128)} %w.5) | copy-start | bytes 1572868
  1.7 0.8 %copy-start.2 = (f32[64,256]{1,0:T(8,128)S(1)}, f32[64,256]{1,0:T(8,128)}, u32[]{:S(2)}) copy-start(f32[64,256]{1,0:T(8,128)} %f.3) | copy-start | bytes 196612
  2.5 0.8 %copy-start.4 = (f32[64,256]{1,0:T(8,128)S(1)}, f32[64,256]{1,0:T(8,128)}, u32[]{:S(2)}) copy-start(f32[64,256]{1,0:T(8,128)} %de.3) | copy-start | bytes 196612
  3.4 0.8 %copy-start.6 = (f32[64,256]{1,0:T(8,128)S(1)}, f32[64,256]{1,0:T(8,128)}, u32[]{:S(2)}) copy-start(f32[64,256]{1,0:T(8,128)} %dn.3) | copy-start | bytes 196612
  4.2 0.8 %copy-start.8 = (f32[64,256]{1,0:T(8,128)S(1)}, f32[64,256]{1,0:T(8,128)}, u32[]{:S(2)}) copy-start(f32[64,256]{1,0:T(8,128)} %st.3) | copy-start | bytes 196612
  5.0 0.8 %copy-start.10 = (s32[64,256]{1,0:T(8,128)S(1)}, s32[64,256]{1,0:T(8,128)}, u32[]{:S(2)}) copy-start(s32[64,256]{1,0:T(8,128)} %mask.3) | copy-start | bytes 196612
  6.2 4.1 %collective-permute-start = (f32[64,128]{1,0:T(8,128)S(1)}, f32[64,128]{1,0:T(8,128)S(1)}, u32[]{:S(2)}, u32[]{:S(2)}) collective-permute-start(f32[64,128]{1,0:T(8,128)S(1)} %get-tuple-element.12), channel_id=1, source_target_pairs={{0,1},{1,2},{2,3},{3,4},{4,5},{5,6},{6,7},{7,8},{8,9},{9,10},{10,1... | collective-permute-start | bytes 98312 | tf_op jit(solution)/shard_map/ppermute | solution.py:399
  9.3 9.8 %copy-start.1 = (f32[8,64,256]{2,1,0:T(8,128)S(1)}, f32[8,64,256]{2,1,0:T(8,128)}, u32[]{:S(2)}) copy-start(f32[8,64,256]{2,1,0:T(8,128)} %w.5) | copy-start | bytes 1572868
  9.3 3.3 %collective-permute-start.1 = (f32[64,128]{1,0:T(8,128)S(1)}, f32[64,128]{1,0:T(8,128)S(1)}, u32[]{:S(2)}, u32[]{:S(2)}) collective-permute-start(f32[64,128]{1,0:T(8,128)S(1)} %get-tuple-element.13), channel_id=1, source_target_pairs={{0,31},{1,0},{2,1},{3,2},{4,3},{5,4},{6,5},{7,6},{8,7},{9,8},{10,9... | collective-permute-start | bytes 98312 | tf_op jit(solution)/shard_map/ppermute | solution.py:400
  12.6 6.4 %copy-start.3 = (f32[64,256]{1,0:T(8,128)S(1)}, f32[64,256]{1,0:T(8,128)}, u32[]{:S(2)}) copy-start(f32[64,256]{1,0:T(8,128)} %f.3) | copy-start | bytes 196612
  12.6 6.4 %copy-start.5 = (f32[64,256]{1,0:T(8,128)S(1)}, f32[64,256]{1,0:T(8,128)}, u32[]{:S(2)}) copy-start(f32[64,256]{1,0:T(8,128)} %de.3) | copy-start | bytes 196612
  12.6 6.4 %copy-start.7 = (f32[64,256]{1,0:T(8,128)S(1)}, f32[64,256]{1,0:T(8,128)}, u32[]{:S(2)}) copy-start(f32[64,256]{1,0:T(8,128)} %dn.3) | copy-start | bytes 196612
  12.6 6.4 %copy-start.9 = (f32[64,256]{1,0:T(8,128)S(1)}, f32[64,256]{1,0:T(8,128)}, u32[]{:S(2)}) copy-start(f32[64,256]{1,0:T(8,128)} %st.3) | copy-start | bytes 196612
  12.6 6.4 %copy-start.11 = (s32[64,256]{1,0:T(8,128)S(1)}, s32[64,256]{1,0:T(8,128)}, u32[]{:S(2)}) copy-start(s32[64,256]{1,0:T(8,128)} %mask.3) | copy-start | bytes 196612
  12.7 6.4 %collective-permute-start.2 = (f32[160,256]{1,0:T(8,128)S(1)}, f32[160,256]{1,0:T(8,128)S(1)}, u32[]{:S(2)}, u32[]{:S(2)}) collective-permute-start(f32[160,256]{1,0:T(8,128)S(1)} %get-tuple-element.14), channel_id=1, source_target_pairs={{0,32},{32,64},{64,96},{96,128},{128,160},{160,192},{192,224},{224... | collective-permute-start | bytes 491528 | tf_op jit(solution)/shard_map/ppermute | solution.py:418
  13.9 5.1 %collective-permute-start.3 = (f32[160,256]{1,0:T(8,128)S(1)}, f32[160,256]{1,0:T(8,128)S(1)}, u32[]{:S(2)}, u32[]{:S(2)}) collective-permute-start(f32[160,256]{1,0:T(8,128)S(1)} %get-tuple-element.15), channel_id=1, source_target_pairs={{0,224},{32,0},{64,32},{96,64},{128,96},{160,128},{192,160},{224,1... | collective-permute-start | bytes 491528 | tf_op jit(solution)/shard_map/ppermute | solution.py:419

commit v3 on v2

--- a/solution.py
+++ b/solution.py
@@ -20,8 +20,7 @@
 FRAME = 80
 TALL = 96
 MSG_W = FIELDS * EDGE
-MSG_C = MSG_W + COSTS * 8
-MSG = MSG_C + EDGE
+MSG = MSG_W + COSTS * 8
 N_LAM = COSTS * ITERS
 N_RHS = N_LAM
 N_MAT = N_LAM + ITERS
@@ -45,32 +44,64 @@
     return pltpu.roll(value, 1, 1)
 
 
-def strips_kernel(f, de, dn, st, mask, w, to_east, to_west):
-    lane = lane_index(ROWS)
+def pack(rows, tiles):
+    lane = lane_index(rows)
+    out = jnp.zeros((rows, LANES), F32)
+    at = 0
+    for tile, first, wide in tiles:
+        if tile is not None:
+            here = (lane >= at) & (lane < at + wide)
+            out = jnp.where(here, turn(tile, at - first), out)
+        at += wide
+    return out
+
+
+def bands_kernel(f, de, dn, st, mask, w, to_north, to_south, whole_mask, sems):
+    copies = []
+    for side, out in enumerate((to_north, to_south)):
+        low = ROWS - EDGE if side == 0 else 0
+        rows = pl.ds(low, EDGE)
+        for k, field in enumerate((f, de, dn, st)):
+            copies.append((field.at[rows, :], out.at[pl.ds(EDGE * k, EDGE), :]))
+        copies.append((mask.at[rows, :], whole_mask.at[side]))
+        low = ROWS - 8 if side == 0 else 0
+        for n in range(COSTS):
+            copies.append((w.at[n, pl.ds(low, 8), :], out.at[pl.ds(MSG_W + 8 * n, 8), :]))
+    copies = [
+        pltpu.make_async_copy(src, dst, sems.at[i]) for i, (src, dst) in enumerate(copies)
+    ]
+    for copy in copies:
+        copy.start()
+    for copy in copies:
+        copy.wait()
+    to_north[MSG_W - EDGE : MSG_W, :] = whole_mask[0].astype(F32)
+    to_south[MSG_W - EDGE : MSG_W, :] = whole_mask[1].astype(F32)
+
+
+def strips_kernel(f, de, dn, st, mask, w, east, west):
     fields = [f[...], de[...], dn[...], st[...], mask[...].astype(F32)]
-    fields += [w[n] for n in range(COSTS)]
-    east = jnp.zeros((ROWS, LANES), F32)
-    west = jnp.zeros((ROWS, LANES), F32)
-    at = 0
-    for k, field in enumerate(fields):
-        wide = DEEP if k < FIELDS else SLIM
-        here = (lane >= at) & (lane < at + wide)
-        east = jnp.where(here, turn(field[:, LANES:], at - (LANES - wide)), east)
-        west = jnp.where(here, turn(field[:, :LANES], at), west)
-        at += wide
-    to_east[...] = east
-    to_west[...] = west
-
-
-def bands_kernel(*refs):
-    ins, (to_north, to_south) = refs[:-2], refs[-2:]
-    for out, (f, de, dn, st, mask, w, sw, se) in ((to_north, ins[:8]), (to_south, ins[8:])):
-        for k, field in enumerate((f, de, dn, st, mask)):
-            out[EDGE * k : EDGE * (k + 1), :] = field[...].astype(F32)
-        for n in range(COSTS):
-            out[MSG_W + 8 * n : MSG_W + 8 * (n + 1), :] = w[n]
-        out[MSG_C:, :LANES] = sw[...]
-        out[MSG_C:, LANES:] = se[...]
+    right = [(v[:, LANES:], LANES - DEEP, DEEP) for v in fields]
+    left = [(v[:, :LANES], 0, DEEP) for v in fields]
+    right += [(w[n, :, LANES:], LANES - SLIM, SLIM) for n in range(COSTS)]
+    left += [(w[n, :, :LANES], 0, SLIM) for n in range(COSTS)]
+    east[...] = pack(ROWS, right)
+    west[...] = pack(ROWS, left)
+
+
+def corners_kernel(east, west, bs, bn, to_east, to_west):
+    for own, out, lanes, first in ((east, to_east, slice(LANES, COLS), True), (west, to_west, slice(0, LANES), False)):
+        out[EDGE : EDGE + ROWS, :] = own[...]
+        for band, low, slim in ((bs, 0, 1), (bn, EDGE + ROWS, 0)):
+            for half in range(2):
+                tiles = []
+                for k in range(FIELDS):
+                    at = EDGE * k + 8 * half
+                    tiles.append((band[at : at + 8, lanes], LANES - DEEP if first else 0, DEEP))
+                for n in range(COSTS):
+                    at = MSG_W + 8 * n
+                    tile = band[at : at + 8, lanes] if half == slim else None
+                    tiles.append((tile, LANES - SLIM if first else 0, SLIM))
+                out[low + 8 * half : low + 8 * half + 8, :] = pack(8, tiles)
 
 
 def side_tile(pw, pe, at, wide):
@@ -93,11 +124,7 @@
             src, off = ln, 8 * rb - 80
         else:
             src, off = None, 8 * rb - 16
-        if src is None:
-            pw, pe = sw[off : off + 8, :], se[off : off + 8, :]
-        else:
-            pw = src[MSG_C + off : MSG_C + off + 8, :LANES]
-            pe = src[MSG_C + off : MSG_C + off + 8, LANES:]
+        pw, pe = sw[8 * rb : 8 * rb + 8, :], se[8 * rb : 8 * rb + 8, :]
         for k in range(FIELDS):
             if src is None:
                 body = own[k][off : off + 8, :].astype(F32)
@@ -390,33 +417,39 @@
     args = (forcing, depth_east, depth_north, surface_term, ocean_mask, cost_weights)
     lats = lax.axis_size("lat")
     devices = lats * lax.axis_size("lon")
-    to_east, to_west = pl.pallas_call(
+    small = pltpu.CompilerParams(vmem_limit_bytes=4 << 20)
+    to_north, to_south = pl.pallas_call(
+        bands_kernel,
+        in_specs=[pl.BlockSpec(memory_space=pltpu.HBM)] * 6,
+        out_specs=[whole()] * 2,
+        out_shape=(struct(MSG, COLS),) * 2,
+        scratch_shapes=[
+            pltpu.VMEM((2, EDGE, COLS), jnp.int32),
+            pltpu.SemaphoreType.DMA((2 * (FIELDS + COSTS),)),
+        ],
+        compiler_params=small,
+        name="bands",
+    )(*[pltpu.with_memory_space_constraint(arg, pltpu.HBM) for arg in args])
+    band_s = lax.ppermute(to_north, "lat", ring("lat", 1))
+    band_n = lax.ppermute(to_south, "lat", ring("lat", -1))
+    east, west = pl.pallas_call(
         strips_kernel,
-        out_shape=(struct(ROWS, LANES), struct(ROWS, LANES)),
-        compiler_params=pltpu.CompilerParams(vmem_limit_bytes=4 << 20),
+        in_specs=[whole()] * 6,
+        out_specs=[whole()] * 2,
+        out_shape=(struct(ROWS, LANES),) * 2,
+        compiler_params=small,
         name="strips",
     )(*args)
+    to_east, to_west = pl.pallas_call(
+        corners_kernel,
+        in_specs=[whole()] * 4,
+        out_specs=[whole()] * 2,
+        out_shape=(struct(TALL, LANES),) * 2,
+        compiler_params=small,
+        name="corners",
+    )(east, west, band_s, band_n)
     side_w = lax.ppermute(to_east, "lon", ring("lon", 1))
     side_e = lax.ppermute(to_west, "lon", ring("lon", -1))
-
-    def band_specs(top):
-        field = pl.BlockSpec((EDGE, COLS), lambda i: (ROWS // EDGE - 1 if top else 0, 0))
-        strip = pl.BlockSpec((EDGE, LANES), lambda i: (ROWS // EDGE - 1 if top else 0, 0))
-        weights = pl.BlockSpec((COSTS, 8, COLS), lambda i: (0, ROWS // 8 - 1 if top else 0, 0))
-        return [field] * 5 + [weights, strip, strip]
-
-    sources = (*args, side_w, side_e)
-    to_north, to_south = pl.pallas_call(
-        bands_kernel,
-        grid=(1,),
-        in_specs=band_specs(True) + band_specs(False),
-        out_specs=[pl.BlockSpec((MSG, COLS), lambda i: (0, 0))] * 2,
-        out_shape=(struct(MSG, COLS), struct(MSG, COLS)),
-        compiler_params=pltpu.CompilerParams(vmem_limit_bytes=4 << 20),
-        name="bands",
-    )(*sources, *sources)
-    band_s = lax.ppermute(to_north, "lat", ring("lat", 1))
-    band_n = lax.ppermute(to_south, "lat", ring("lat", -1))
     row = lax.axis_index("lat")
     flags = jnp.stack([row > 0, row < lats - 1]).astype(jnp.int32)
     vecs, coefs, wside, wet, dots = pl.pallas_call(

time: 59.9 us -> 54.7 us (0.913)
  local copies, waits for them, and re-layouts: 5.26 us -> 0.03 us
  blocking collectives: 29.1 us -> 27.4 us
  starting transfers between devices: 7.04 us -> 8.43 us
  Pallas kernels: 11.6 us -> 12.3 us
    unnamed x24 -> x12, local copies, waits for them, and re-layouts: 5.26 us -> 0.03 us
    all_to_all x1, blocking collectives: 29.1 us -> 27.4 us  [body(): all_dots = lax.all_to_all(dots, ('lat', 'lon'), 0, 0, tiled=True)]
    pallas_call x2 -> x3, Pallas kernels: 0.3 us -> 1.55 us  [the longest x1 1.14 us: body(): pl.pallas_call(bands_kernel, in_specs=[pl.BlockSpec(memory_space=pltpu.HB...]
    ppermute x1, starting transfers between devices: 3.09 us -> 3.95 us  [body(): side_w = lax.ppermute(to_east, 'lon', ring('lon', 1))]
    ppermute x1, starting transfers between devices: 1.29 us -> 2.11 us  [body(): band_s = lax.ppermute(to_north, 'lat', ring('lat', 1))]
  transfers between devices with their start and end apart: 4 -> 4, of which waited for: 3 -> 3; matrix products, arithmetic and copies ran while one was open for 0% -> 0% of each run, Pallas kernels for 0% -> 1%
where the time goes in v3:
time: 54.7 us; the launch traced here: 54.6 us
  blocking collectives  27.4 us (50%)
  Pallas kernels  12.3 us (22%)
  starting transfers between devices  8.43 us (15%)
  waiting for transfers between devices  5.56 us (10%)
  between operations  0.74 us (1%)
    all_to_all x1, blocking collectives, body(): all_dots = lax.all_to_all(dots, ('lat', 'lon'), 0, 0, tiled=True)  27.4 us
    pallas_call x1, Pallas kernels, body(): pl.pallas_call(adjoint_kernel, grid=(COSTS,), in_specs=[pl.BlockSpec((dev...  8.53 us
    ppermute x1, starting transfers between devices, body(): side_w = lax.ppermute(to_east, 'lon', ring('lon', 1))  3.95 us
    ppermute x1, starting transfers between devices, body(): band_n = lax.ppermute(to_south, 'lat', ring('lat', -1))  2.37 us
    ppermute x1, waiting for transfers between devices, body(): side_e = lax.ppermute(to_west, 'lon', ring('lon', -1))  2.34 us
    pallas_call x1, Pallas kernels, body(): pl.pallas_call(forward_kernel, in_specs=[pl.BlockSpec(memory_space=pltpu....  2.26 us
    ppermute x1, waiting for transfers between devices, body(): band_s = lax.ppermute(to_north, 'lat', ring('lat', 1))  2.12 us
    ppermute x1, starting transfers between devices, body(): band_s = lax.ppermute(to_north, 'lat', ring('lat', 1))  2.11 us
  transfers between devices with their start and end apart: 4, of which 3 were waited for; matrix products, arithmetic and copies ran while one was open for 0% of the time, Pallas kernels for 1%

profile of v3, /device:TPU:1, one launch (start us, length us, event | category | flops | bytes accessed | tf_op | source)
XLA Modules:
  0.0 54.6 jit_solution(17532160513369751281)
XLA Ops:
  0.6 0.0 copy-start
  0.6 0.0 copy-start.5
  0.7 0.0 copy-start.4
  0.7 0.0 copy-start.3
  0.7 0.0 copy-start.2
  0.7 0.0 copy-start.1
  0.7 1.1 %bands.1 = (f32[144,256]{1,0:T(8,128)S(1)}, f32[144,256]{1,0:T(8,128)S(1)}) custom-call(f32[64,256]{1,0:T(8,128)} %f.5, f32[64,256]{1,0:T(8,128)} %de.5, f32[64,256]{1,0:T(8,128)} %dn.5, f32[64,256]{1,0:T(8,128)} %st.5, s32[64,256]{1,0:T(8,128)} %mask.5, f32[8,64,256]{2,1,0:T(8,128)} %w.7), custom_call_target="tpu_custom_call" | custom-call | tf_op jit(solution)/shard_map/bands/pallas_call | solution.py:421
  1.8 2.1 %collective-permute-start = (f32[144,256]{1,0:T(8,128)S(1)}, f32[144,256]{1,0:T(8,128)S(1)}, u32[]{:S(2)}, u32[]{:S(2)}) collective-permute-start(f32[144,256]{1,0:T(8,128)S(1)} %get-tuple-element.14), channel_id=1, source_target_pairs={{0,32},{32,64},{64,96},{96,128},{128,160},{160,192},{192,224},{224... | collective-permute-start | bytes 442376 | tf_op jit(solution)/shard_map/ppermute | solution.py:433
  3.9 2.4 %collective-permute-start.1 = (f32[144,256]{1,0:T(8,128)S(1)}, f32[144,256]{1,0:T(8,128)S(1)}, u32[]{:S(2)}, u32[]{:S(2)}) collective-permute-start(f32[144,256]{1,0:T(8,128)S(1)} %get-tuple-element.15), channel_id=1, source_target_pairs={{0,224},{32,0},{64,32},{96,64},{128,96},{160,128},{192,160},{224,1... | collective-permute-start | bytes 442376 | tf_op jit(solution)/shard_map/ppermute | solution.py:434
  6.3 0.0 copy-done
  6.3 0.0 copy-done.5
  6.3 0.0 copy-done.4
  6.3 0.0 copy-done.3
  6.3 0.0 copy-done.2
  6.3 0.0 copy-done.1
  6.3 0.3 strips.1
  6.6 2.1 %collective-permute-done.bs.ls.ws = f32[144,256]{1,0:T(8,128)S(1)} collective-permute-done((f32[144,256]{1,0:T(8,128)S(1)}, f32[144,256]{1,0:T(8,128)S(1)}, u32[]{:S(2)}, u32[]{:S(2)}) %collective-permute-start) | collective-permute-done | bytes 147488 | tf_op jit(solution)/shard_map/ppermute | solution.py:433
  8.8 0.0 collective-permute-done.1.bn.ln.wn
  8.8 0.1 corners.1
  8.9 3.9 %collective-permute-start.2 = (f32[96,128]{1,0:T(8,128)S(1)}, f32[96,128]{1,0:T(8,128)S(1)}, u32[]{:S(2)}, u32[]{:S(2)}) collective-permute-start(f32[96,128]{1,0:T(8,128)S(1)} %get-tuple-element.18), channel_id=1, source_target_pairs={{0,1},{1,2},{2,3},{3,4},{4,5},{5,6},{6,7},{7,8},{8,9},{9,10},{10,1... | collective-permute-start | bytes 147464 | tf_op jit(solution)/shard_map/ppermute | solution.py:451
  12.9 0.0 collective-permute-start.3
  12.9 0.1 add_convert_fusion.flags
  12.9 1.1 %collective-permute-done.2.sw = f32[96,128]{1,0:T(8,128)S(1)} collective-permute-done((f32[96,128]{1,0:T(8,128)S(1)}, f32[96,128]{1,0:T(8,128)S(1)}, u32[]{:S(2)}, u32[]{:S(2)}) %collective-permute-start.2) | collective-permute-done | bytes 49184 | tf_op jit(solution)/shard_map/ppermute | solution.py:451
  14.0 2.3 %collective-permute-done.3.se = f32[96,128]{1,0:T(8,128)S(1)} collective-permute-done((f32[96,128]{1,0:T(8,128)S(1)}, f32[96,128]{1,0:T(8,128)S(1)}, u32[]{:S(2)}, u32[]{:S(2)}) %collective-permute-start.3) | collective-permute-done | bytes 49184 | tf_op jit(solution)/shard_map/ppermute | solution.py:452
  16.4 2.3 %forward.1 = (f32[6,80,384]{2,1,0:T(8,128)S(1)}, f32[7,80,384]{2,1,0:T(8,128)S(1)}, f32[8,80,128]{2,1,0:T(8,128)S(1)}, f32[2,64,256]{2,1,0:T(8,128)S(1)}, f32[256,128]{1,0:T(8,128)S(1)}) custom-call(s32[2]{0:T(128)S(1)} %add_convert_fusion.flags, f32[64,256]{1,0:T(8,128)S(1)} %copy-done.1, f32[64,256]{1,0:T(8,128)S(1)} %copy-done.2, ...), custom_call_target="tpu_custom_call" | custom-call | tf_op jit(solution)/shard_map/forward/pallas_call | solution.py:455
  18.6 27.4 %all_to_all.11 = f32[256,1,128]{2,1,0:T(1,128)S(1)} all-to-all(f32[256,1,128]{2,1,0:T(1,128)S(1)} %bitcast.7), channel_id=1, replica_groups=mesh['lat'=8,'lon'=32] {'lat','lon'}, dimensions={0} | all-to-all | bytes 262144 | tf_op jit(solution)/shard_map/all_to_all | solution.py:472
  46.0 8.5 %adjoint.1 = (f32[8,64,256]{2,1,0:T(8,128)}, f32[8,64,256]{2,1,0:T(8,128)}, f32[8,64,256]{2,1,0:T(8,128)}) custom-call(f32[256,128]{1,0:T(8,128)S(1)} %bitcast.6, f32[6,80,384]{2,1,0:T(8,128)S(1)} %get-tuple-element.21.vecs, f32[7,80,384]{2,1,0:T(8,128)S(1)} %get-tuple-element.22.coefs, f32[2,64,256]{2,1,0:T(8,128)S(1)} %get-tuple-element.23.mask, ...), custom_call_target="tpu_custom_call" | custom-call | tf_op jit(solution)/shard_map/adjoint/pallas_call | solution.py:475
Async XLA Ops:
  0.6 5.7 %copy-start = (f32[8,64,256]{2,1,0:T(8,128)S(1)}, f32[8,64,256]{2,1,0:T(8,128)}, u32[]{:S(2)}) copy-start(f32[8,64,256]{2,1,0:T(8,128)} %w.7) | copy-start | bytes 1572868
  0.6 5.7 %copy-start.5 = (s32[64,256]{1,0:T(8,128)S(1)}, s32[64,256]{1,0:T(8,128)}, u32[]{:S(2)}) copy-start(s32[64,256]{1,0:T(8,128)} %mask.5) | copy-start | bytes 196612
  0.7 5.7 %copy-start.4 = (f32[64,256]{1,0:T(8,128)S(1)}, f32[64,256]{1,0:T(8,128)}, u32[]{:S(2)}) copy-start(f32[64,256]{1,0:T(8,128)} %st.5) | copy-start | bytes 196612
  0.7 5.7 %copy-start.3 = (f32[64,256]{1,0:T(8,128)S(1)}, f32[64,256]{1,0:T(8,128)}, u32[]{:S(2)}) copy-start(f32[64,256]{1,0:T(8,128)} %dn.5) | copy-start | bytes 196612
  0.7 5.7 %copy-start.2 = (f32[64,256]{1,0:T(8,128)S(1)}, f32[64,256]{1,0:T(8,128)}, u32[]{:S(2)}) copy-start(f32[64,256]{1,0:T(8,128)} %de.5) | copy-start | bytes 196612
  0.7 5.7 %copy-start.1 = (f32[64,256]{1,0:T(8,128)S(1)}, f32[64,256]{1,0:T(8,128)}, u32[]{:S(2)}) copy-start(f32[64,256]{1,0:T(8,128)} %f.5) | copy-start | bytes 196612
  1.8 6.9 %collective-permute-start = (f32[144,256]{1,0:T(8,128)S(1)}, f32[144,256]{1,0:T(8,128)S(1)}, u32[]{:S(2)}, u32[]{:S(2)}) collective-permute-start(f32[144,256]{1,0:T(8,128)S(1)} %get-tuple-element.14), channel_id=1, source_target_pairs={{0,32},{32,64},{64,96},{96,128},{128,160},{160,192},{192,224},{224... | collective-permute-start | bytes 442376 | tf_op jit(solution)/shard_map/ppermute | solution.py:433
  3.9 4.8 %collective-permute-start.1 = (f32[144,256]{1,0:T(8,128)S(1)}, f32[144,256]{1,0:T(8,128)S(1)}, u32[]{:S(2)}, u32[]{:S(2)}) collective-permute-start(f32[144,256]{1,0:T(8,128)S(1)} %get-tuple-element.15), channel_id=1, source_target_pairs={{0,224},{32,0},{64,32},{96,64},{128,96},{160,128},{192,160},{224,1... | collective-permute-start | bytes 442376 | tf_op jit(solution)/shard_map/ppermute | solution.py:434
  8.9 5.1 %collective-permute-start.2 = (f32[96,128]{1,0:T(8,128)S(1)}, f32[96,128]{1,0:T(8,128)S(1)}, u32[]{:S(2)}, u32[]{:S(2)}) collective-permute-start(f32[96,128]{1,0:T(8,128)S(1)} %get-tuple-element.18), channel_id=1, source_target_pairs={{0,1},{1,2},{2,3},{3,4},{4,5},{5,6},{6,7},{7,8},{8,9},{9,10},{10,1... | collective-permute-start | bytes 147464 | tf_op jit(solution)/shard_map/ppermute | solution.py:451
  12.9 3.5 %collective-permute-start.3 = (f32[96,128]{1,0:T(8,128)S(1)}, f32[96,128]{1,0:T(8,128)S(1)}, u32[]{:S(2)}, u32[]{:S(2)}) collective-permute-start(f32[96,128]{1,0:T(8,128)S(1)} %get-tuple-element.19), channel_id=1, source_target_pairs={{0,31},{1,0},{2,1},{3,2},{4,3},{5,4},{6,5},{7,6},{8,7},{9,8},{10,9... | collective-permute-start | bytes 147464 | tf_op jit(solution)/shard_map/ppermute | solution.py:452

commit v4 on v3

v4 whole, which is shorter than its diff:
```python
import functools

import jax
import jax.numpy as jnp
from jax import lax
from jax.experimental import pallas as pl
from jax.experimental.pallas import tpu as pltpu
from jax.sharding import PartitionSpec as P

ITERS = 6
COSTS = 8
ROWS = 64
COLS = 256
LANES = 128
TILES = 3
DEEP = 13
SLIM = 6
EDGE = 16
FIELDS = 5
FRAME = 80
TALL = 96
MSG_W = FIELDS * EDGE
MSG = MSG_W + COSTS * 8
N_LAM = COSTS * ITERS
N_RHS = N_LAM
N_MAT = N_LAM + ITERS
F32 = jnp.float32
HIGH = lax.Precision.HIGHEST


def lane_index(rows):
    return lax.broadcasted_iota(jnp.int32, (rows, LANES), 1)


def turn(value, amount):
    return pltpu.roll(value, amount % value.shape[1], 1)


def pack(rows, tiles):
    lane = lane_index(rows)
    out = jnp.zeros((rows, LANES), F32)
    at = 0
    for tile, first, wide in tiles:
        if tile is not None:
            here = (lane >= at) & (lane < at + wide)
            out = jnp.where(here, turn(tile, at - first), out)
        at += wide
    return out


def bands_kernel(f, de, dn, st, mask, w, to_north, to_south, whole_mask, sems):
    copies = []
    for side, out in enumerate((to_north, to_south)):
        low = ROWS - EDGE if side == 0 else 0
        rows = pl.ds(low, EDGE)
        for k, field in enumerate((f, de, dn, st)):
            copies.append((field.at[rows, :], out.at[pl.ds(EDGE * k, EDGE), :]))
        copies.append((mask.at[rows, :], whole_mask.at[side]))
        low = ROWS - 8 if side == 0 else 0
        for n in range(COSTS):
            copies.append((w.at[n, pl.ds(low, 8), :], out.at[pl.ds(MSG_W + 8 * n, 8), :]))
    copies = [
        pltpu.make_async_copy(src, dst, sems.at[i]) for i, (src, dst) in enumerate(copies)
    ]
    for copy in copies:
        copy.start()
    for copy in copies:
        copy.wait()
    to_north[MSG_W - EDGE : MSG_W, :] = whole_mask[0].astype(F32)
    to_south[MSG_W - EDGE : MSG_W, :] = whole_mask[1].astype(F32)


def strips_kernel(f, de, dn, st, mask, w, east, west):
    fields = [f[...], de[...], dn[...], st[...], mask[...].astype(F32)]
    right = [(v[:, LANES:], LANES - DEEP, DEEP) for v in fields]
    left = [(v[:, :LANES], 0, DEEP) for v in fields]
    right += [(w[n, :, LANES:], LANES - SLIM, SLIM) for n in range(COSTS)]
    left += [(w[n, :, :LANES], 0, SLIM) for n in range(COSTS)]
    east[...] = pack(ROWS, right)
    west[...] = pack(ROWS, left)


def corners_kernel(east, west, bs, bn, to_east, to_west):
    for own, out, lanes, first in ((east, to_east, slice(LANES, COLS), True), (west, to_west, slice(0, LANES), False)):
        out[EDGE : EDGE + ROWS, :] = own[...]
        for band, low, slim in ((bs, 0, 1), (bn, EDGE + ROWS, 0)):
            for half in range(2):
                tiles = []
                for k in range(FIELDS):
                    at = EDGE * k + 8 * half
                    tiles.append((band[at : at + 8, lanes], LANES - DEEP if first else 0, DEEP))
                for n in range(COSTS):
                    at = MSG_W + 8 * n
                    tile = band[at : at + 8, lanes] if half == slim else None
                    tiles.append((tile, LANES - SLIM if first else 0, SLIM))
                out[low + 8 * half : low + 8 * half + 8, :] = pack(8, tiles)


def side_tile(pw, pe, at, wide):
    lane = lane_index(pw.shape[0])
    west = jnp.where(lane >= LANES - wide, turn(pw, LANES - wide - at), 0.0)
    return jnp.where(lane < wide, turn(pe, -at), west)


def east_of(tiles):
    last = lane_index(8) == LANES - 1
    turned = [pltpu.roll(tile, LANES - 1, 1) for tile in tiles]
    return [jnp.where(last, turned[(t + 1) % TILES], turned[t]) for t in range(TILES)]


def west_of(tiles):
    first = lane_index(8) == 0
    turned = [pltpu.roll(tile, 1, 1) for tile in tiles]
    return [jnp.where(first, turned[t - 1], turned[t]) for t in range(TILES)]


def forward_kernel(
    flags, f, de, dn, st, mask, w, ls, ln, sw, se,
    vecs, links, inv2, wside, wet, dots,
    raw, north, vec, link, diag, part,
):
    own = (f, de, dn, st, mask)
    blocks = range(TALL // 8)
    tiles = range(TILES)
    for rb in blocks:
        at = 8 + 8 * rb
        src, off = None, 8 * rb - EDGE
        if rb < 2:
            src, off = ls, 8 * rb
        elif rb >= 10:
            src, off = ln, 8 * rb - 80
        pw, pe = sw[8 * rb : 8 * rb + 8, :], se[8 * rb : 8 * rb + 8, :]
        for k in range(FIELDS):
            values = []
            for t in range(2):
                lanes = slice(LANES * t, LANES * (t + 1))
                if src is None:
                    values.append(own[k][off : off + 8, lanes].astype(F32))
                else:
                    values.append(src[EDGE * k + off : EDGE * k + off + 8, lanes])
            values.append(side_tile(pw, pe, DEEP * k, DEEP))
            if k == FIELDS - 1 and src is not None:
                inside = flags[0 if rb < 2 else 1] > 0
                values = [jnp.where(inside, value, 0.0) for value in values]
            for t in tiles:
                raw[k, t, at : at + 8, :] = values[t]
        if 1 <= rb < 11:
            for n in range(COSTS):
                wside[n, 8 * rb - 8 : 8 * rb, :] = side_tile(
                    pw, pe, FIELDS * DEEP + SLIM * n, SLIM
                )
    for rb in blocks:
        here = slice(8 + 8 * rb, 16 + 8 * rb)
        above = slice(9 + 8 * rb, 17 + 8 * rb)
        for t in tiles:
            mn = raw[4, t, here, :] * raw[4, t, above, :]
            north[t, here, :] = raw[2, t, here, :] * mn
            if 2 <= rb < 10 and t < 2:
                wet[1, 8 * rb - 16 : 8 * rb - 8, LANES * t : LANES * (t + 1)] = mn
    for rb in blocks:
        here = slice(8 + 8 * rb, 16 + 8 * rb)
        below = slice(7 + 8 * rb, 15 + 8 * rb)
        m = [raw[4, t, here, :] for t in tiles]
        me = [a * b for a, b in zip(m, east_of(m))]
        ex = [raw[1, t, here, :] * me[t] for t in tiles]
        exw = west_of(ex)
        for t in tiles:
            ey, eys = north[t, here, :], north[t, below, :]
            total = m[t] * raw[3, t, here, :] + 1.0 - m[t] + ex[t] + exw[t] + ey + eys
            inv = 1.0 / total
            twice = inv + inv
            v0 = raw[0, t, here, :] * inv
            vec[0, t, here, :] = v0
            values = [twice * face for face in (ex[t], exw[t], ey, eys)]
            for k in range(4):
                link[k, t, here, :] = values[k]
            if 1 <= rb < 11:
                to = slice(8 * rb - 8, 8 * rb)
                vecs[0, t, to, :] = v0
                inv2[t, to, :] = twice
                for k in range(4):
                    links[k, t, to, :] = values[k]
            if 2 <= rb < 10 and t < 2:
                to, lanes = slice(8 * rb - 16, 8 * rb - 8), slice(LANES * t, LANES * (t + 1))
                wet[0, to, lanes] = me[t]
                diag[to, lanes] = total
    for j in range(ITERS):
        for rb in blocks:
            here = slice(8 + 8 * rb, 16 + 8 * rb)
            above = slice(9 + 8 * rb, 17 + 8 * rb)
            below = slice(7 + 8 * rb, 15 + 8 * rb)
            v = [vec[j, t, here, :] for t in tiles]
            ve, vw = east_of(v), west_of(v)
            for t in tiles:
                new = (
                    link[0, t, here, :] * ve[t]
                    + link[1, t, here, :] * vw[t]
                    + link[2, t, here, :] * vec[j, t, above, :]
                    + link[3, t, here, :] * vec[j, t, below, :]
                )
                new = 0.5 * new if j == 0 else new - vec[j - 1, t, here, :]
                vec[j + 1, t, here, :] = new
                if 1 <= rb < 11:
                    vecs[j + 1, t, 8 * rb - 8 : 8 * rb, :] = new
    count = ITERS + ITERS * (ITERS + 1) // 2
    own_tiles = [(rb, t) for rb in range(ROWS // 8) for t in range(2)]
    sums = [None] * count
    for rb, t in own_tiles:
        here, lanes = slice(8 * rb, 8 * rb + 8), slice(LANES * t, LANES * (t + 1))
        vs = [vec[j, t, 24 + 8 * rb : 32 + 8 * rb, :] for j in range(ITERS + 1)]
        total = diag[here, lanes]
        forcing = f[here, lanes]
        terms = [forcing * vs[j] for j in range(ITERS)]
        for j in range(ITERS):
            turned = vs[1] if j == 0 else 0.5 * (vs[j + 1] + vs[j - 1])
            image = total * (vs[j] - turned)
            terms += [image * vs[i] for i in range(j + 1)]
        sums = [b if a is None else a + b for a, b in zip(sums, terms)]
    part[N_RHS + count :, :] = jnp.zeros((LANES - N_RHS - count, LANES), F32)
    for k in range(count):
        part[N_RHS + k : N_RHS + k + 1, :] = jnp.sum(sums[k], axis=0, keepdims=True)
    for n in range(COSTS):
        sums = [None] * ITERS
        for rb, t in own_tiles:
            weight = w[n, 8 * rb : 8 * rb + 8, LANES * t : LANES * (t + 1)]
            for j in range(ITERS):
                term = weight * vec[j, t, 24 + 8 * rb : 32 + 8 * rb, :]
                sums[j] = term if sums[j] is None else sums[j] + term
        for j in range(ITERS):
            k = COSTS * j + n
            part[k : k + 1, :] = jnp.sum(sums[j], axis=0, keepdims=True)
    row = lax.dot_general(
        jnp.ones((8, LANES), F32), part[...], (((1,), (1,)), ((), ())),
        precision=HIGH, preferred_element_type=F32,
    )
    for at in range(0, dots.shape[0], 8):
        dots[at : at + 8, :] = row


def small_solve(total):
    wide = lambda k: jnp.broadcast_to(total[k : k + 1, :], (8, LANES))
    mat = {}
    k = N_MAT
    for j in range(ITERS):
        for i in range(j + 1):
            mat[j, i] = wide(k)
            k += 1
    low, inv = {}, []
    for j in range(ITERS):
        pivot = mat[j, j]
        for k in range(j):
            pivot = pivot - low[j, k] * mat[j, k]
        inv.append(1.0 / pivot)
        for i in range(j + 1, ITERS):
            entry = mat[i, j]
            for k in range(j):
                entry = entry - low[j, k] * mat[i, k]
            mat[i, j] = entry
            low[i, j] = entry * inv[j]

    def solve(rhs):
        y = []
        for i in range(ITERS):
            t = rhs[i]
            for k in range(i):
                t = t - low[i, k] * y[k]
            y.append(t)
        out = [None] * ITERS
        for i in range(ITERS - 1, -1, -1):
            t = y[i] * inv[i]
            for k in range(i + 1, ITERS):
                t = t - low[k, i] * out[k]
            out[i] = t
        return out

    return (
        solve([wide(N_RHS + i) for i in range(ITERS)]),
        solve([total[COSTS * j : COSTS * (j + 1), :] for j in range(ITERS)]),
    )


def imaged(coef):
    get = lambda k: coef[k] if 0 <= k < ITERS else None
    out = []
    for k in range(ITERS + 1):
        low, mid, high = get(k - 1), get(k), get(k + 1)
        value = jnp.zeros_like(coef[0]) if mid is None else mid + mid
        if low is not None:
            value = value - (low + low if k == 1 else low)
        if high is not None:
            value = value - high
        out.append(value)
    return out


def mixed(factors, values):
    total = None
    for factor, value in zip(factors, values):
        term = factor * value
        total = term if total is None else total + term
    return total


def adjoint_kernel(
    all_dots, vecs, links, inv2, wet, w, wside, ws, wn,
    adj, east, north,
    lam, lam2, cs, slope, lag, rs, ys, ss, ps, acc,
):
    n = pl.program_id(0)
    blocks = range(FRAME // 8)
    tiles = range(TILES)
    lanes_of = lambda t: slice(LANES * t, LANES * (t + 1))

    @pl.when(n == 0)
    def _():
        rows = [all_dots[at : at + 8, :] for at in range(0, all_dots.shape[0], 8)]
        while len(rows) > 1:
            rows = [a + b for a, b in zip(rows[::2], rows[1::2])]
        total = lax.dot_general(
            rows[0], jnp.ones((8, LANES), F32), (((0,), (0,)), ((), ())),
            precision=HIGH, preferred_element_type=F32,
        )
        c, weights = small_solve(total)
        for j in range(ITERS):
            lam[8 * j : 8 * j + 8, :] = weights[j]
            cs[8 * j : 8 * j + 8, :] = c[j]
        for k, value in enumerate(imaged(weights)):
            lam2[8 * k : 8 * k + 8, :] = value
        c2 = imaged(c)
        for rb in blocks:
            here = slice(8 * rb, 8 * rb + 8)
            for t in tiles:
                v = [vecs[k, t, here, :] for k in range(ITERS + 1)]
                rs[t, here, :] = v[0] + v[0] - mixed(c2, v)
                if rb >= 1:
                    lag[0, t, here, :] = v[1] - v[0]
                    for j in range(1, ITERS - 1):
                        lag[j, t, here, :] = 0.5 * (v[j + 1] + v[j - 1]) - v[j]
        for rb in range(1, 9):
            here = slice(8 * rb, 8 * rb + 8)
            above = slice(8 * rb + 1, 8 * rb + 9)
            to = slice(8 * rb - 8, 8 * rb)
            sums = [[None, None], [None, None]]
            for j in range(ITERS):
                v = [vecs[j, t, here, :] for t in tiles]
                ve = east_of(v)
                for t in range(2):
                    for d, near in enumerate((ve[t], vecs[j, t, above, :])):
                        step = v[t] - near
                        if j < ITERS - 1:
                            slope[d, j, t, to, :] = step
                        term = c[j] * step
                        sums[d][t] = term if j == 0 else sums[d][t] + term
            for d in range(2):
                for t in range(2):
                    slope[d, ITERS - 1, t, to, :] = sums[d][t]

    spread = lambda ref, k: jnp.broadcast_to(ref[pl.ds(8 * k + n, 1), :], (8, LANES))
    rows = [spread(lam, j) for j in range(ITERS)]
    rows2 = [spread(lam2, k) for k in range(ITERS + 1)]
    last = ITERS - 1
    c_last = cs[8 * last : 8 * last + 8, :]
    for rb in blocks:
        at = 8 + 8 * rb
        here = slice(8 * rb, 8 * rb + 8)
        for t in tiles:
            v = [vecs[k, t, here, :] for k in range(ITERS + 1)]
            if t == 2:
                weight = wside[0, here, :]
            elif rb == 0:
                weight = ws[:, lanes_of(t)]
            elif rb == 9:
                weight = wn[:, lanes_of(t)]
            else:
                weight = w[0, 8 * rb - 8 : 8 * rb, lanes_of(t)]
            s = inv2[t, here, :] * weight - mixed(rows2, v)
            ss[t, here, :] = s
            ps[last - 1, t, at : at + 8, :] = c_last * s + rows[last] * rs[t, here, :]
            if rb >= 1:
                ys[t, here, :] = mixed(rows, v)
    for rb in range(1, 9):
        here = slice(8 * rb, 8 * rb + 8)
        above = slice(8 * rb + 1, 8 * rb + 9)
        to = slice(8 * rb - 8, 8 * rb)
        y = [ys[t, here, :] for t in tiles]
        ye = east_of(y)
        for t in range(2):
            acc[0, t, to, :] = (y[t] - ye[t]) * slope[0, last, t, to, :]
            acc[1, t, to, :] = (y[t] - ys[t, above, :]) * slope[1, last, t, to, :]
    lagged = lambda rb: slice(8 * rb - 8, 8 * rb)
    for j in range(ITERS - 2, -1, -1):
        c_j = cs[8 * j : 8 * j + 8, :]
        for rb in blocks:
            if j == 0 and rb == 0:
                continue
            at = 8 + 8 * rb
            here = slice(8 * rb, 8 * rb + 8)
            p = [ps[j, t, at : at + 8, :] for t in tiles]
            pe, pw = east_of(p), west_of(p)
            for t in tiles:
                pn = ps[j, t, at + 1 : at + 9, :]
                bar = (
                    links[0, t, here, :] * pe[t]
                    + links[1, t, here, :] * pw[t]
                    + links[2, t, here, :] * pn
                    + links[3, t, here, :] * ps[j, t, at - 1 : at + 7, :]
                ) + (c_j * ss[t, here, :] + rows[j] * rs[t, here, :])
                if j < ITERS - 2:
                    bar = bar - ps[j + 1, t, at : at + 8, :]
                if j == 1:
                    bar = 0.5 * bar
                if j > 0:
                    ps[j - 1, t, at : at + 8, :] = bar
                if rb >= 1:
                    d = p[t] * lag[j, t, here, :]
                    if j < ITERS - 2:
                        d = acc[2, t, lagged(rb), :] + d
                    if j == 0:
                        g = 0.5 * bar
                        d = d + g * vecs[0, t, here, :]
                    acc[2, t, lagged(rb), :] = d
                if 1 <= rb < 9 and t < 2:
                    to = lagged(rb)
                    acc[0, t, to, :] = acc[0, t, to, :] + (p[t] - pe[t]) * slope[0, j, t, to, :]
                    acc[1, t, to, :] = acc[1, t, to, :] + (p[t] - pn) * slope[1, j, t, to, :]
                    if j == 0:
                        adj[0, to, lanes_of(t)] = ys[t, here, :] + g
    for rb in range(ROWS // 8):
        to = slice(8 * rb, 8 * rb + 8)
        d = [acc[2, t, to, :] for t in tiles]
        de = east_of(d)
        for t in range(2):
            above = acc[2, t, 8 * rb + 1 : 8 * rb + 9, :]
            east[0, to, lanes_of(t)] = -wet[0, to, lanes_of(t)] * (acc[0, t, to, :] + d[t] + de[t])
            north[0, to, lanes_of(t)] = -wet[1, to, lanes_of(t)] * (acc[1, t, to, :] + d[t] + above)


def ring(axis, steps):
    count = lax.axis_size(axis)
    return [(source, (source + steps) % count) for source in range(count)]


def struct(*shape):
    return jax.ShapeDtypeStruct(shape, F32)


def whole():
    return pl.BlockSpec(memory_space=pltpu.VMEM)


def body(forcing, depth_east, depth_north, surface_term, ocean_mask, cost_weights):
    args = (forcing, depth_east, depth_north, surface_term, ocean_mask, cost_weights)
    lats = lax.axis_size("lat")
    devices = lats * lax.axis_size("lon")
    small = pltpu.CompilerParams(vmem_limit_bytes=4 << 20)
    to_north, to_south = pl.pallas_call(
        bands_kernel,
        in_specs=[pl.BlockSpec(memory_space=pltpu.HBM)] * 6,
        out_specs=[whole()] * 2,
        out_shape=(struct(MSG, COLS),) * 2,
        scratch_shapes=[
            pltpu.VMEM((2, EDGE, COLS), jnp.int32),
            pltpu.SemaphoreType.DMA((2 * (FIELDS + COSTS),)),
        ],
        compiler_params=small,
        name="bands",
    )(*[pltpu.with_memory_space_constraint(arg, pltpu.HBM) for arg in args])
    band_s = lax.ppermute(to_north, "lat", ring("lat", 1))
    band_n = lax.ppermute(to_south, "lat", ring("lat", -1))
    east, west = pl.pallas_call(
        strips_kernel,
        in_specs=[whole()] * 6,
        out_specs=[whole()] * 2,
        out_shape=(struct(ROWS, LANES),) * 2,
        compiler_params=small,
        name="strips",
    )(*args)
    to_east, to_west = pl.pallas_call(
        corners_kernel,
        in_specs=[whole()] * 4,
        out_specs=[whole()] * 2,
        out_shape=(struct(TALL, LANES),) * 2,
        compiler_params=small,
        name="corners",
    )(east, west, band_s, band_n)
    side_w = lax.ppermute(to_east, "lon", ring("lon", 1))
    side_e = lax.ppermute(to_west, "lon", ring("lon", -1))
    row = lax.axis_index("lat")
    flags = jnp.stack([row > 0, row < lats - 1]).astype(jnp.int32)
    vecs, links, inv2, wside, wet, dots = pl.pallas_call(
        forward_kernel,
        in_specs=[pl.BlockSpec(memory_space=pltpu.SMEM)] + [whole()] * 10,
        out_specs=[whole()] * 6,
        out_shape=(
            struct(ITERS + 1, TILES, FRAME, LANES), struct(4, TILES, FRAME, LANES),
            struct(TILES, FRAME, LANES), struct(COSTS, FRAME, LANES),
            struct(2, ROWS, COLS), struct(devices, LANES),
        ),
        scratch_shapes=[
            pltpu.VMEM((FIELDS, TILES, TALL + 16, LANES), F32),
            pltpu.VMEM((TILES, TALL + 16, LANES), F32),
            pltpu.VMEM((ITERS + 1, TILES, TALL + 16, LANES), F32),
            pltpu.VMEM((4, TILES, TALL + 16, LANES), F32),
            pltpu.VMEM((ROWS, COLS), F32),
            pltpu.VMEM((LANES, LANES), F32),
        ],
        compiler_params=pltpu.CompilerParams(vmem_limit_bytes=14 << 20),
        name="forward",
    )(flags, *args, band_s, band_n, side_w, side_e)
    all_dots = lax.all_to_all(dots, ("lat", "lon"), 0, 0, tiled=True)
    out_spec = pl.BlockSpec((1, ROWS, COLS), lambda n: (n, 0, 0))
    full = lambda *shape: pl.BlockSpec(shape, lambda n: (0,) * len(shape))
    return pl.pallas_call(
        adjoint_kernel,
        grid=(COSTS,),
        in_specs=[
            full(devices, LANES),
            full(ITERS + 1, TILES, FRAME, LANES),
            full(4, TILES, FRAME, LANES),
            full(TILES, FRAME, LANES),
            full(2, ROWS, COLS),
            pl.BlockSpec((1, ROWS, COLS), lambda n: (n, 0, 0)),
            pl.BlockSpec((1, FRAME, LANES), lambda n: (n, 0, 0)),
            pl.BlockSpec((8, COLS), lambda n: (MSG_W // 8 + n, 0)),
            pl.BlockSpec((8, COLS), lambda n: (MSG_W // 8 + n, 0)),
        ],
        out_specs=[out_spec] * 3,
        out_shape=(struct(COSTS, ROWS, COLS),) * 3,
        scratch_shapes=[
            pltpu.VMEM((N_LAM, LANES), F32),
            pltpu.VMEM((N_LAM + 8, LANES), F32),
            pltpu.VMEM((8 * ITERS, LANES), F32),
            pltpu.VMEM((2, ITERS, 2, ROWS, LANES), F32),
            pltpu.VMEM((ITERS - 1, TILES, FRAME, LANES), F32),
            pltpu.VMEM((TILES, FRAME, LANES), F32),
            pltpu.VMEM((TILES, FRAME, LANES), F32),
            pltpu.VMEM((TILES, FRAME, LANES), F32),
            pltpu.VMEM((ITERS - 1, TILES, FRAME + 16, LANES), F32),
            pltpu.VMEM((3, TILES, FRAME - 8, LANES), F32),
        ],
        compiler_params=pltpu.CompilerParams(
            dimension_semantics=("arbitrary",), vmem_limit_bytes=18 << 20
        ),
        name="adjoint",
    )(all_dots, vecs, links, inv2, wet, cost_weights, wside, band_s, band_n)


def solution(mesh):
    return jax.shard_map(
        body,
        mesh=mesh,
        in_specs=(P("lat", "lon"),) * 5 + (P(None, "lat", "lon"),),
        out_specs=(P(None, "lat", "lon"),) * 3,
        check_vma=False,
    )
```

time: 54.7 us -> 54.6 us (level)
  no operation moved by 1% of the time
where the time goes in v4:
time: 54.6 us; the launch traced here: 54.4 us
  blocking collectives  27.4 us (50%)
  Pallas kernels  12.2 us (22%)
  starting transfers between devices  8.43 us (15%)
  waiting for transfers between devices  5.56 us (10%)
  between operations  0.74 us (1%)
    all_to_all x1, blocking collectives, body(): all_dots = lax.all_to_all(dots, ('lat', 'lon'), 0, 0, tiled=True)  27.4 us
    pallas_call x1, Pallas kernels, body(): pl.pallas_call(adjoint_kernel, grid=(COSTS,), in_specs=[full(devices, LAN...  8.5 us
    ppermute x1, starting transfers between devices, body(): side_w = lax.ppermute(to_east, 'lon', ring('lon', 1))  3.95 us
    ppermute x1, starting transfers between devices, body(): band_n = lax.ppermute(to_south, 'lat', ring('lat', -1))  2.37 us
    ppermute x1, waiting for transfers between devices, body(): side_e = lax.ppermute(to_west, 'lon', ring('lon', -1))  2.34 us
    pallas_call x1, Pallas kernels, body(): pl.pallas_call(forward_kernel, in_specs=[pl.BlockSpec(memory_space=pltpu....  2.17 us
    ppermute x1, waiting for transfers between devices, body(): band_s = lax.ppermute(to_north, 'lat', ring('lat', 1))  2.12 us
    ppermute x1, starting transfers between devices, body(): band_s = lax.ppermute(to_north, 'lat', ring('lat', 1))  2.11 us
  transfers between devices with their start and end apart: 4, of which 3 were waited for; matrix products, arithmetic and copies ran while one was open for 0% of the time, Pallas kernels for 1%

profile of v4, /device:TPU:1, one launch (start us, length us, event | category | flops | bytes accessed | tf_op | source)
XLA Modules:
  0.0 54.4 jit_solution(5409169608528488831)
XLA Ops:
  0.6 0.0 copy-start
  0.6 0.0 copy-start.5
  0.7 0.0 copy-start.4
  0.7 0.0 copy-start.3
  0.7 0.0 copy-start.2
  0.7 0.0 copy-start.1
  0.7 1.1 %bands.1 = (f32[144,256]{1,0:T(8,128)S(1)}, f32[144,256]{1,0:T(8,128)S(1)}) custom-call(f32[64,256]{1,0:T(8,128)} %f.5, f32[64,256]{1,0:T(8,128)} %de.5, f32[64,256]{1,0:T(8,128)} %dn.5, f32[64,256]{1,0:T(8,128)} %st.5, s32[64,256]{1,0:T(8,128)} %mask.5, f32[8,64,256]{2,1,0:T(8,128)} %w.7), custom_call_target="tpu_custom_call" | custom-call | tf_op jit(solution)/shard_map/bands/pallas_call | solution.py:456
  1.8 2.1 %collective-permute-start = (f32[144,256]{1,0:T(8,128)S(1)}, f32[144,256]{1,0:T(8,128)S(1)}, u32[]{:S(2)}, u32[]{:S(2)}) collective-permute-start(f32[144,256]{1,0:T(8,128)S(1)} %get-tuple-element.15), channel_id=1, source_target_pairs={{0,32},{32,64},{64,96},{96,128},{128,160},{160,192},{192,224},{224... | collective-permute-start | bytes 442376 | tf_op jit(solution)/shard_map/ppermute | solution.py:468
  3.9 2.4 %collective-permute-start.1 = (f32[144,256]{1,0:T(8,128)S(1)}, f32[144,256]{1,0:T(8,128)S(1)}, u32[]{:S(2)}, u32[]{:S(2)}) collective-permute-start(f32[144,256]{1,0:T(8,128)S(1)} %get-tuple-element.16), channel_id=1, source_target_pairs={{0,224},{32,0},{64,32},{96,64},{128,96},{160,128},{192,160},{224,1... | collective-permute-start | bytes 442376 | tf_op jit(solution)/shard_map/ppermute | solution.py:469
  6.3 0.0 copy-done
  6.3 0.0 copy-done.5
  6.3 0.0 copy-done.4
  6.3 0.0 copy-done.3
  6.3 0.0 copy-done.2
  6.3 0.0 copy-done.1
  6.3 0.3 strips.1
  6.6 2.1 %collective-permute-done.bs.ls.ws = f32[144,256]{1,0:T(8,128)S(1)} collective-permute-done((f32[144,256]{1,0:T(8,128)S(1)}, f32[144,256]{1,0:T(8,128)S(1)}, u32[]{:S(2)}, u32[]{:S(2)}) %collective-permute-start) | collective-permute-done | bytes 147488 | tf_op jit(solution)/shard_map/ppermute | solution.py:468
  8.8 0.0 collective-permute-done.1.bn.ln.wn
  8.8 0.1 corners.1
  8.9 3.9 %collective-permute-start.2 = (f32[96,128]{1,0:T(8,128)S(1)}, f32[96,128]{1,0:T(8,128)S(1)}, u32[]{:S(2)}, u32[]{:S(2)}) collective-permute-start(f32[96,128]{1,0:T(8,128)S(1)} %get-tuple-element.19), channel_id=1, source_target_pairs={{0,1},{1,2},{2,3},{3,4},{4,5},{5,6},{6,7},{7,8},{8,9},{9,10},{10,1... | collective-permute-start | bytes 147464 | tf_op jit(solution)/shard_map/ppermute | solution.py:486
  12.9 0.0 collective-permute-start.3
  12.9 0.1 add_convert_fusion.flags
  12.9 1.1 %collective-permute-done.2.sw = f32[96,128]{1,0:T(8,128)S(1)} collective-permute-done((f32[96,128]{1,0:T(8,128)S(1)}, f32[96,128]{1,0:T(8,128)S(1)}, u32[]{:S(2)}, u32[]{:S(2)}) %collective-permute-start.2) | collective-permute-done | bytes 49184 | tf_op jit(solution)/shard_map/ppermute | solution.py:486
  14.0 2.3 %collective-permute-done.3.se = f32[96,128]{1,0:T(8,128)S(1)} collective-permute-done((f32[96,128]{1,0:T(8,128)S(1)}, f32[96,128]{1,0:T(8,128)S(1)}, u32[]{:S(2)}, u32[]{:S(2)}) %collective-permute-start.3) | collective-permute-done | bytes 49184 | tf_op jit(solution)/shard_map/ppermute | solution.py:487
  16.4 2.2 %forward.1 = (f32[7,3,80,128]{3,2,1,0:T(8,128)S(1)}, f32[4,3,80,128]{3,2,1,0:T(8,128)S(1)}, f32[3,80,128]{2,1,0:T(8,128)S(1)}, f32[8,80,128]{2,1,0:T(8,128)S(1)}...) custom-call(s32[2]{0:T(128)S(1)} %add_convert_fusion.flags, f32[64,256]{1,0:T(8,128)S(1)} %copy-done.1, ...), custom_call_target="tpu_custom_call" | custom-call | tf_op jit(solution)/shard_map/forward/pallas_call | solution.py:490
  18.5 27.4 %all_to_all.11 = f32[256,1,128]{2,1,0:T(1,128)S(1)} all-to-all(f32[256,1,128]{2,1,0:T(1,128)S(1)} %bitcast.7), channel_id=1, replica_groups=mesh['lat'=8,'lon'=32] {'lat','lon'}, dimensions={0} | all-to-all | bytes 262144 | tf_op jit(solution)/shard_map/all_to_all | solution.py:510
  45.9 8.5 %adjoint.1 = (f32[8,64,256]{2,1,0:T(8,128)}, f32[8,64,256]{2,1,0:T(8,128)}, f32[8,64,256]{2,1,0:T(8,128)}) custom-call(f32[256,128]{1,0:T(8,128)S(1)} %bitcast.6, f32[7,3,80,128]{3,2,1,0:T(8,128)S(1)} %get-tuple-element.22.vecs, f32[4,3,80,128]{3,2,1,0:T(8,128)S(1)} %get-tuple-element.23.links, f32[3,80,128]{2,1,0:T(8,128)S(1)} %get-tuple-element.24.inv2, ...), custom_call_target="tpu_custom_call" | custom-call | tf_op jit(solution)/shard_map/adjoint/pallas_call | solution.py:513
Async XLA Ops:
  0.6 5.7 %copy-start = (f32[8,64,256]{2,1,0:T(8,128)S(1)}, f32[8,64,256]{2,1,0:T(8,128)}, u32[]{:S(2)}) copy-start(f32[8,64,256]{2,1,0:T(8,128)} %w.7) | copy-start | bytes 1572868
  0.6 5.7 %copy-start.5 = (s32[64,256]{1,0:T(8,128)S(1)}, s32[64,256]{1,0:T(8,128)}, u32[]{:S(2)}) copy-start(s32[64,256]{1,0:T(8,128)} %mask.5) | copy-start | bytes 196612
  0.7 5.7 %copy-start.4 = (f32[64,256]{1,0:T(8,128)S(1)}, f32[64,256]{1,0:T(8,128)}, u32[]{:S(2)}) copy-start(f32[64,256]{1,0:T(8,128)} %st.5) | copy-start | bytes 196612
  0.7 5.7 %copy-start.3 = (f32[64,256]{1,0:T(8,128)S(1)}, f32[64,256]{1,0:T(8,128)}, u32[]{:S(2)}) copy-start(f32[64,256]{1,0:T(8,128)} %dn.5) | copy-start | bytes 196612
  0.7 5.7 %copy-start.2 = (f32[64,256]{1,0:T(8,128)S(1)}, f32[64,256]{1,0:T(8,128)}, u32[]{:S(2)}) copy-start(f32[64,256]{1,0:T(8,128)} %de.5) | copy-start | bytes 196612
  0.7 5.7 %copy-start.1 = (f32[64,256]{1,0:T(8,128)S(1)}, f32[64,256]{1,0:T(8,128)}, u32[]{:S(2)}) copy-start(f32[64,256]{1,0:T(8,128)} %f.5) | copy-start | bytes 196612
  1.8 6.9 %collective-permute-start = (f32[144,256]{1,0:T(8,128)S(1)}, f32[144,256]{1,0:T(8,128)S(1)}, u32[]{:S(2)}, u32[]{:S(2)}) collective-permute-start(f32[144,256]{1,0:T(8,128)S(1)} %get-tuple-element.15), channel_id=1, source_target_pairs={{0,32},{32,64},{64,96},{96,128},{128,160},{160,192},{192,224},{224... | collective-permute-start | bytes 442376 | tf_op jit(solution)/shard_map/ppermute | solution.py:468
  3.9 4.8 %collective-permute-start.1 = (f32[144,256]{1,0:T(8,128)S(1)}, f32[144,256]{1,0:T(8,128)S(1)}, u32[]{:S(2)}, u32[]{:S(2)}) collective-permute-start(f32[144,256]{1,0:T(8,128)S(1)} %get-tuple-element.16), channel_id=1, source_target_pairs={{0,224},{32,0},{64,32},{96,64},{128,96},{160,128},{192,160},{224,1... | collective-permute-start | bytes 442376 | tf_op jit(solution)/shard_map/ppermute | solution.py:469
  8.9 5.1 %collective-permute-start.2 = (f32[96,128]{1,0:T(8,128)S(1)}, f32[96,128]{1,0:T(8,128)S(1)}, u32[]{:S(2)}, u32[]{:S(2)}) collective-permute-start(f32[96,128]{1,0:T(8,128)S(1)} %get-tuple-element.19), channel_id=1, source_target_pairs={{0,1},{1,2},{2,3},{3,4},{4,5},{5,6},{6,7},{7,8},{8,9},{9,10},{10,1... | collective-permute-start | bytes 147464 | tf_op jit(solution)/shard_map/ppermute | solution.py:486
  12.9 3.5 %collective-permute-start.3 = (f32[96,128]{1,0:T(8,128)S(1)}, f32[96,128]{1,0:T(8,128)S(1)}, u32[]{:S(2)}, u32[]{:S(2)}) collective-permute-start(f32[96,128]{1,0:T(8,128)S(1)} %get-tuple-element.20), channel_id=1, source_target_pairs={{0,31},{1,0},{2,1},{3,2},{4,3},{5,4},{6,5},{7,6},{8,7},{9,8},{10,9... | collective-permute-start | bytes 147464 | tf_op jit(solution)/shard_map/ppermute | solution.py:487

commit v5 on v4

--- a/solution.py
+++ b/solution.py
@@ -116,7 +116,7 @@
 
 def forward_kernel(
     flags, f, de, dn, st, mask, w, ls, ln, sw, se,
-    vecs, links, inv2, wside, wet, dots,
+    vecs, links, wside, wet, dots,
     raw, north, vec, link, diag, part,
 ):
     own = (f, de, dn, st, mask)
@@ -177,7 +177,7 @@
             if 1 <= rb < 11:
                 to = slice(8 * rb - 8, 8 * rb)
                 vecs[0, t, to, :] = v0
-                inv2[t, to, :] = twice
+                vecs[ITERS + 1, t, to, :] = twice
                 for k in range(4):
                     links[k, t, to, :] = values[k]
             if 2 <= rb < 10 and t < 2:
@@ -302,7 +302,7 @@
 
 
 def adjoint_kernel(
-    all_dots, vecs, links, inv2, wet, w, wside, ws, wn,
+    all_dots, vecs, links, wet, w, wside, ws, wn,
     adj, east, north,
     lam, lam2, cs, slope, lag, rs, ys, ss, ps, acc,
 ):
@@ -373,7 +373,7 @@
                 weight = wn[:, lanes_of(t)]
             else:
                 weight = w[0, 8 * rb - 8 : 8 * rb, lanes_of(t)]
-            s = inv2[t, here, :] * weight - mixed(rows2, v)
+            s = vecs[ITERS + 1, t, here, :] * weight - mixed(rows2, v)
             ss[t, here, :] = s
             ps[last - 1, t, at : at + 8, :] = c_last * s + rows[last] * rs[t, here, :]
             if rb >= 1:
@@ -487,13 +487,13 @@
     side_e = lax.ppermute(to_west, "lon", ring("lon", -1))
     row = lax.axis_index("lat")
     flags = jnp.stack([row > 0, row < lats - 1]).astype(jnp.int32)
-    vecs, links, inv2, wside, wet, dots = pl.pallas_call(
+    vecs, links, wside, wet, dots = pl.pallas_call(
         forward_kernel,
         in_specs=[pl.BlockSpec(memory_space=pltpu.SMEM)] + [whole()] * 10,
-        out_specs=[whole()] * 6,
+        out_specs=[whole()] * 5,
         out_shape=(
-            struct(ITERS + 1, TILES, FRAME, LANES), struct(4, TILES, FRAME, LANES),
-            struct(TILES, FRAME, LANES), struct(COSTS, FRAME, LANES),
+            struct(ITERS + 2, TILES, FRAME, LANES), struct(4, TILES, FRAME, LANES),
+            struct(COSTS, FRAME, LANES),
             struct(2, ROWS, COLS), struct(devices, LANES),
         ),
         scratch_shapes=[
@@ -509,16 +509,14 @@
     )(flags, *args, band_s, band_n, side_w, side_e)
     all_dots = lax.all_to_all(dots, ("lat", "lon"), 0, 0, tiled=True)
     out_spec = pl.BlockSpec((1, ROWS, COLS), lambda n: (n, 0, 0))
-    full = lambda *shape: pl.BlockSpec(shape, lambda n: (0,) * len(shape))
     return pl.pallas_call(
         adjoint_kernel,
         grid=(COSTS,),
         in_specs=[
-            full(devices, LANES),
-            full(ITERS + 1, TILES, FRAME, LANES),
-            full(4, TILES, FRAME, LANES),
-            full(TILES, FRAME, LANES),
-            full(2, ROWS, COLS),
+            whole(),
+            whole(),
+            whole(),
+            whole(),
             pl.BlockSpec((1, ROWS, COLS), lambda n: (n, 0, 0)),
             pl.BlockSpec((1, FRAME, LANES), lambda n: (n, 0, 0)),
             pl.BlockSpec((8, COLS), lambda n: (MSG_W // 8 + n, 0)),
@@ -542,7 +540,7 @@
             dimension_semantics=("arbitrary",), vmem_limit_bytes=18 << 20
         ),
         name="adjoint",
-    )(all_dots, vecs, links, inv2, wet, cost_weights, wside, band_s, band_n)
+    )(all_dots, vecs, links, wet, cost_weights, wside, band_s, band_n)
 
 
 def solution(mesh):

time: 54.6 us -> 53.3 us (0.976)
  Pallas kernels: 12.2 us -> 10.9 us
    pallas_call x1, Pallas kernels: 8.5 us -> 7.27 us  [body(): pl.pallas_call(adjoint_kernel, grid=(COSTS,), in_specs=[whole(), whole(),...]
where the time goes in v5:
time: 53.3 us; the launch traced here: 53.1 us
  blocking collectives  27.4 us (51%)
  Pallas kernels  10.9 us (20%)
  starting transfers between devices  8.43 us (16%)
  waiting for transfers between devices  5.56 us (10%)
  between operations  0.74 us (1%)
    all_to_all x1, blocking collectives, body(): all_dots = lax.all_to_all(dots, ('lat', 'lon'), 0, 0, tiled=True)  27.4 us
    pallas_call x1, Pallas kernels, body(): pl.pallas_call(adjoint_kernel, grid=(COSTS,), in_specs=[whole(), whole(),...  7.27 us
    ppermute x1, starting transfers between devices, body(): side_w = lax.ppermute(to_east, 'lon', ring('lon', 1))  3.95 us
    ppermute x1, starting transfers between devices, body(): band_n = lax.ppermute(to_south, 'lat', ring('lat', -1))  2.37 us
    ppermute x1, waiting for transfers between devices, body(): side_e = lax.ppermute(to_west, 'lon', ring('lon', -1))  2.34 us
    ppermute x1, waiting for transfers between devices, body(): band_s = lax.ppermute(to_north, 'lat', ring('lat', 1))  2.12 us
    ppermute x1, starting transfers between devices, body(): band_s = lax.ppermute(to_north, 'lat', ring('lat', 1))  2.11 us
    pallas_call x1, Pallas kernels, body(): pl.pallas_call(forward_kernel, in_specs=[pl.BlockSpec(memory_space=pltpu....  2.05 us
  transfers between devices with their start and end apart: 4, of which 3 were waited for; matrix products, arithmetic and copies ran while one was open for 0% of the time, Pallas kernels for 1%

profile of v5, /device:TPU:1, one launch (start us, length us, event | category | flops | bytes accessed | tf_op | source)
XLA Modules:
  0.0 53.1 jit_solution(8144798491475375111)
XLA Ops:
  0.6 0.0 copy-start
  0.6 0.0 copy-start.5
  0.7 0.0 copy-start.4
  0.7 0.0 copy-start.3
  0.7 0.0 copy-start.2
  0.7 0.0 copy-start.1
  0.7 1.1 %bands.1 = (f32[144,256]{1,0:T(8,128)S(1)}, f32[144,256]{1,0:T(8,128)S(1)}) custom-call(f32[64,256]{1,0:T(8,128)} %f.5, f32[64,256]{1,0:T(8,128)} %de.5, f32[64,256]{1,0:T(8,128)} %dn.5, f32[64,256]{1,0:T(8,128)} %st.5, s32[64,256]{1,0:T(8,128)} %mask.5, f32[8,64,256]{2,1,0:T(8,128)} %w.7), custom_call_target="tpu_custom_call" | custom-call | tf_op jit(solution)/shard_map/bands/pallas_call | solution.py:456
  1.8 2.1 %collective-permute-start = (f32[144,256]{1,0:T(8,128)S(1)}, f32[144,256]{1,0:T(8,128)S(1)}, u32[]{:S(2)}, u32[]{:S(2)}) collective-permute-start(f32[144,256]{1,0:T(8,128)S(1)} %get-tuple-element.14), channel_id=1, source_target_pairs={{0,32},{32,64},{64,96},{96,128},{128,160},{160,192},{192,224},{224... | collective-permute-start | bytes 442376 | tf_op jit(solution)/shard_map/ppermute | solution.py:468
  3.9 2.4 %collective-permute-start.1 = (f32[144,256]{1,0:T(8,128)S(1)}, f32[144,256]{1,0:T(8,128)S(1)}, u32[]{:S(2)}, u32[]{:S(2)}) collective-permute-start(f32[144,256]{1,0:T(8,128)S(1)} %get-tuple-element.15), channel_id=1, source_target_pairs={{0,224},{32,0},{64,32},{96,64},{128,96},{160,128},{192,160},{224,1... | collective-permute-start | bytes 442376 | tf_op jit(solution)/shard_map/ppermute | solution.py:469
  6.3 0.0 copy-done
  6.3 0.0 copy-done.5
  6.3 0.0 copy-done.4
  6.3 0.0 copy-done.3
  6.3 0.0 copy-done.2
  6.3 0.0 copy-done.1
  6.3 0.3 strips.1
  6.6 2.1 %collective-permute-done.bs.ls.ws = f32[144,256]{1,0:T(8,128)S(1)} collective-permute-done((f32[144,256]{1,0:T(8,128)S(1)}, f32[144,256]{1,0:T(8,128)S(1)}, u32[]{:S(2)}, u32[]{:S(2)}) %collective-permute-start) | collective-permute-done | bytes 147488 | tf_op jit(solution)/shard_map/ppermute | solution.py:468
  8.8 0.0 collective-permute-done.1.bn.ln.wn
  8.8 0.1 corners.1
  8.9 3.9 %collective-permute-start.2 = (f32[96,128]{1,0:T(8,128)S(1)}, f32[96,128]{1,0:T(8,128)S(1)}, u32[]{:S(2)}, u32[]{:S(2)}) collective-permute-start(f32[96,128]{1,0:T(8,128)S(1)} %get-tuple-element.18), channel_id=1, source_target_pairs={{0,1},{1,2},{2,3},{3,4},{4,5},{5,6},{6,7},{7,8},{8,9},{9,10},{10,1... | collective-permute-start | bytes 147464 | tf_op jit(solution)/shard_map/ppermute | solution.py:486
  12.9 0.0 collective-permute-start.3
  12.9 0.1 add_convert_fusion.flags
  12.9 1.1 %collective-permute-done.2.sw = f32[96,128]{1,0:T(8,128)S(1)} collective-permute-done((f32[96,128]{1,0:T(8,128)S(1)}, f32[96,128]{1,0:T(8,128)S(1)}, u32[]{:S(2)}, u32[]{:S(2)}) %collective-permute-start.2) | collective-permute-done | bytes 49184 | tf_op jit(solution)/shard_map/ppermute | solution.py:486
  14.0 2.3 %collective-permute-done.3.se = f32[96,128]{1,0:T(8,128)S(1)} collective-permute-done((f32[96,128]{1,0:T(8,128)S(1)}, f32[96,128]{1,0:T(8,128)S(1)}, u32[]{:S(2)}, u32[]{:S(2)}) %collective-permute-start.3) | collective-permute-done | bytes 49184 | tf_op jit(solution)/shard_map/ppermute | solution.py:487
  16.4 2.1 %forward.1 = (f32[8,3,80,128]{3,2,1,0:T(8,128)S(1)}, f32[4,3,80,128]{3,2,1,0:T(8,128)S(1)}, f32[8,80,128]{2,1,0:T(8,128)S(1)}, f32[2,64,256]{2,1,0:T(8,128)S(1)}, f32[256,128]{1,0:T(8,128)S(1)}) custom-call(s32[2]{0:T(128)S(1)} %add_convert_fusion.flags, f32[64,256]{1,0:T(8,128)S(1)} %copy-done.1, f32[64,256]{1,0:T(8,128)S(1)} %copy-done.2, ...), custom_call_target="tpu_custom_call" | custom-call | tf_op jit(solution)/shard_map/forward/pallas_call | solution.py:490
  18.4 27.4 %all_to_all.11 = f32[256,1,128]{2,1,0:T(1,128)S(1)} all-to-all(f32[256,1,128]{2,1,0:T(1,128)S(1)} %bitcast.7), channel_id=1, replica_groups=mesh['lat'=8,'lon'=32] {'lat','lon'}, dimensions={0} | all-to-all | bytes 262144 | tf_op jit(solution)/shard_map/all_to_all | solution.py:510
  45.8 7.3 %adjoint.1 = (f32[8,64,256]{2,1,0:T(8,128)}, f32[8,64,256]{2,1,0:T(8,128)}, f32[8,64,256]{2,1,0:T(8,128)}) custom-call(f32[256,128]{1,0:T(8,128)S(1)} %bitcast.6, f32[8,3,80,128]{3,2,1,0:T(8,128)S(1)} %get-tuple-element.21.vecs, f32[4,3,80,128]{3,2,1,0:T(8,128)S(1)} %get-tuple-element.22.links, f32[2,64,256]{2,1,0:T(8,128)S(1)} %get-tuple-element.23.wet, ...), custom_call_target="tpu_custom_call" | custom-call | tf_op jit(solution)/shard_map/adjoint/pallas_call | solution.py:512
Async XLA Ops:
  0.6 5.7 %copy-start = (f32[8,64,256]{2,1,0:T(8,128)S(1)}, f32[8,64,256]{2,1,0:T(8,128)}, u32[]{:S(2)}) copy-start(f32[8,64,256]{2,1,0:T(8,128)} %w.7) | copy-start | bytes 1572868
  0.6 5.7 %copy-start.5 = (s32[64,256]{1,0:T(8,128)S(1)}, s32[64,256]{1,0:T(8,128)}, u32[]{:S(2)}) copy-start(s32[64,256]{1,0:T(8,128)} %mask.5) | copy-start | bytes 196612
  0.7 5.7 %copy-start.4 = (f32[64,256]{1,0:T(8,128)S(1)}, f32[64,256]{1,0:T(8,128)}, u32[]{:S(2)}) copy-start(f32[64,256]{1,0:T(8,128)} %st.5) | copy-start | bytes 196612
  0.7 5.7 %copy-start.3 = (f32[64,256]{1,0:T(8,128)S(1)}, f32[64,256]{1,0:T(8,128)}, u32[]{:S(2)}) copy-start(f32[64,256]{1,0:T(8,128)} %dn.5) | copy-start | bytes 196612
  0.7 5.7 %copy-start.2 = (f32[64,256]{1,0:T(8,128)S(1)}, f32[64,256]{1,0:T(8,128)}, u32[]{:S(2)}) copy-start(f32[64,256]{1,0:T(8,128)} %de.5) | copy-start | bytes 196612
  0.7 5.7 %copy-start.1 = (f32[64,256]{1,0:T(8,128)S(1)}, f32[64,256]{1,0:T(8,128)}, u32[]{:S(2)}) copy-start(f32[64,256]{1,0:T(8,128)} %f.5) | copy-start | bytes 196612
  1.8 6.9 %collective-permute-start = (f32[144,256]{1,0:T(8,128)S(1)}, f32[144,256]{1,0:T(8,128)S(1)}, u32[]{:S(2)}, u32[]{:S(2)}) collective-permute-start(f32[144,256]{1,0:T(8,128)S(1)} %get-tuple-element.14), channel_id=1, source_target_pairs={{0,32},{32,64},{64,96},{96,128},{128,160},{160,192},{192,224},{224... | collective-permute-start | bytes 442376 | tf_op jit(solution)/shard_map/ppermute | solution.py:468
  3.9 4.8 %collective-permute-start.1 = (f32[144,256]{1,0:T(8,128)S(1)}, f32[144,256]{1,0:T(8,128)S(1)}, u32[]{:S(2)}, u32[]{:S(2)}) collective-permute-start(f32[144,256]{1,0:T(8,128)S(1)} %get-tuple-element.15), channel_id=1, source_target_pairs={{0,224},{32,0},{64,32},{96,64},{128,96},{160,128},{192,160},{224,1... | collective-permute-start | bytes 442376 | tf_op jit(solution)/shard_map/ppermute | solution.py:469
  8.9 5.1 %collective-permute-start.2 = (f32[96,128]{1,0:T(8,128)S(1)}, f32[96,128]{1,0:T(8,128)S(1)}, u32[]{:S(2)}, u32[]{:S(2)}) collective-permute-start(f32[96,128]{1,0:T(8,128)S(1)} %get-tuple-element.18), channel_id=1, source_target_pairs={{0,1},{1,2},{2,3},{3,4},{4,5},{5,6},{6,7},{7,8},{8,9},{9,10},{10,1... | collective-permute-start | bytes 147464 | tf_op jit(solution)/shard_map/ppermute | solution.py:486
  12.9 3.5 %collective-permute-start.3 = (f32[96,128]{1,0:T(8,128)S(1)}, f32[96,128]{1,0:T(8,128)S(1)}, u32[]{:S(2)}, u32[]{:S(2)}) collective-permute-start(f32[96,128]{1,0:T(8,128)S(1)} %get-tuple-element.19), channel_id=1, source_target_pairs={{0,31},{1,0},{2,1},{3,2},{4,3},{5,4},{6,5},{7,6},{8,7},{9,8},{10,9... | collective-permute-start | bytes 147464 | tf_op jit(solution)/shard_map/ppermute | solution.py:487

commit v6 on v5

--- a/solution.py
+++ b/solution.py
@@ -13,6 +13,7 @@
 COLS = 256
 LANES = 128
 TILES = 3
+PAIR = 2
 DEEP = 13
 SLIM = 6
 EDGE = 16
@@ -36,15 +37,20 @@
     return pltpu.roll(value, amount % value.shape[1], 1)
 
 
-def pack(rows, tiles):
+def starts(shift):
+    wides = [DEEP] * FIELDS + [SLIM] * COSTS
+    firsts = [sum(wides[:k]) - (wides[k] if shift else 0) for k in range(len(wides))]
+    return list(zip(firsts, wides))
+
+
+def pack(rows, tiles, shift):
     lane = lane_index(rows)
     out = jnp.zeros((rows, LANES), F32)
-    at = 0
-    for tile, first, wide in tiles:
-        if tile is not None:
-            here = (lane >= at) & (lane < at + wide)
+    for entry, (at, wide) in zip(tiles, starts(shift)):
+        if entry is not None:
+            tile, first = entry
+            here = (lane >= at) & (lane < at + wide) if at >= 0 else lane >= at + LANES
             out = jnp.where(here, turn(tile, at - first), out)
-        at += wide
     return out
 
 
@@ -72,12 +78,12 @@
 
 def strips_kernel(f, de, dn, st, mask, w, east, west):
     fields = [f[...], de[...], dn[...], st[...], mask[...].astype(F32)]
-    right = [(v[:, LANES:], LANES - DEEP, DEEP) for v in fields]
-    left = [(v[:, :LANES], 0, DEEP) for v in fields]
-    right += [(w[n, :, LANES:], LANES - SLIM, SLIM) for n in range(COSTS)]
-    left += [(w[n, :, :LANES], 0, SLIM) for n in range(COSTS)]
-    east[...] = pack(ROWS, right)
-    west[...] = pack(ROWS, left)
+    right = [(v[:, LANES:], LANES - DEEP) for v in fields]
+    left = [(v[:, :LANES], 0) for v in fields]
+    right += [(w[n, :, LANES:], LANES - SLIM) for n in range(COSTS)]
+    left += [(w[n, :, :LANES], 0) for n in range(COSTS)]
+    east[...] = pack(ROWS, right, True)
+    west[...] = pack(ROWS, left, False)
 
 
 def corners_kernel(east, west, bs, bn, to_east, to_west):
@@ -88,18 +94,19 @@
                 tiles = []
                 for k in range(FIELDS):
                     at = EDGE * k + 8 * half
-                    tiles.append((band[at : at + 8, lanes], LANES - DEEP if first else 0, DEEP))
+                    tiles.append((band[at : at + 8, lanes], LANES - DEEP if first else 0))
                 for n in range(COSTS):
                     at = MSG_W + 8 * n
-                    tile = band[at : at + 8, lanes] if half == slim else None
-                    tiles.append((tile, LANES - SLIM if first else 0, SLIM))
-                out[low + 8 * half : low + 8 * half + 8, :] = pack(8, tiles)
-
-
-def side_tile(pw, pe, at, wide):
+                    entry = (band[at : at + 8, lanes], LANES - SLIM if first else 0)
+                    tiles.append(entry if half == slim else None)
+                out[low + 8 * half : low + 8 * half + 8, :] = pack(8, tiles, first)
+
+
+def side_tile(pw, pe, k):
     lane = lane_index(pw.shape[0])
-    west = jnp.where(lane >= LANES - wide, turn(pw, LANES - wide - at), 0.0)
-    return jnp.where(lane < wide, turn(pe, -at), west)
+    at, wide = starts(False)[k]
+    both = jnp.where((lane >= at) & (lane < at + wide), pe, pw)
+    return jnp.where((lane < wide) | (lane >= LANES - wide), turn(both, -at), 0.0)
 
 
 def east_of(tiles):
@@ -138,7 +145,7 @@
                     values.append(own[k][off : off + 8, lanes].astype(F32))
                 else:
                     values.append(src[EDGE * k + off : EDGE * k + off + 8, lanes])
-            values.append(side_tile(pw, pe, DEEP * k, DEEP))
+            values.append(side_tile(pw, pe, k))
             if k == FIELDS - 1 and src is not None:
                 inside = flags[0 if rb < 2 else 1] > 0
                 values = [jnp.where(inside, value, 0.0) for value in values]
@@ -146,9 +153,7 @@
                 raw[k, t, at : at + 8, :] = values[t]
         if 1 <= rb < 11:
             for n in range(COSTS):
-                wside[n, 8 * rb - 8 : 8 * rb, :] = side_tile(
-                    pw, pe, FIELDS * DEEP + SLIM * n, SLIM
-                )
+                wside[n, 8 * rb - 8 : 8 * rb, :] = side_tile(pw, pe, FIELDS + n)
     for rb in blocks:
         here = slice(8 + 8 * rb, 16 + 8 * rb)
         above = slice(9 + 8 * rb, 17 + 8 * rb)
@@ -355,39 +360,43 @@
                 for t in range(2):
                     slope[d, ITERS - 1, t, to, :] = sums[d][t]
 
-    spread = lambda ref, k: jnp.broadcast_to(ref[pl.ds(8 * k + n, 1), :], (8, LANES))
-    rows = [spread(lam, j) for j in range(ITERS)]
-    rows2 = [spread(lam2, k) for k in range(ITERS + 1)]
+    pair = range(PAIR)
+    spread = lambda ref, k, h: jnp.broadcast_to(ref[pl.ds(8 * k + PAIR * n + h, 1), :], (8, LANES))
+    rows = [[spread(lam, j, h) for j in range(ITERS)] for h in pair]
+    rows2 = [[spread(lam2, k, h) for k in range(ITERS + 1)] for h in pair]
     last = ITERS - 1
     c_last = cs[8 * last : 8 * last + 8, :]
+    lagged = lambda rb: slice(8 * rb - 8, 8 * rb)
     for rb in blocks:
         at = 8 + 8 * rb
         here = slice(8 * rb, 8 * rb + 8)
         for t in tiles:
             v = [vecs[k, t, here, :] for k in range(ITERS + 1)]
-            if t == 2:
-                weight = wside[0, here, :]
-            elif rb == 0:
-                weight = ws[:, lanes_of(t)]
-            elif rb == 9:
-                weight = wn[:, lanes_of(t)]
-            else:
-                weight = w[0, 8 * rb - 8 : 8 * rb, lanes_of(t)]
-            s = vecs[ITERS + 1, t, here, :] * weight - mixed(rows2, v)
-            ss[t, here, :] = s
-            ps[last - 1, t, at : at + 8, :] = c_last * s + rows[last] * rs[t, here, :]
-            if rb >= 1:
-                ys[t, here, :] = mixed(rows, v)
+            scale, res = vecs[ITERS + 1, t, here, :], rs[t, here, :]
+            for h in pair:
+                if t == 2:
+                    weight = wside[h, here, :]
+                elif rb == 0:
+                    weight = ws[8 * h : 8 * h + 8, lanes_of(t)]
+                elif rb == 9:
+                    weight = wn[8 * h : 8 * h + 8, lanes_of(t)]
+                else:
+                    weight = w[h, lagged(rb), lanes_of(t)]
+                s = scale * weight - mixed(rows2[h], v)
+                ss[h, t, here, :] = s
+                ps[h, last - 1, t, at : at + 8, :] = c_last * s + rows[h][last] * res
+                if rb >= 1:
+                    ys[h, t, here, :] = mixed(rows[h], v)
     for rb in range(1, 9):
         here = slice(8 * rb, 8 * rb + 8)
         above = slice(8 * rb + 1, 8 * rb + 9)
-        to = slice(8 * rb - 8, 8 * rb)
-        y = [ys[t, here, :] for t in tiles]
-        ye = east_of(y)
-        for t in range(2):
-            acc[0, t, to, :] = (y[t] - ye[t]) * slope[0, last, t, to, :]
-            acc[1, t, to, :] = (y[t] - ys[t, above, :]) * slope[1, last, t, to, :]
-    lagged = lambda rb: slice(8 * rb - 8, 8 * rb)
+        to = lagged(rb)
+        for h in pair:
+            y = [ys[h, t, here, :] for t in tiles]
+            ye = east_of(y)
+            for t in range(2):
+                acc[h, 0, t, to, :] = (y[t] - ye[t]) * slope[0, last, t, to, :]
+                acc[h, 1, t, to, :] = (y[t] - ys[h, t, above, :]) * slope[1, last, t, to, :]
     for j in range(ITERS - 2, -1, -1):
         c_j = cs[8 * j : 8 * j + 8, :]
         for rb in blocks:
@@ -395,44 +404,54 @@
                 continue
             at = 8 + 8 * rb
             here = slice(8 * rb, 8 * rb + 8)
-            p = [ps[j, t, at : at + 8, :] for t in tiles]
-            pe, pw = east_of(p), west_of(p)
+            p = [[ps[h, j, t, at : at + 8, :] for t in tiles] for h in pair]
+            pe, pw = [east_of(q) for q in p], [west_of(q) for q in p]
             for t in tiles:
-                pn = ps[j, t, at + 1 : at + 9, :]
-                bar = (
-                    links[0, t, here, :] * pe[t]
-                    + links[1, t, here, :] * pw[t]
-                    + links[2, t, here, :] * pn
-                    + links[3, t, here, :] * ps[j, t, at - 1 : at + 7, :]
-                ) + (c_j * ss[t, here, :] + rows[j] * rs[t, here, :])
-                if j < ITERS - 2:
-                    bar = bar - ps[j + 1, t, at : at + 8, :]
-                if j == 1:
-                    bar = 0.5 * bar
-                if j > 0:
-                    ps[j - 1, t, at : at + 8, :] = bar
+                link = [links[k, t, here, :] for k in range(4)]
+                res = rs[t, here, :]
                 if rb >= 1:
-                    d = p[t] * lag[j, t, here, :]
+                    late = lag[j, t, here, :]
+                    if j == 0:
+                        v0 = vecs[0, t, here, :]
+                inside = 1 <= rb < 9 and t < 2
+                if inside:
+                    to = lagged(rb)
+                    slope_e, slope_n = slope[0, j, t, to, :], slope[1, j, t, to, :]
+                for h in pair:
+                    here_p = p[h][t]
+                    pn = ps[h, j, t, at + 1 : at + 9, :]
+                    bar = (
+                        link[0] * pe[h][t] + link[1] * pw[h][t]
+                        + link[2] * pn + link[3] * ps[h, j, t, at - 1 : at + 7, :]
+                    ) + (c_j * ss[h, t, here, :] + rows[h][j] * res)
                     if j < ITERS - 2:
-                        d = acc[2, t, lagged(rb), :] + d
-                    if j == 0:
-                        g = 0.5 * bar
-                        d = d + g * vecs[0, t, here, :]
-                    acc[2, t, lagged(rb), :] = d
-                if 1 <= rb < 9 and t < 2:
-                    to = lagged(rb)
-                    acc[0, t, to, :] = acc[0, t, to, :] + (p[t] - pe[t]) * slope[0, j, t, to, :]
-                    acc[1, t, to, :] = acc[1, t, to, :] + (p[t] - pn) * slope[1, j, t, to, :]
-                    if j == 0:
-                        adj[0, to, lanes_of(t)] = ys[t, here, :] + g
+                        bar = bar - ps[h, j + 1, t, at : at + 8, :]
+                    if j == 1:
+                        bar = 0.5 * bar
+                    if j > 0:
+                        ps[h, j - 1, t, at : at + 8, :] = bar
+                    if rb >= 1:
+                        d = here_p * late
+                        if j < ITERS - 2:
+                            d = acc[h, 2, t, lagged(rb), :] + d
+                        if j == 0:
+                            g = 0.5 * bar
+                            d = d + g * v0
+                        acc[h, 2, t, lagged(rb), :] = d
+                    if inside:
+                        acc[h, 0, t, to, :] = acc[h, 0, t, to, :] + (here_p - pe[h][t]) * slope_e
+                        acc[h, 1, t, to, :] = acc[h, 1, t, to, :] + (here_p - pn) * slope_n
+                        if j == 0:
+                            adj[h, to, lanes_of(t)] = ys[h, t, here, :] + g
     for rb in range(ROWS // 8):
         to = slice(8 * rb, 8 * rb + 8)
-        d = [acc[2, t, to, :] for t in tiles]
-        de = east_of(d)
-        for t in range(2):
-            above = acc[2, t, 8 * rb + 1 : 8 * rb + 9, :]
-            east[0, to, lanes_of(t)] = -wet[0, to, lanes_of(t)] * (acc[0, t, to, :] + d[t] + de[t])
-            north[0, to, lanes_of(t)] = -wet[1, to, lanes_of(t)] * (acc[1, t, to, :] + d[t] + above)
+        for h in pair:
+            d = [acc[h, 2, t, to, :] for t in tiles]
+            de = east_of(d)
+            for t in range(2):
+                above = acc[h, 2, t, 8 * rb + 1 : 8 * rb + 9, :]
+                east[h, to, lanes_of(t)] = -wet[0, to, lanes_of(t)] * (acc[h, 0, t, to, :] + d[t] + de[t])
+                north[h, to, lanes_of(t)] = -wet[1, to, lanes_of(t)] * (acc[h, 1, t, to, :] + d[t] + above)
 
 
 def ring(axis, steps):
@@ -508,19 +527,19 @@
         name="forward",
     )(flags, *args, band_s, band_n, side_w, side_e)
     all_dots = lax.all_to_all(dots, ("lat", "lon"), 0, 0, tiled=True)
-    out_spec = pl.BlockSpec((1, ROWS, COLS), lambda n: (n, 0, 0))
+    out_spec = pl.BlockSpec((PAIR, ROWS, COLS), lambda n: (n, 0, 0))
     return pl.pallas_call(
         adjoint_kernel,
-        grid=(COSTS,),
+        grid=(COSTS // PAIR,),
         in_specs=[
             whole(),
             whole(),
             whole(),
             whole(),
-            pl.BlockSpec((1, ROWS, COLS), lambda n: (n, 0, 0)),
-            pl.BlockSpec((1, FRAME, LANES), lambda n: (n, 0, 0)),
-            pl.BlockSpec((8, COLS), lambda n: (MSG_W // 8 + n, 0)),
-            pl.BlockSpec((8, COLS), lambda n: (MSG_W // 8 + n, 0)),
+            pl.BlockSpec((PAIR, ROWS, COLS), lambda n: (n, 0, 0)),
+            pl.BlockSpec((PAIR, FRAME, LANES), lambda n: (n, 0, 0)),
+            pl.BlockSpec((8 * PAIR, COLS), lambda n: (MSG_W // (8 * PAIR) + n, 0)),
+            pl.BlockSpec((8 * PAIR, COLS), lambda n: (MSG_W // (8 * PAIR) + n, 0)),
         ],
         out_specs=[out_spec] * 3,
         out_shape=(struct(COSTS, ROWS, COLS),) * 3,
@@ -531,10 +550,10 @@
             pltpu.VMEM((2, ITERS, 2, ROWS, LANES), F32),
             pltpu.VMEM((ITERS - 1, TILES, FRAME, LANES), F32),
             pltpu.VMEM((TILES, FRAME, LANES), F32),
-            pltpu.VMEM((TILES, FRAME, LANES), F32),
-            pltpu.VMEM((TILES, FRAME, LANES), F32),
-            pltpu.VMEM((ITERS - 1, TILES, FRAME + 16, LANES), F32),
-            pltpu.VMEM((3, TILES, FRAME - 8, LANES), F32),
+            pltpu.VMEM((PAIR, TILES, FRAME, LANES), F32),
+            pltpu.VMEM((PAIR, TILES, FRAME, LANES), F32),
+            pltpu.VMEM((PAIR, ITERS - 1, TILES, FRAME + 16, LANES), F32),
+            pltpu.VMEM((PAIR, 3, TILES, FRAME - 8, LANES), F32),
         ],
         compiler_params=pltpu.CompilerParams(
             dimension_semantics=("arbitrary",), vmem_limit_bytes=18 << 20

time: 53.3 us -> 52.7 us (0.989)
  Pallas kernels: 10.9 us -> 10.3 us
where the time goes in v6:
time: 52.7 us; the launch traced here: 52.6 us
  blocking collectives  27.4 us (52%)
  Pallas kernels  10.3 us (20%)
  starting transfers between devices  8.43 us (16%)
  waiting for transfers between devices  5.56 us (11%)
  between operations  0.74 us (1%)
    all_to_all x1, blocking collectives, body(): all_dots = lax.all_to_all(dots, ('lat', 'lon'), 0, 0, tiled=True)  27.4 us
    pallas_call x1, Pallas kernels, body(): pl.pallas_call(adjoint_kernel, grid=(COSTS // PAIR,), in_specs=[whole(),...  6.85 us
    ppermute x1, starting transfers between devices, body(): side_w = lax.ppermute(to_east, 'lon', ring('lon', 1))  3.95 us
    ppermute x1, starting transfers between devices, body(): band_n = lax.ppermute(to_south, 'lat', ring('lat', -1))  2.37 us
    ppermute x1, waiting for transfers between devices, body(): side_e = lax.ppermute(to_west, 'lon', ring('lon', -1))  2.34 us
    ppermute x1, waiting for transfers between devices, body(): band_s = lax.ppermute(to_north, 'lat', ring('lat', 1))  2.12 us
    ppermute x1, starting transfers between devices, body(): band_s = lax.ppermute(to_north, 'lat', ring('lat', 1))  2.11 us
    pallas_call x1, Pallas kernels, body(): pl.pallas_call(forward_kernel, in_specs=[pl.BlockSpec(memory_space=pltpu....  1.95 us
  transfers between devices with their start and end apart: 4, of which 3 were waited for; matrix products, arithmetic and copies ran while one was open for 0% of the time, Pallas kernels for 1%

profile of v6, /device:TPU:1, one launch (start us, length us, event | category | flops | bytes accessed | tf_op | source)
XLA Modules:
  0.0 52.6 jit_solution(9951954441016822524)
XLA Ops:
  0.6 0.0 copy-start
  0.6 0.0 copy-start.5
  0.7 0.0 copy-start.4
  0.7 0.0 copy-start.3
  0.7 0.0 copy-start.2
  0.7 0.0 copy-start.1
  0.7 1.1 %bands.1 = (f32[144,256]{1,0:T(8,128)S(1)}, f32[144,256]{1,0:T(8,128)S(1)}) custom-call(f32[64,256]{1,0:T(8,128)} %f.5, f32[64,256]{1,0:T(8,128)} %de.5, f32[64,256]{1,0:T(8,128)} %dn.5, f32[64,256]{1,0:T(8,128)} %st.5, s32[64,256]{1,0:T(8,128)} %mask.5, f32[8,64,256]{2,1,0:T(8,128)} %w.7), custom_call_target="tpu_custom_call" | custom-call | tf_op jit(solution)/shard_map/bands/pallas_call | solution.py:475
  1.8 2.1 %collective-permute-start = (f32[144,256]{1,0:T(8,128)S(1)}, f32[144,256]{1,0:T(8,128)S(1)}, u32[]{:S(2)}, u32[]{:S(2)}) collective-permute-start(f32[144,256]{1,0:T(8,128)S(1)} %get-tuple-element.14), channel_id=1, source_target_pairs={{0,32},{32,64},{64,96},{96,128},{128,160},{160,192},{192,224},{224... | collective-permute-start | bytes 442376 | tf_op jit(solution)/shard_map/ppermute | solution.py:487
  3.9 2.4 %collective-permute-start.1 = (f32[144,256]{1,0:T(8,128)S(1)}, f32[144,256]{1,0:T(8,128)S(1)}, u32[]{:S(2)}, u32[]{:S(2)}) collective-permute-start(f32[144,256]{1,0:T(8,128)S(1)} %get-tuple-element.15), channel_id=1, source_target_pairs={{0,224},{32,0},{64,32},{96,64},{128,96},{160,128},{192,160},{224,1... | collective-permute-start | bytes 442376 | tf_op jit(solution)/shard_map/ppermute | solution.py:488
  6.3 0.0 copy-done
  6.3 0.0 copy-done.5
  6.3 0.0 copy-done.4
  6.3 0.0 copy-done.3
  6.3 0.0 copy-done.2
  6.3 0.0 copy-done.1
  6.3 0.3 strips.1
  6.6 2.1 %collective-permute-done.bs.ls.ws = f32[144,256]{1,0:T(8,128)S(1)} collective-permute-done((f32[144,256]{1,0:T(8,128)S(1)}, f32[144,256]{1,0:T(8,128)S(1)}, u32[]{:S(2)}, u32[]{:S(2)}) %collective-permute-start) | collective-permute-done | bytes 147488 | tf_op jit(solution)/shard_map/ppermute | solution.py:487
  8.8 0.0 collective-permute-done.1.bn.ln.wn
  8.8 0.1 corners.1
  8.9 3.9 %collective-permute-start.2 = (f32[96,128]{1,0:T(8,128)S(1)}, f32[96,128]{1,0:T(8,128)S(1)}, u32[]{:S(2)}, u32[]{:S(2)}) collective-permute-start(f32[96,128]{1,0:T(8,128)S(1)} %get-tuple-element.18), channel_id=1, source_target_pairs={{0,1},{1,2},{2,3},{3,4},{4,5},{5,6},{6,7},{7,8},{8,9},{9,10},{10,1... | collective-permute-start | bytes 147464 | tf_op jit(solution)/shard_map/ppermute | solution.py:505
  12.8 0.0 collective-permute-start.3
  12.9 0.1 add_convert_fusion.flags
  12.9 1.1 %collective-permute-done.2.sw = f32[96,128]{1,0:T(8,128)S(1)} collective-permute-done((f32[96,128]{1,0:T(8,128)S(1)}, f32[96,128]{1,0:T(8,128)S(1)}, u32[]{:S(2)}, u32[]{:S(2)}) %collective-permute-start.2) | collective-permute-done | bytes 49184 | tf_op jit(solution)/shard_map/ppermute | solution.py:505
  14.0 2.3 %collective-permute-done.3.se = f32[96,128]{1,0:T(8,128)S(1)} collective-permute-done((f32[96,128]{1,0:T(8,128)S(1)}, f32[96,128]{1,0:T(8,128)S(1)}, u32[]{:S(2)}, u32[]{:S(2)}) %collective-permute-start.3) | collective-permute-done | bytes 49184 | tf_op jit(solution)/shard_map/ppermute | solution.py:506
  16.4 1.9 %forward.1 = (f32[8,3,80,128]{3,2,1,0:T(8,128)S(1)}, f32[4,3,80,128]{3,2,1,0:T(8,128)S(1)}, f32[8,80,128]{2,1,0:T(8,128)S(1)}, f32[2,64,256]{2,1,0:T(8,128)S(1)}, f32[256,128]{1,0:T(8,128)S(1)}) custom-call(s32[2]{0:T(128)S(1)} %add_convert_fusion.flags, f32[64,256]{1,0:T(8,128)S(1)} %copy-done.1, f32[64,256]{1,0:T(8,128)S(1)} %copy-done.2, ...), custom_call_target="tpu_custom_call" | custom-call | tf_op jit(solution)/shard_map/forward/pallas_call | solution.py:509
  18.3 27.4 %all_to_all.11 = f32[256,1,128]{2,1,0:T(1,128)S(1)} all-to-all(f32[256,1,128]{2,1,0:T(1,128)S(1)} %bitcast.7), channel_id=1, replica_groups=mesh['lat'=8,'lon'=32] {'lat','lon'}, dimensions={0} | all-to-all | bytes 262144 | tf_op jit(solution)/shard_map/all_to_all | solution.py:529
  45.7 6.9 %adjoint.1 = (f32[8,64,256]{2,1,0:T(8,128)}, f32[8,64,256]{2,1,0:T(8,128)}, f32[8,64,256]{2,1,0:T(8,128)}) custom-call(f32[256,128]{1,0:T(8,128)S(1)} %bitcast.6, f32[8,3,80,128]{3,2,1,0:T(8,128)S(1)} %get-tuple-element.21.vecs, f32[4,3,80,128]{3,2,1,0:T(8,128)S(1)} %get-tuple-element.22.links, f32[2,64,256]{2,1,0:T(8,128)S(1)} %get-tuple-element.23.wet, ...), custom_call_target="tpu_custom_call" | custom-call | tf_op jit(solution)/shard_map/adjoint/pallas_call | solution.py:531
Async XLA Ops:
  0.6 5.7 %copy-start = (f32[8,64,256]{2,1,0:T(8,128)S(1)}, f32[8,64,256]{2,1,0:T(8,128)}, u32[]{:S(2)}) copy-start(f32[8,64,256]{2,1,0:T(8,128)} %w.7) | copy-start | bytes 1572868
  0.6 5.7 %copy-start.5 = (s32[64,256]{1,0:T(8,128)S(1)}, s32[64,256]{1,0:T(8,128)}, u32[]{:S(2)}) copy-start(s32[64,256]{1,0:T(8,128)} %mask.5) | copy-start | bytes 196612
  0.7 5.7 %copy-start.4 = (f32[64,256]{1,0:T(8,128)S(1)}, f32[64,256]{1,0:T(8,128)}, u32[]{:S(2)}) copy-start(f32[64,256]{1,0:T(8,128)} %st.5) | copy-start | bytes 196612
  0.7 5.7 %copy-start.3 = (f32[64,256]{1,0:T(8,128)S(1)}, f32[64,256]{1,0:T(8,128)}, u32[]{:S(2)}) copy-start(f32[64,256]{1,0:T(8,128)} %dn.5) | copy-start | bytes 196612
  0.7 5.7 %copy-start.2 = (f32[64,256]{1,0:T(8,128)S(1)}, f32[64,256]{1,0:T(8,128)}, u32[]{:S(2)}) copy-start(f32[64,256]{1,0:T(8,128)} %de.5) | copy-start | bytes 196612
  0.7 5.7 %copy-start.1 = (f32[64,256]{1,0:T(8,128)S(1)}, f32[64,256]{1,0:T(8,128)}, u32[]{:S(2)}) copy-start(f32[64,256]{1,0:T(8,128)} %f.5) | copy-start | bytes 196612
  1.8 6.9 %collective-permute-start = (f32[144,256]{1,0:T(8,128)S(1)}, f32[144,256]{1,0:T(8,128)S(1)}, u32[]{:S(2)}, u32[]{:S(2)}) collective-permute-start(f32[144,256]{1,0:T(8,128)S(1)} %get-tuple-element.14), channel_id=1, source_target_pairs={{0,32},{32,64},{64,96},{96,128},{128,160},{160,192},{192,224},{224... | collective-permute-start | bytes 442376 | tf_op jit(solution)/shard_map/ppermute | solution.py:487
  3.9 4.8 %collective-permute-start.1 = (f32[144,256]{1,0:T(8,128)S(1)}, f32[144,256]{1,0:T(8,128)S(1)}, u32[]{:S(2)}, u32[]{:S(2)}) collective-permute-start(f32[144,256]{1,0:T(8,128)S(1)} %get-tuple-element.15), channel_id=1, source_target_pairs={{0,224},{32,0},{64,32},{96,64},{128,96},{160,128},{192,160},{224,1... | collective-permute-start | bytes 442376 | tf_op jit(solution)/shard_map/ppermute | solution.py:488
  8.9 5.1 %collective-permute-start.2 = (f32[96,128]{1,0:T(8,128)S(1)}, f32[96,128]{1,0:T(8,128)S(1)}, u32[]{:S(2)}, u32[]{:S(2)}) collective-permute-start(f32[96,128]{1,0:T(8,128)S(1)} %get-tuple-element.18), channel_id=1, source_target_pairs={{0,1},{1,2},{2,3},{3,4},{4,5},{5,6},{6,7},{7,8},{8,9},{9,10},{10,1... | collective-permute-start | bytes 147464 | tf_op jit(solution)/shard_map/ppermute | solution.py:505
  12.8 3.5 %collective-permute-start.3 = (f32[96,128]{1,0:T(8,128)S(1)}, f32[96,128]{1,0:T(8,128)S(1)}, u32[]{:S(2)}, u32[]{:S(2)}) collective-permute-start(f32[96,128]{1,0:T(8,128)S(1)} %get-tuple-element.19), channel_id=1, source_target_pairs={{0,31},{1,0},{2,1},{3,2},{4,3},{5,4},{6,5},{7,6},{8,7},{9,8},{10,9... | collective-permute-start | bytes 147464 | tf_op jit(solution)/shard_map/ppermute | solution.py:506

commit v7 on v6

--- a/solution.py
+++ b/solution.py
@@ -63,8 +63,7 @@
             copies.append((field.at[rows, :], out.at[pl.ds(EDGE * k, EDGE), :]))
         copies.append((mask.at[rows, :], whole_mask.at[side]))
         low = ROWS - 8 if side == 0 else 0
-        for n in range(COSTS):
-            copies.append((w.at[n, pl.ds(low, 8), :], out.at[pl.ds(MSG_W + 8 * n, 8), :]))
+        copies.append((w.at[:, pl.ds(low, 8), :], out.at[pl.ds(MSG_W, 8 * COSTS), :].reshape(COSTS, 8, COLS)))
     copies = [
         pltpu.make_async_copy(src, dst, sems.at[i]) for i, (src, dst) in enumerate(copies)
     ]
@@ -147,8 +146,8 @@
                     values.append(src[EDGE * k + off : EDGE * k + off + 8, lanes])
             values.append(side_tile(pw, pe, k))
             if k == FIELDS - 1 and src is not None:
-                inside = flags[0 if rb < 2 else 1] > 0
-                values = [jnp.where(inside, value, 0.0) for value in values]
+                inside = flags[0 if rb < 2 else 1]
+                values = [inside * value for value in values]
             for t in tiles:
                 raw[k, t, at : at + 8, :] = values[t]
         if 1 <= rb < 11:
@@ -325,6 +324,23 @@
             rows[0], jnp.ones((8, LANES), F32), (((0,), (0,)), ((), ())),
             precision=HIGH, preferred_element_type=F32,
         )
+        for rb in range(1, 10):
+            here = slice(8 * rb, 8 * rb + 8)
+            above = slice(8 * rb + 1, 8 * rb + 9)
+            to = slice(8 * rb - 8, 8 * rb)
+            for j in range(ITERS):
+                v = [vecs[j, t, here, :] for t in tiles]
+                if j < ITERS - 1:
+                    for t in tiles:
+                        later = vecs[j + 1, t, here, :]
+                        if j > 0:
+                            later = 0.5 * (later + vecs[j - 1, t, here, :])
+                        lag[j, t, here, :] = later - v[t]
+                if rb < 9:
+                    ve = east_of(v)
+                    for t in range(2):
+                        slope[0, j, t, to, :] = v[t] - ve[t]
+                        slope[1, j, t, to, :] = v[t] - vecs[j, t, above, :]
         c, weights = small_solve(total)
         for j in range(ITERS):
             lam[8 * j : 8 * j + 8, :] = weights[j]
@@ -337,28 +353,12 @@
             for t in tiles:
                 v = [vecs[k, t, here, :] for k in range(ITERS + 1)]
                 rs[t, here, :] = v[0] + v[0] - mixed(c2, v)
-                if rb >= 1:
-                    lag[0, t, here, :] = v[1] - v[0]
-                    for j in range(1, ITERS - 1):
-                        lag[j, t, here, :] = 0.5 * (v[j + 1] + v[j - 1]) - v[j]
-        for rb in range(1, 9):
-            here = slice(8 * rb, 8 * rb + 8)
-            above = slice(8 * rb + 1, 8 * rb + 9)
-            to = slice(8 * rb - 8, 8 * rb)
-            sums = [[None, None], [None, None]]
-            for j in range(ITERS):
-                v = [vecs[j, t, here, :] for t in tiles]
-                ve = east_of(v)
-                for t in range(2):
-                    for d, near in enumerate((ve[t], vecs[j, t, above, :])):
-                        step = v[t] - near
-                        if j < ITERS - 1:
-                            slope[d, j, t, to, :] = step
-                        term = c[j] * step
-                        sums[d][t] = term if j == 0 else sums[d][t] + term
+        for rb in range(ROWS // 8):
+            to = slice(8 * rb, 8 * rb + 8)
             for d in range(2):
                 for t in range(2):
-                    slope[d, ITERS - 1, t, to, :] = sums[d][t]
+                    steps = [slope[d, j, t, to, :] for j in range(ITERS)]
+                    slope[d, ITERS - 1, t, to, :] = mixed(c, steps)
 
     pair = range(PAIR)
     spread = lambda ref, k, h: jnp.broadcast_to(ref[pl.ds(8 * k + PAIR * n + h, 1), :], (8, LANES))
@@ -479,7 +479,7 @@
         out_shape=(struct(MSG, COLS),) * 2,
         scratch_shapes=[
             pltpu.VMEM((2, EDGE, COLS), jnp.int32),
-            pltpu.SemaphoreType.DMA((2 * (FIELDS + COSTS),)),
+            pltpu.SemaphoreType.DMA((2 * (FIELDS + 1),)),
         ],
         compiler_params=small,
         name="bands",
@@ -505,10 +505,11 @@
     side_w = lax.ppermute(to_east, "lon", ring("lon", 1))
     side_e = lax.ppermute(to_west, "lon", ring("lon", -1))
     row = lax.axis_index("lat")
-    flags = jnp.stack([row > 0, row < lats - 1]).astype(jnp.int32)
+    flags = jnp.stack([row > 0, row < lats - 1, row > 0, row > 0]).astype(F32)
+    flags = jnp.broadcast_to(flags[:, None, None], (4, 8, LANES))
     vecs, links, wside, wet, dots = pl.pallas_call(
         forward_kernel,
-        in_specs=[pl.BlockSpec(memory_space=pltpu.SMEM)] + [whole()] * 10,
+        in_specs=[whole()] * 11,
         out_specs=[whole()] * 5,
         out_shape=(
             struct(ITERS + 2, TILES, FRAME, LANES), struct(4, TILES, FRAME, LANES),

time: 52.7 us -> 52.2 us (level)
  no operation moved by 1% of the time
where the time goes in v7:
time: 52.2 us; the launch traced here: 52.1 us
  blocking collectives  27.4 us (52%)
  Pallas kernels  9.78 us (19%)
  starting transfers between devices  8.43 us (16%)
  waiting for transfers between devices  5.56 us (11%)
  between operations  0.74 us (1%)
    all_to_all x1, blocking collectives, body(): all_dots = lax.all_to_all(dots, ('lat', 'lon'), 0, 0, tiled=True)  27.4 us
    pallas_call x1, Pallas kernels, body(): pl.pallas_call(adjoint_kernel, grid=(COSTS // PAIR,), in_specs=[whole(),...  6.82 us
    ppermute x1, starting transfers between devices, body(): side_w = lax.ppermute(to_east, 'lon', ring('lon', 1))  3.95 us
    ppermute x1, starting transfers between devices, body(): band_n = lax.ppermute(to_south, 'lat', ring('lat', -1))  2.37 us
    ppermute x1, waiting for transfers between devices, body(): side_e = lax.ppermute(to_west, 'lon', ring('lon', -1))  2.34 us
    ppermute x1, waiting for transfers between devices, body(): band_s = lax.ppermute(to_north, 'lat', ring('lat', 1))  2.12 us
    ppermute x1, starting transfers between devices, body(): band_s = lax.ppermute(to_north, 'lat', ring('lat', 1))  2.11 us
    pallas_call x1, Pallas kernels, body(): pl.pallas_call(forward_kernel, in_specs=[whole()] * 11, out_specs=[whole(...  1.44 us
  transfers between devices with their start and end apart: 4, of which 3 were waited for; matrix products, arithmetic and copies ran while one was open for 0% of the time, Pallas kernels for 1%

profile of v7, /device:TPU:1, one launch (start us, length us, event | category | flops | bytes accessed | tf_op | source)
XLA Modules:
  0.0 52.1 jit_solution(144989950091828138)
XLA Ops:
  0.6 0.0 copy-start
  0.6 0.0 copy-start.5
  0.7 0.0 copy-start.4
  0.7 0.0 copy-start.3
  0.7 0.0 copy-start.2
  0.7 0.0 copy-start.1
  0.7 1.1 %bands.1 = (f32[144,256]{1,0:T(8,128)S(1)}, f32[144,256]{1,0:T(8,128)S(1)}) custom-call(f32[64,256]{1,0:T(8,128)} %f.5, f32[64,256]{1,0:T(8,128)} %de.5, f32[64,256]{1,0:T(8,128)} %dn.5, f32[64,256]{1,0:T(8,128)} %st.5, s32[64,256]{1,0:T(8,128)} %mask.5, f32[8,64,256]{2,1,0:T(8,128)} %w.7), custom_call_target="tpu_custom_call" | custom-call | tf_op jit(solution)/shard_map/bands/pallas_call | solution.py:475
  1.8 2.1 %collective-permute-start = (f32[144,256]{1,0:T(8,128)S(1)}, f32[144,256]{1,0:T(8,128)S(1)}, u32[]{:S(2)}, u32[]{:S(2)}) collective-permute-start(f32[144,256]{1,0:T(8,128)S(1)} %get-tuple-element.14), channel_id=1, source_target_pairs={{0,32},{32,64},{64,96},{96,128},{128,160},{160,192},{192,224},{224... | collective-permute-start | bytes 442376 | tf_op jit(solution)/shard_map/ppermute | solution.py:487
  3.9 2.4 %collective-permute-start.1 = (f32[144,256]{1,0:T(8,128)S(1)}, f32[144,256]{1,0:T(8,128)S(1)}, u32[]{:S(2)}, u32[]{:S(2)}) collective-permute-start(f32[144,256]{1,0:T(8,128)S(1)} %get-tuple-element.15), channel_id=1, source_target_pairs={{0,224},{32,0},{64,32},{96,64},{128,96},{160,128},{192,160},{224,1... | collective-permute-start | bytes 442376 | tf_op jit(solution)/shard_map/ppermute | solution.py:488
  6.3 0.0 copy-done
  6.3 0.0 copy-done.5
  6.3 0.0 copy-done.4
  6.3 0.0 copy-done.3
  6.3 0.0 copy-done.2
  6.3 0.0 copy-done.1
  6.3 0.3 strips.1
  6.6 2.1 %collective-permute-done.bs.ls.ws = f32[144,256]{1,0:T(8,128)S(1)} collective-permute-done((f32[144,256]{1,0:T(8,128)S(1)}, f32[144,256]{1,0:T(8,128)S(1)}, u32[]{:S(2)}, u32[]{:S(2)}) %collective-permute-start) | collective-permute-done | bytes 147488 | tf_op jit(solution)/shard_map/ppermute | solution.py:487
  8.7 0.0 collective-permute-done.1.bn.ln.wn
  8.7 0.1 corners.1
  8.9 3.9 %collective-permute-start.2 = (f32[96,128]{1,0:T(8,128)S(1)}, f32[96,128]{1,0:T(8,128)S(1)}, u32[]{:S(2)}, u32[]{:S(2)}) collective-permute-start(f32[96,128]{1,0:T(8,128)S(1)} %get-tuple-element.18), channel_id=1, source_target_pairs={{0,1},{1,2},{2,3},{3,4},{4,5},{5,6},{6,7},{7,8},{8,9},{9,10},{10,1... | collective-permute-start | bytes 147464 | tf_op jit(solution)/shard_map/ppermute | solution.py:505
  12.8 0.0 collective-permute-start.3
  12.8 0.1 add_convert_fusion
  12.9 1.1 %collective-permute-done.2.sw = f32[96,128]{1,0:T(8,128)S(1)} collective-permute-done((f32[96,128]{1,0:T(8,128)S(1)}, f32[96,128]{1,0:T(8,128)S(1)}, u32[]{:S(2)}, u32[]{:S(2)}) %collective-permute-start.2) | collective-permute-done | bytes 49184 | tf_op jit(solution)/shard_map/ppermute | solution.py:505
  14.0 2.3 %collective-permute-done.3.se = f32[96,128]{1,0:T(8,128)S(1)} collective-permute-done((f32[96,128]{1,0:T(8,128)S(1)}, f32[96,128]{1,0:T(8,128)S(1)}, u32[]{:S(2)}, u32[]{:S(2)}) %collective-permute-start.3) | collective-permute-done | bytes 49184 | tf_op jit(solution)/shard_map/ppermute | solution.py:506
  16.3 0.1 broadcast_in_dim.2.flags
  16.4 1.4 %forward.1 = (f32[8,3,80,128]{3,2,1,0:T(8,128)S(1)}, f32[4,3,80,128]{3,2,1,0:T(8,128)S(1)}, f32[8,80,128]{2,1,0:T(8,128)S(1)}, f32[2,64,256]{2,1,0:T(8,128)S(1)}, f32[256,128]{1,0:T(8,128)S(1)}) custom-call(f32[4,8,128]{2,1,0:T(8,128)S(1)} %broadcast_in_dim.2.flags, f32[64,256]{1,0:T(8,128)S(1)} %copy-done.1, f32[64,256]{1,0:T(8,128)S(1)} %copy-done.2, ...), custom_call_target="tpu_custom_call" | custom-call | tf_op jit(solution)/shard_map/forward/pallas_call | solution.py:510
  17.9 27.4 %all_to_all.11 = f32[256,1,128]{2,1,0:T(1,128)S(1)} all-to-all(f32[256,1,128]{2,1,0:T(1,128)S(1)} %bitcast.7), channel_id=1, replica_groups=mesh['lat'=8,'lon'=32] {'lat','lon'}, dimensions={0} | all-to-all | bytes 262144 | tf_op jit(solution)/shard_map/all_to_all | solution.py:530
  45.3 6.8 %adjoint.1 = (f32[8,64,256]{2,1,0:T(8,128)}, f32[8,64,256]{2,1,0:T(8,128)}, f32[8,64,256]{2,1,0:T(8,128)}) custom-call(f32[256,128]{1,0:T(8,128)S(1)} %bitcast.6, f32[8,3,80,128]{3,2,1,0:T(8,128)S(1)} %get-tuple-element.21.vecs, f32[4,3,80,128]{3,2,1,0:T(8,128)S(1)} %get-tuple-element.22.links, f32[2,64,256]{2,1,0:T(8,128)S(1)} %get-tuple-element.23.wet, ...), custom_call_target="tpu_custom_call" | custom-call | tf_op jit(solution)/shard_map/adjoint/pallas_call | solution.py:532
Async XLA Ops:
  0.6 5.7 %copy-start = (f32[8,64,256]{2,1,0:T(8,128)S(1)}, f32[8,64,256]{2,1,0:T(8,128)}, u32[]{:S(2)}) copy-start(f32[8,64,256]{2,1,0:T(8,128)} %w.7) | copy-start | bytes 1572868
  0.6 5.7 %copy-start.5 = (s32[64,256]{1,0:T(8,128)S(1)}, s32[64,256]{1,0:T(8,128)}, u32[]{:S(2)}) copy-start(s32[64,256]{1,0:T(8,128)} %mask.5) | copy-start | bytes 196612
  0.7 5.7 %copy-start.4 = (f32[64,256]{1,0:T(8,128)S(1)}, f32[64,256]{1,0:T(8,128)}, u32[]{:S(2)}) copy-start(f32[64,256]{1,0:T(8,128)} %st.5) | copy-start | bytes 196612
  0.7 5.6 %copy-start.3 = (f32[64,256]{1,0:T(8,128)S(1)}, f32[64,256]{1,0:T(8,128)}, u32[]{:S(2)}) copy-start(f32[64,256]{1,0:T(8,128)} %dn.5) | copy-start | bytes 196612
  0.7 5.6 %copy-start.2 = (f32[64,256]{1,0:T(8,128)S(1)}, f32[64,256]{1,0:T(8,128)}, u32[]{:S(2)}) copy-start(f32[64,256]{1,0:T(8,128)} %de.5) | copy-start | bytes 196612
  0.7 5.6 %copy-start.1 = (f32[64,256]{1,0:T(8,128)S(1)}, f32[64,256]{1,0:T(8,128)}, u32[]{:S(2)}) copy-start(f32[64,256]{1,0:T(8,128)} %f.5) | copy-start | bytes 196612
  1.8 6.9 %collective-permute-start = (f32[144,256]{1,0:T(8,128)S(1)}, f32[144,256]{1,0:T(8,128)S(1)}, u32[]{:S(2)}, u32[]{:S(2)}) collective-permute-start(f32[144,256]{1,0:T(8,128)S(1)} %get-tuple-element.14), channel_id=1, source_target_pairs={{0,32},{32,64},{64,96},{96,128},{128,160},{160,192},{192,224},{224... | collective-permute-start | bytes 442376 | tf_op jit(solution)/shard_map/ppermute | solution.py:487
  3.9 4.8 %collective-permute-start.1 = (f32[144,256]{1,0:T(8,128)S(1)}, f32[144,256]{1,0:T(8,128)S(1)}, u32[]{:S(2)}, u32[]{:S(2)}) collective-permute-start(f32[144,256]{1,0:T(8,128)S(1)} %get-tuple-element.15), channel_id=1, source_target_pairs={{0,224},{32,0},{64,32},{96,64},{128,96},{160,128},{192,160},{224,1... | collective-permute-start | bytes 442376 | tf_op jit(solution)/shard_map/ppermute | solution.py:488
  8.9 5.1 %collective-permute-start.2 = (f32[96,128]{1,0:T(8,128)S(1)}, f32[96,128]{1,0:T(8,128)S(1)}, u32[]{:S(2)}, u32[]{:S(2)}) collective-permute-start(f32[96,128]{1,0:T(8,128)S(1)} %get-tuple-element.18), channel_id=1, source_target_pairs={{0,1},{1,2},{2,3},{3,4},{4,5},{5,6},{6,7},{7,8},{8,9},{9,10},{10,1... | collective-permute-start | bytes 147464 | tf_op jit(solution)/shard_map/ppermute | solution.py:505
  12.8 3.5 %collective-permute-start.3 = (f32[96,128]{1,0:T(8,128)S(1)}, f32[96,128]{1,0:T(8,128)S(1)}, u32[]{:S(2)}, u32[]{:S(2)}) collective-permute-start(f32[96,128]{1,0:T(8,128)S(1)} %get-tuple-element.19), channel_id=1, source_target_pairs={{0,31},{1,0},{2,1},{3,2},{4,3},{5,4},{6,5},{7,6},{8,7},{9,8},{10,9... | collective-permute-start | bytes 147464 | tf_op jit(solution)/shard_map/ppermute | solution.py:506

commit v8 on v7

--- a/solution.py
+++ b/solution.py
@@ -189,7 +189,7 @@
                 wet[0, to, lanes] = me[t]
                 diag[to, lanes] = total
     for j in range(ITERS):
-        for rb in blocks:
+        for rb in blocks if j < 3 else blocks[1:-1]:
             here = slice(8 + 8 * rb, 16 + 8 * rb)
             above = slice(9 + 8 * rb, 17 + 8 * rb)
             below = slice(7 + 8 * rb, 15 + 8 * rb)

time: 52.2 us -> 52.2 us (level)
  no operation moved by 1% of the time
where the time goes in v8:
time: 52.2 us; the launch traced here: 52 us
  blocking collectives  27.4 us (52%)
  Pallas kernels  9.74 us (19%)
  starting transfers between devices  8.43 us (16%)
  waiting for transfers between devices  5.56 us (11%)
  between operations  0.74 us (1%)
    all_to_all x1, blocking collectives, body(): all_dots = lax.all_to_all(dots, ('lat', 'lon'), 0, 0, tiled=True)  27.4 us
    pallas_call x1, Pallas kernels, body(): pl.pallas_call(adjoint_kernel, grid=(COSTS // PAIR,), in_specs=[whole(),...  6.82 us
    ppermute x1, starting transfers between devices, body(): side_w = lax.ppermute(to_east, 'lon', ring('lon', 1))  3.95 us
    ppermute x1, starting transfers between devices, body(): band_n = lax.ppermute(to_south, 'lat', ring('lat', -1))  2.37 us
    ppermute x1, waiting for transfers between devices, body(): side_e = lax.ppermute(to_west, 'lon', ring('lon', -1))  2.34 us
    ppermute x1, waiting for transfers between devices, body(): band_s = lax.ppermute(to_north, 'lat', ring('lat', 1))  2.12 us
    ppermute x1, starting transfers between devices, body(): band_s = lax.ppermute(to_north, 'lat', ring('lat', 1))  2.11 us
    pallas_call x1, Pallas kernels, body(): pl.pallas_call(forward_kernel, in_specs=[whole()] * 11, out_specs=[whole(...  1.4 us
  transfers between devices with their start and end apart: 4, of which 3 were waited for; matrix products, arithmetic and copies ran while one was open for 0% of the time, Pallas kernels for 1%

profile of v8, /device:TPU:1, one launch (start us, length us, event | category | flops | bytes accessed | tf_op | source)
XLA Modules:
  0.0 52.0 jit_solution(4436518529958250134)
XLA Ops:
  0.6 0.0 copy-start
  0.6 0.0 copy-start.5
  0.7 0.0 copy-start.4
  0.7 0.0 copy-start.3
  0.7 0.0 copy-start.2
  0.7 0.0 copy-start.1
  0.7 1.1 %bands.1 = (f32[144,256]{1,0:T(8,128)S(1)}, f32[144,256]{1,0:T(8,128)S(1)}) custom-call(f32[64,256]{1,0:T(8,128)} %f.5, f32[64,256]{1,0:T(8,128)} %de.5, f32[64,256]{1,0:T(8,128)} %dn.5, f32[64,256]{1,0:T(8,128)} %st.5, s32[64,256]{1,0:T(8,128)} %mask.5, f32[8,64,256]{2,1,0:T(8,128)} %w.7), custom_call_target="tpu_custom_call" | custom-call | tf_op jit(solution)/shard_map/bands/pallas_call | solution.py:475
  1.8 2.1 %collective-permute-start = (f32[144,256]{1,0:T(8,128)S(1)}, f32[144,256]{1,0:T(8,128)S(1)}, u32[]{:S(2)}, u32[]{:S(2)}) collective-permute-start(f32[144,256]{1,0:T(8,128)S(1)} %get-tuple-element.14), channel_id=1, source_target_pairs={{0,32},{32,64},{64,96},{96,128},{128,160},{160,192},{192,224},{224... | collective-permute-start | bytes 442376 | tf_op jit(solution)/shard_map/ppermute | solution.py:487
  3.9 2.4 %collective-permute-start.1 = (f32[144,256]{1,0:T(8,128)S(1)}, f32[144,256]{1,0:T(8,128)S(1)}, u32[]{:S(2)}, u32[]{:S(2)}) collective-permute-start(f32[144,256]{1,0:T(8,128)S(1)} %get-tuple-element.15), channel_id=1, source_target_pairs={{0,224},{32,0},{64,32},{96,64},{128,96},{160,128},{192,160},{224,1... | collective-permute-start | bytes 442376 | tf_op jit(solution)/shard_map/ppermute | solution.py:488
  6.3 0.0 copy-done
  6.3 0.0 copy-done.5
  6.3 0.0 copy-done.4
  6.3 0.0 copy-done.3
  6.3 0.0 copy-done.2
  6.3 0.0 copy-done.1
  6.3 0.3 strips.1
  6.6 2.1 %collective-permute-done.bs.ls.ws = f32[144,256]{1,0:T(8,128)S(1)} collective-permute-done((f32[144,256]{1,0:T(8,128)S(1)}, f32[144,256]{1,0:T(8,128)S(1)}, u32[]{:S(2)}, u32[]{:S(2)}) %collective-permute-start) | collective-permute-done | bytes 147488 | tf_op jit(solution)/shard_map/ppermute | solution.py:487
  8.7 0.0 collective-permute-done.1.bn.ln.wn
  8.7 0.1 corners.1
  8.9 3.9 %collective-permute-start.2 = (f32[96,128]{1,0:T(8,128)S(1)}, f32[96,128]{1,0:T(8,128)S(1)}, u32[]{:S(2)}, u32[]{:S(2)}) collective-permute-start(f32[96,128]{1,0:T(8,128)S(1)} %get-tuple-element.18), channel_id=1, source_target_pairs={{0,1},{1,2},{2,3},{3,4},{4,5},{5,6},{6,7},{7,8},{8,9},{9,10},{10,1... | collective-permute-start | bytes 147464 | tf_op jit(solution)/shard_map/ppermute | solution.py:505
  12.8 0.0 collective-permute-start.3
  12.8 0.1 add_convert_fusion
  12.9 1.1 %collective-permute-done.2.sw = f32[96,128]{1,0:T(8,128)S(1)} collective-permute-done((f32[96,128]{1,0:T(8,128)S(1)}, f32[96,128]{1,0:T(8,128)S(1)}, u32[]{:S(2)}, u32[]{:S(2)}) %collective-permute-start.2) | collective-permute-done | bytes 49184 | tf_op jit(solution)/shard_map/ppermute | solution.py:505
  14.0 2.3 %collective-permute-done.3.se = f32[96,128]{1,0:T(8,128)S(1)} collective-permute-done((f32[96,128]{1,0:T(8,128)S(1)}, f32[96,128]{1,0:T(8,128)S(1)}, u32[]{:S(2)}, u32[]{:S(2)}) %collective-permute-start.3) | collective-permute-done | bytes 49184 | tf_op jit(solution)/shard_map/ppermute | solution.py:506
  16.3 0.1 broadcast_in_dim.2.flags
  16.4 1.4 %forward.1 = (f32[8,3,80,128]{3,2,1,0:T(8,128)S(1)}, f32[4,3,80,128]{3,2,1,0:T(8,128)S(1)}, f32[8,80,128]{2,1,0:T(8,128)S(1)}, f32[2,64,256]{2,1,0:T(8,128)S(1)}, f32[256,128]{1,0:T(8,128)S(1)}) custom-call(f32[4,8,128]{2,1,0:T(8,128)S(1)} %broadcast_in_dim.2.flags, f32[64,256]{1,0:T(8,128)S(1)} %copy-done.1, f32[64,256]{1,0:T(8,128)S(1)} %copy-done.2, ...), custom_call_target="tpu_custom_call" | custom-call | tf_op jit(solution)/shard_map/forward/pallas_call | solution.py:510
  17.8 27.4 %all_to_all.11 = f32[256,1,128]{2,1,0:T(1,128)S(1)} all-to-all(f32[256,1,128]{2,1,0:T(1,128)S(1)} %bitcast.7), channel_id=1, replica_groups=mesh['lat'=8,'lon'=32] {'lat','lon'}, dimensions={0} | all-to-all | bytes 262144 | tf_op jit(solution)/shard_map/all_to_all | solution.py:530
  45.2 6.8 %adjoint.1 = (f32[8,64,256]{2,1,0:T(8,128)}, f32[8,64,256]{2,1,0:T(8,128)}, f32[8,64,256]{2,1,0:T(8,128)}) custom-call(f32[256,128]{1,0:T(8,128)S(1)} %bitcast.6, f32[8,3,80,128]{3,2,1,0:T(8,128)S(1)} %get-tuple-element.21.vecs, f32[4,3,80,128]{3,2,1,0:T(8,128)S(1)} %get-tuple-element.22.links, f32[2,64,256]{2,1,0:T(8,128)S(1)} %get-tuple-element.23.wet, ...), custom_call_target="tpu_custom_call" | custom-call | tf_op jit(solution)/shard_map/adjoint/pallas_call | solution.py:532
Async XLA Ops:
  0.6 5.7 %copy-start = (f32[8,64,256]{2,1,0:T(8,128)S(1)}, f32[8,64,256]{2,1,0:T(8,128)}, u32[]{:S(2)}) copy-start(f32[8,64,256]{2,1,0:T(8,128)} %w.7) | copy-start | bytes 1572868
  0.6 5.7 %copy-start.5 = (s32[64,256]{1,0:T(8,128)S(1)}, s32[64,256]{1,0:T(8,128)}, u32[]{:S(2)}) copy-start(s32[64,256]{1,0:T(8,128)} %mask.5) | copy-start | bytes 196612
  0.7 5.7 %copy-start.4 = (f32[64,256]{1,0:T(8,128)S(1)}, f32[64,256]{1,0:T(8,128)}, u32[]{:S(2)}) copy-start(f32[64,256]{1,0:T(8,128)} %st.5) | copy-start | bytes 196612
  0.7 5.6 %copy-start.3 = (f32[64,256]{1,0:T(8,128)S(1)}, f32[64,256]{1,0:T(8,128)}, u32[]{:S(2)}) copy-start(f32[64,256]{1,0:T(8,128)} %dn.5) | copy-start | bytes 196612
  0.7 5.6 %copy-start.2 = (f32[64,256]{1,0:T(8,128)S(1)}, f32[64,256]{1,0:T(8,128)}, u32[]{:S(2)}) copy-start(f32[64,256]{1,0:T(8,128)} %de.5) | copy-start | bytes 196612
  0.7 5.6 %copy-start.1 = (f32[64,256]{1,0:T(8,128)S(1)}, f32[64,256]{1,0:T(8,128)}, u32[]{:S(2)}) copy-start(f32[64,256]{1,0:T(8,128)} %f.5) | copy-start | bytes 196612
  1.8 6.9 %collective-permute-start = (f32[144,256]{1,0:T(8,128)S(1)}, f32[144,256]{1,0:T(8,128)S(1)}, u32[]{:S(2)}, u32[]{:S(2)}) collective-permute-start(f32[144,256]{1,0:T(8,128)S(1)} %get-tuple-element.14), channel_id=1, source_target_pairs={{0,32},{32,64},{64,96},{96,128},{128,160},{160,192},{192,224},{224... | collective-permute-start | bytes 442376 | tf_op jit(solution)/shard_map/ppermute | solution.py:487
  3.9 4.8 %collective-permute-start.1 = (f32[144,256]{1,0:T(8,128)S(1)}, f32[144,256]{1,0:T(8,128)S(1)}, u32[]{:S(2)}, u32[]{:S(2)}) collective-permute-start(f32[144,256]{1,0:T(8,128)S(1)} %get-tuple-element.15), channel_id=1, source_target_pairs={{0,224},{32,0},{64,32},{96,64},{128,96},{160,128},{192,160},{224,1... | collective-permute-start | bytes 442376 | tf_op jit(solution)/shard_map/ppermute | solution.py:488
  8.9 5.1 %collective-permute-start.2 = (f32[96,128]{1,0:T(8,128)S(1)}, f32[96,128]{1,0:T(8,128)S(1)}, u32[]{:S(2)}, u32[]{:S(2)}) collective-permute-start(f32[96,128]{1,0:T(8,128)S(1)} %get-tuple-element.18), channel_id=1, source_target_pairs={{0,1},{1,2},{2,3},{3,4},{4,5},{5,6},{6,7},{7,8},{8,9},{9,10},{10,1... | collective-permute-start | bytes 147464 | tf_op jit(solution)/shard_map/ppermute | solution.py:505
  12.8 3.5 %collective-permute-start.3 = (f32[96,128]{1,0:T(8,128)S(1)}, f32[96,128]{1,0:T(8,128)S(1)}, u32[]{:S(2)}, u32[]{:S(2)}) collective-permute-start(f32[96,128]{1,0:T(8,128)S(1)} %get-tuple-element.19), channel_id=1, source_target_pairs={{0,31},{1,0},{2,1},{3,2},{4,3},{5,4},{6,5},{7,6},{8,7},{9,8},{10,9... | collective-permute-start | bytes 147464 | tf_op jit(solution)/shard_map/ppermute | solution.py:506

commit v9 on v8

--- a/solution.py
+++ b/solution.py
@@ -320,10 +320,15 @@
         rows = [all_dots[at : at + 8, :] for at in range(0, all_dots.shape[0], 8)]
         while len(rows) > 1:
             rows = [a + b for a, b in zip(rows[::2], rows[1::2])]
-        total = lax.dot_general(
-            rows[0], jnp.ones((8, LANES), F32), (((0,), (0,)), ((), ())),
-            precision=HIGH, preferred_element_type=F32,
-        )
+        total, rest = None, rows[0]
+        for _ in range(3):
+            piece = rest.astype(jnp.bfloat16)
+            rest = rest - piece.astype(F32)
+            term = lax.dot_general(
+                piece, jnp.ones((8, LANES), jnp.bfloat16), (((0,), (0,)), ((), ())),
+                preferred_element_type=F32,
+            )
+            total = term if total is None else total + term
         for rb in range(1, 10):
             here = slice(8 * rb, 8 * rb + 8)
             above = slice(8 * rb + 1, 8 * rb + 9)

time: 52.2 us -> 52.1 us (level)
  no operation moved by 1% of the time
where the time goes in v9:
time: 52.1 us; the launch traced here: 52 us
  blocking collectives  27.4 us (53%)
  Pallas kernels  9.7 us (19%)
  starting transfers between devices  8.43 us (16%)
  waiting for transfers between devices  5.56 us (11%)
  between operations  0.74 us (1%)
    all_to_all x1, blocking collectives, body(): all_dots = lax.all_to_all(dots, ('lat', 'lon'), 0, 0, tiled=True)  27.4 us
    pallas_call x1, Pallas kernels, body(): pl.pallas_call(adjoint_kernel, grid=(COSTS // PAIR,), in_specs=[whole(),...  6.78 us
    ppermute x1, starting transfers between devices, body(): side_w = lax.ppermute(to_east, 'lon', ring('lon', 1))  3.95 us
    ppermute x1, starting transfers between devices, body(): band_n = lax.ppermute(to_south, 'lat', ring('lat', -1))  2.37 us
    ppermute x1, waiting for transfers between devices, body(): side_e = lax.ppermute(to_west, 'lon', ring('lon', -1))  2.34 us
    ppermute x1, waiting for transfers between devices, body(): band_s = lax.ppermute(to_north, 'lat', ring('lat', 1))  2.12 us
    ppermute x1, starting transfers between devices, body(): band_s = lax.ppermute(to_north, 'lat', ring('lat', 1))  2.11 us
    pallas_call x1, Pallas kernels, body(): pl.pallas_call(forward_kernel, in_specs=[whole()] * 11, out_specs=[whole(...  1.4 us
  transfers between devices with their start and end apart: 4, of which 3 were waited for; matrix products, arithmetic and copies ran while one was open for 0% of the time, Pallas kernels for 1%

profile of v9, /device:TPU:1, one launch (start us, length us, event | category | flops | bytes accessed | tf_op | source)
XLA Modules:
  0.0 52.0 jit_solution(16327483960059258511)
XLA Ops:
  0.6 0.0 copy-start
  0.6 0.0 copy-start.5
  0.7 0.0 copy-start.4
  0.7 0.0 copy-start.3
  0.7 0.0 copy-start.2
  0.7 0.0 copy-start.1
  0.7 1.1 %bands.1 = (f32[144,256]{1,0:T(8,128)S(1)}, f32[144,256]{1,0:T(8,128)S(1)}) custom-call(f32[64,256]{1,0:T(8,128)} %f.5, f32[64,256]{1,0:T(8,128)} %de.5, f32[64,256]{1,0:T(8,128)} %dn.5, f32[64,256]{1,0:T(8,128)} %st.5, s32[64,256]{1,0:T(8,128)} %mask.5, f32[8,64,256]{2,1,0:T(8,128)} %w.7), custom_call_target="tpu_custom_call" | custom-call | tf_op jit(solution)/shard_map/bands/pallas_call | solution.py:480
  1.8 2.1 %collective-permute-start = (f32[144,256]{1,0:T(8,128)S(1)}, f32[144,256]{1,0:T(8,128)S(1)}, u32[]{:S(2)}, u32[]{:S(2)}) collective-permute-start(f32[144,256]{1,0:T(8,128)S(1)} %get-tuple-element.14), channel_id=1, source_target_pairs={{0,32},{32,64},{64,96},{96,128},{128,160},{160,192},{192,224},{224... | collective-permute-start | bytes 442376 | tf_op jit(solution)/shard_map/ppermute | solution.py:492
  3.9 2.4 %collective-permute-start.1 = (f32[144,256]{1,0:T(8,128)S(1)}, f32[144,256]{1,0:T(8,128)S(1)}, u32[]{:S(2)}, u32[]{:S(2)}) collective-permute-start(f32[144,256]{1,0:T(8,128)S(1)} %get-tuple-element.15), channel_id=1, source_target_pairs={{0,224},{32,0},{64,32},{96,64},{128,96},{160,128},{192,160},{224,1... | collective-permute-start | bytes 442376 | tf_op jit(solution)/shard_map/ppermute | solution.py:493
  6.3 0.0 copy-done
  6.3 0.0 copy-done.5
  6.3 0.0 copy-done.4
  6.3 0.0 copy-done.3
  6.3 0.0 copy-done.2
  6.3 0.0 copy-done.1
  6.3 0.3 strips.1
  6.6 2.1 %collective-permute-done.bs.ls.ws = f32[144,256]{1,0:T(8,128)S(1)} collective-permute-done((f32[144,256]{1,0:T(8,128)S(1)}, f32[144,256]{1,0:T(8,128)S(1)}, u32[]{:S(2)}, u32[]{:S(2)}) %collective-permute-start) | collective-permute-done | bytes 147488 | tf_op jit(solution)/shard_map/ppermute | solution.py:492
  8.7 0.0 collective-permute-done.1.bn.ln.wn
  8.7 0.1 corners.1
  8.9 3.9 %collective-permute-start.2 = (f32[96,128]{1,0:T(8,128)S(1)}, f32[96,128]{1,0:T(8,128)S(1)}, u32[]{:S(2)}, u32[]{:S(2)}) collective-permute-start(f32[96,128]{1,0:T(8,128)S(1)} %get-tuple-element.18), channel_id=1, source_target_pairs={{0,1},{1,2},{2,3},{3,4},{4,5},{5,6},{6,7},{7,8},{8,9},{9,10},{10,1... | collective-permute-start | bytes 147464 | tf_op jit(solution)/shard_map/ppermute | solution.py:510
  12.8 0.0 collective-permute-start.3
  12.8 0.1 add_convert_fusion
  12.9 1.1 %collective-permute-done.2.sw = f32[96,128]{1,0:T(8,128)S(1)} collective-permute-done((f32[96,128]{1,0:T(8,128)S(1)}, f32[96,128]{1,0:T(8,128)S(1)}, u32[]{:S(2)}, u32[]{:S(2)}) %collective-permute-start.2) | collective-permute-done | bytes 49184 | tf_op jit(solution)/shard_map/ppermute | solution.py:510
  14.0 2.3 %collective-permute-done.3.se = f32[96,128]{1,0:T(8,128)S(1)} collective-permute-done((f32[96,128]{1,0:T(8,128)S(1)}, f32[96,128]{1,0:T(8,128)S(1)}, u32[]{:S(2)}, u32[]{:S(2)}) %collective-permute-start.3) | collective-permute-done | bytes 49184 | tf_op jit(solution)/shard_map/ppermute | solution.py:511
  16.3 0.1 broadcast_in_dim.2.flags
  16.4 1.4 %forward.1 = (f32[8,3,80,128]{3,2,1,0:T(8,128)S(1)}, f32[4,3,80,128]{3,2,1,0:T(8,128)S(1)}, f32[8,80,128]{2,1,0:T(8,128)S(1)}, f32[2,64,256]{2,1,0:T(8,128)S(1)}, f32[256,128]{1,0:T(8,128)S(1)}) custom-call(f32[4,8,128]{2,1,0:T(8,128)S(1)} %broadcast_in_dim.2.flags, f32[64,256]{1,0:T(8,128)S(1)} %copy-done.1, f32[64,256]{1,0:T(8,128)S(1)} %copy-done.2, ...), custom_call_target="tpu_custom_call" | custom-call | tf_op jit(solution)/shard_map/forward/pallas_call | solution.py:515
  17.8 27.4 %all_to_all.11 = f32[256,1,128]{2,1,0:T(1,128)S(1)} all-to-all(f32[256,1,128]{2,1,0:T(1,128)S(1)} %bitcast.7), channel_id=1, replica_groups=mesh['lat'=8,'lon'=32] {'lat','lon'}, dimensions={0} | all-to-all | bytes 262144 | tf_op jit(solution)/shard_map/all_to_all | solution.py:535
  45.2 6.8 %adjoint.1 = (f32[8,64,256]{2,1,0:T(8,128)}, f32[8,64,256]{2,1,0:T(8,128)}, f32[8,64,256]{2,1,0:T(8,128)}) custom-call(f32[256,128]{1,0:T(8,128)S(1)} %bitcast.6, f32[8,3,80,128]{3,2,1,0:T(8,128)S(1)} %get-tuple-element.21.vecs, f32[4,3,80,128]{3,2,1,0:T(8,128)S(1)} %get-tuple-element.22.links, f32[2,64,256]{2,1,0:T(8,128)S(1)} %get-tuple-element.23.wet, ...), custom_call_target="tpu_custom_call" | custom-call | tf_op jit(solution)/shard_map/adjoint/pallas_call | solution.py:537
Async XLA Ops:
  0.6 5.7 %copy-start = (f32[8,64,256]{2,1,0:T(8,128)S(1)}, f32[8,64,256]{2,1,0:T(8,128)}, u32[]{:S(2)}) copy-start(f32[8,64,256]{2,1,0:T(8,128)} %w.7) | copy-start | bytes 1572868
  0.6 5.7 %copy-start.5 = (s32[64,256]{1,0:T(8,128)S(1)}, s32[64,256]{1,0:T(8,128)}, u32[]{:S(2)}) copy-start(s32[64,256]{1,0:T(8,128)} %mask.5) | copy-start | bytes 196612
  0.7 5.7 %copy-start.4 = (f32[64,256]{1,0:T(8,128)S(1)}, f32[64,256]{1,0:T(8,128)}, u32[]{:S(2)}) copy-start(f32[64,256]{1,0:T(8,128)} %st.5) | copy-start | bytes 196612
  0.7 5.6 %copy-start.3 = (f32[64,256]{1,0:T(8,128)S(1)}, f32[64,256]{1,0:T(8,128)}, u32[]{:S(2)}) copy-start(f32[64,256]{1,0:T(8,128)} %dn.5) | copy-start | bytes 196612
  0.7 5.6 %copy-start.2 = (f32[64,256]{1,0:T(8,128)S(1)}, f32[64,256]{1,0:T(8,128)}, u32[]{:S(2)}) copy-start(f32[64,256]{1,0:T(8,128)} %de.5) | copy-start | bytes 196612
  0.7 5.6 %copy-start.1 = (f32[64,256]{1,0:T(8,128)S(1)}, f32[64,256]{1,0:T(8,128)}, u32[]{:S(2)}) copy-start(f32[64,256]{1,0:T(8,128)} %f.5) | copy-start | bytes 196612
  1.8 6.9 %collective-permute-start = (f32[144,256]{1,0:T(8,128)S(1)}, f32[144,256]{1,0:T(8,128)S(1)}, u32[]{:S(2)}, u32[]{:S(2)}) collective-permute-start(f32[144,256]{1,0:T(8,128)S(1)} %get-tuple-element.14), channel_id=1, source_target_pairs={{0,32},{32,64},{64,96},{96,128},{128,160},{160,192},{192,224},{224... | collective-permute-start | bytes 442376 | tf_op jit(solution)/shard_map/ppermute | solution.py:492
  3.9 4.8 %collective-permute-start.1 = (f32[144,256]{1,0:T(8,128)S(1)}, f32[144,256]{1,0:T(8,128)S(1)}, u32[]{:S(2)}, u32[]{:S(2)}) collective-permute-start(f32[144,256]{1,0:T(8,128)S(1)} %get-tuple-element.15), channel_id=1, source_target_pairs={{0,224},{32,0},{64,32},{96,64},{128,96},{160,128},{192,160},{224,1... | collective-permute-start | bytes 442376 | tf_op jit(solution)/shard_map/ppermute | solution.py:493
  8.9 5.1 %collective-permute-start.2 = (f32[96,128]{1,0:T(8,128)S(1)}, f32[96,128]{1,0:T(8,128)S(1)}, u32[]{:S(2)}, u32[]{:S(2)}) collective-permute-start(f32[96,128]{1,0:T(8,128)S(1)} %get-tuple-element.18), channel_id=1, source_target_pairs={{0,1},{1,2},{2,3},{3,4},{4,5},{5,6},{6,7},{7,8},{8,9},{9,10},{10,1... | collective-permute-start | bytes 147464 | tf_op jit(solution)/shard_map/ppermute | solution.py:510
  12.8 3.5 %collective-permute-start.3 = (f32[96,128]{1,0:T(8,128)S(1)}, f32[96,128]{1,0:T(8,128)S(1)}, u32[]{:S(2)}, u32[]{:S(2)}) collective-permute-start(f32[96,128]{1,0:T(8,128)S(1)} %get-tuple-element.19), channel_id=1, source_target_pairs={{0,31},{1,0},{2,1},{3,2},{4,3},{5,4},{6,5},{7,6},{8,7},{9,8},{10,9... | collective-permute-start | bytes 147464 | tf_op jit(solution)/shard_map/ppermute | solution.py:511
